TPU v7x, 32 devices: a whole 2x2x4 slice. The times are simulated.
32 devices in a mesh: expert: 8 (over z, y), tensor: 4 (over x, core).
Axes of the slice: x: 2, y: 2, z: 4, core: 2. Of those that a mesh axis runs over, the one named last changes fastest.
Arguments:
- tokens: bfloat16 [2048, 2048], P('expert'), may hold values from -6 to 6
- seq_length: int32 [8], P('expert'), may hold values from 256 to 256, as said below
- expert_routes: int32 [2048, 8], P('expert'), may hold values from 0 to 15, all different within a row; in each aligned block of 256 rows (0 to 255, 256 to 511, ...) at most 160 rows name the same one
- attention_gain: float32 [2048], replicated, may hold values from 0.5 to 1.5
- query_weight: bfloat16 [2048, 4096], P(None, 'tensor'), may hold values from -0.125 to 0.125
- key_weight: bfloat16 [2048, 512], P(None, 'tensor'), may hold values from -0.125 to 0.125
- value_weight: bfloat16 [2048, 512], P(None, 'tensor'), may hold values from -0.125 to 0.125
- query_gain: float32 [128], replicated, may hold values from 0.5 to 1.5
- key_gain: float32 [128], replicated, may hold values from 0.5 to 1.5
- output_weight: bfloat16 [2048, 4096], P(None, 'tensor'), may hold values from -0.5 to 0.5
- routing_gain: float32 [2048], replicated, may hold values from 0.5 to 1.5
- router_weight: bfloat16 [2048, 16], replicated, may hold values from -0.26367188 to 0.26367188
- gate_weight: bfloat16 [16, 2048, 768], P('expert', None, 'tensor'), may hold values from -0.125 to 0.125
- up_weight: bfloat16 [16, 2048, 768], P('expert', None, 'tensor'), may hold values from -0.125 to 0.125
- down_weight: bfloat16 [16, 768, 2048], P('expert', 'tensor'), may hold values from -0.625 to 0.625
- cotangent: bfloat16 [2048, 2048], P('expert'), may hold values from -6 to 6
Outputs:
- mixed: bfloat16 [2048, 2048], P('expert')
- tokens_grad: bfloat16 [2048, 2048], P('expert')
- attention_gain_grad: float32 [2048], P('expert')
- query_weight_grad: float32 [2048, 4096], P('expert', 'tensor')
- key_weight_grad: float32 [2048, 512], P('expert', 'tensor')
- value_weight_grad: float32 [2048, 512], P('expert', 'tensor')
- query_gain_grad: float32 [128], P('expert')
- key_gain_grad: float32 [128], P('expert')
- output_weight_grad: float32 [2048, 4096], P('expert', 'tensor')
- routing_gain_grad: float32 [2048], P('expert')
- router_weight_grad: float32 [2048, 16], P('expert')
- gate_weight_grad: float32 [16, 2048, 768], P('expert', None, 'tensor')
- up_weight_grad: float32 [16, 2048, 768], P('expert', None, 'tensor')
- down_weight_grad: float32 [16, 768, 2048], P('expert', 'tensor')
Inputs may be any that keep to these rules, and one draw needn't show every extreme that they name: `seq_length`: each group holds one sequence starting at its first row; some group's sequence fills all 256 rows. `expert_routes`: each row names 8 different experts; within the rows of one group no expert is named more than 160 times.
All inputs are finite; a program needn't handle non-finite values.
Results may differ from a plain program's by a relative error of at most 0.025.
Values may be sent and summed in bfloat16 or wider, within the bound.
A program may use at most 192 MiB of HBM per device.

v0:
```python
import jax
import jax.numpy as jnp
from jax import lax
from jax.sharding import PartitionSpec as P

EPSILON = 1e-06
THETA = 1000000.0
NEGATIVE = -1e30


def rms_scale(values):
    return lax.rsqrt(jnp.mean(values * values, axis=-1, keepdims=True) + EPSILON)


def rope_tables(count, width):
    half = width // 2
    freqs = THETA ** (-(jnp.arange(half, dtype=jnp.float32) * 2.0 / width))
    angles = jnp.arange(count, dtype=jnp.float32)[:, None] * freqs[None, :]
    cosine = jnp.concatenate([jnp.cos(angles), jnp.cos(angles)], axis=1)
    sine = jnp.concatenate([jnp.sin(angles), jnp.sin(angles)], axis=1)
    return (cosine, sine)


def rotate(values, cosine, sine):
    half = values.shape[-1] // 2
    turned = jnp.concatenate([-values[..., half:], values[..., :half]], axis=-1)
    return values * cosine[:, None, :] + turned * sine[:, None, :]


def rotate_back(grads, cosine, sine):
    half = grads.shape[-1] // 2
    scaled = grads * sine[:, None, :]
    turned = jnp.concatenate([scaled[..., half:], -scaled[..., :half]], axis=-1)
    return grads * cosine[:, None, :] + turned


def head_norm(values, gain):
    scale = rms_scale(values)
    normed = values * scale
    return (normed * gain, normed, scale)


def head_norm_back(grads, normed, scale, gain):
    gain_grad = jnp.sum(grads * normed, axis=(0, 1))
    inner = grads * gain
    values_grad = scale * (inner - normed * jnp.mean(inner * normed, axis=-1, keepdims=True))
    return (values_grad, gain_grad)


def contract(left, right, left_dim, right_dim):
    return lax.dot_general(
        left, right, (((left_dim,), (right_dim,)), ((), ())), preferred_element_type=jnp.float32
    )


def block_scores(qblock, start, keys, length):
    block = qblock.shape[0]
    count = keys.shape[0]
    factor = qblock.shape[-1] ** (-0.5)
    rows = start + jnp.arange(block, dtype=jnp.int32)
    columns = jnp.arange(count, dtype=jnp.int32)
    allowed = (columns[None, :] <= rows[:, None]) & (columns[None, :] < length)
    scores = jnp.einsum("qagh,kah->agqk", qblock, keys, preferred_element_type=jnp.float32) * factor
    return (jnp.where(allowed[None, None, :, :], scores, NEGATIVE), factor)


def attend_block(qblock, start, keys, values, length):
    scores, factor = block_scores(qblock, start, keys, length)
    peak = jnp.max(scores, axis=-1, keepdims=True)
    expo = jnp.exp(scores - peak)
    total = jnp.sum(expo, axis=-1, keepdims=True)
    probs_low = (expo / total).astype(jnp.bfloat16)
    output = jnp.einsum("agqk,kah->qagh", probs_low, values, preferred_element_type=jnp.float32)
    return (output, (peak + jnp.log(total))[..., 0])


def attend_back(qblock, dblock, lse_block, start, keys, values, length):
    scores, factor = block_scores(qblock, start, keys, length)
    probs = jnp.exp(scores - lse_block[..., None])
    probs_grad = jnp.einsum("qagh,kah->agqk", dblock, values, preferred_element_type=jnp.float32)
    delta = jnp.sum(probs * probs_grad, axis=-1, keepdims=True)
    score_grad = (probs * (probs_grad - delta)).astype(jnp.bfloat16)
    query_grad = (
        jnp.einsum("agqk,kah->qagh", score_grad, keys, preferred_element_type=jnp.float32) * factor
    )
    key_grad = (
        jnp.einsum("agqk,qagh->kah", score_grad, qblock, preferred_element_type=jnp.float32)
        * factor
    )
    value_grad = jnp.einsum(
        "agqk,qagh->kah", probs.astype(jnp.bfloat16), dblock, preferred_element_type=jnp.float32
    )
    return (query_grad, key_grad, value_grad)


def shards(
    tokens,
    seq_length,
    expert_routes,
    attention_gain,
    query_weight,
    key_weight,
    value_weight,
    query_gain,
    key_gain,
    output_weight,
    routing_gain,
    router_weight,
    gate_weight,
    up_weight,
    down_weight,
    cotangent,
):
    count = tokens.shape[0]
    width = tokens.shape[1]
    head_size = query_gain.shape[0]
    local_heads = query_weight.shape[1] // head_size
    local_groups = key_weight.shape[1] // head_size
    ratio = local_heads // local_groups
    length = seq_length[0]
    experts = router_weight.shape[1]
    top = expert_routes.shape[1]
    owned = gate_weight.shape[0]
    sources = experts // owned
    parts = lax.axis_size("tensor")
    part = lax.axis_index("tensor")
    quarter = (count * top * 5 + 16 * experts - 1) // (16 * experts)
    inputs = tokens.astype(jnp.float32)
    scale1 = rms_scale(inputs)
    normed1 = inputs * scale1
    xnorm1 = (normed1 * attention_gain).astype(jnp.bfloat16)
    query_raw = jnp.dot(xnorm1, query_weight, preferred_element_type=jnp.float32).reshape(
        count, local_heads, head_size
    )
    key_raw = jnp.dot(xnorm1, key_weight, preferred_element_type=jnp.float32).reshape(
        count, local_groups, head_size
    )
    value_low = (
        jnp.dot(xnorm1, value_weight, preferred_element_type=jnp.float32)
        .astype(jnp.bfloat16)
        .reshape(count, local_groups, head_size)
    )
    query_gained, query_normed, query_scale = head_norm(query_raw, query_gain)
    key_gained, key_normed, key_scale = head_norm(key_raw, key_gain)
    cosine, sine = rope_tables(count, head_size)
    query_low = rotate(query_gained, cosine, sine).astype(jnp.bfloat16)
    key_low = rotate(key_gained, cosine, sine).astype(jnp.bfloat16)
    block = min(512, count)
    blocks = count // block
    starts = jnp.arange(blocks, dtype=jnp.int32) * block
    query_blocks = query_low.reshape(blocks, block, local_groups, ratio, head_size)

    def forward_block(item):
        qblock, start = item
        return attend_block(qblock, start, key_low, value_low, length)

    outputs, lse = lax.map(forward_block, (query_blocks, starts))
    valid = (jnp.arange(count, dtype=jnp.int32) < length)[:, None]
    heads_low = jnp.where(valid, outputs.reshape(count, local_heads * head_size), 0.0).astype(
        jnp.bfloat16
    )
    attention_part = contract(heads_low, output_weight, 1, 1)
    attention_full = lax.psum(attention_part, "tensor")
    hidden = inputs + attention_full
    scale2 = rms_scale(hidden)
    normed2 = hidden * scale2
    xnorm2 = (normed2 * routing_gain).astype(jnp.bfloat16)
    logits = jnp.dot(xnorm2, router_weight, preferred_element_type=jnp.float32)
    peak = jnp.max(logits, axis=1, keepdims=True)
    expo = jnp.exp(logits - peak)
    router = expo / jnp.sum(expo, axis=1, keepdims=True)
    onehot = expert_routes[:, :, None] == jnp.arange(experts, dtype=jnp.int32)[None, None, :]
    chosen = jnp.sum(jnp.where(onehot, router[:, None, :], 0.0), axis=-1)
    chosen_total = jnp.sum(chosen, axis=1, keepdims=True)
    route_weight = chosen / chosen_total
    flat_routes = expert_routes.reshape(-1)
    hits = (flat_routes[:, None] == jnp.arange(experts, dtype=jnp.int32)[None, :]).astype(jnp.int32)
    ranks = jnp.sum((jnp.cumsum(hits, axis=0) - 1) * hits, axis=1)
    mine = ranks % parts == part
    slot_index = jnp.where(mine, ranks // parts * experts + flat_routes, quarter * experts)
    table = (
        jnp.full((quarter * experts,), count * top, jnp.int32)
        .at[slot_index]
        .set(jnp.arange(count * top, dtype=jnp.int32), mode="drop")
    )
    slot_token = table // top
    send_rows = jnp.take(xnorm2, slot_token, axis=0, mode="fill", fill_value=0).reshape(
        quarter, experts, width
    )
    arrived = lax.all_to_all(send_rows, "expert", split_axis=1, concat_axis=1, tiled=True)
    gate_full, up_full, down_full = (
        lax.all_gather(gate_weight, "tensor", axis=2, tiled=True),
        lax.all_gather(up_weight, "tensor", axis=2, tiled=True),
        lax.all_gather(down_weight, "tensor", axis=1, tiled=True),
    )
    rows_own = arrived.reshape(quarter, sources, owned, width)
    gate_val = jnp.einsum("csjd,jdf->csjf", rows_own, gate_full, preferred_element_type=jnp.float32)
    up_val = jnp.einsum("csjd,jdf->csjf", rows_own, up_full, preferred_element_type=jnp.float32)
    sigmoid_gate = jax.nn.sigmoid(gate_val)
    activated = gate_val * sigmoid_gate
    inner_low = (activated * up_val).astype(jnp.bfloat16)
    expert_total = jnp.einsum(
        "csjf,jfd->csjd", inner_low, down_full, preferred_element_type=jnp.float32
    )
    expert_low = expert_total.astype(jnp.bfloat16).reshape(quarter, experts, width)
    returned = lax.all_to_all(
        expert_low, "expert", split_axis=1, concat_axis=1, tiled=True
    ).reshape(quarter * experts, width)
    picked = jnp.take(returned, slot_index, axis=0, mode="fill", fill_value=0).reshape(
        count, top, width
    )
    mine_rows = mine.reshape(count, top)
    mine_weight = jnp.where(mine_rows, route_weight, 0.0)
    moe_part = jnp.sum(mine_weight[:, :, None] * picked, axis=1)
    moe_full = lax.psum(moe_part.astype(jnp.bfloat16), "tensor").astype(jnp.float32)
    mixed = (hidden + moe_full).astype(jnp.bfloat16)
    upstream = cotangent.astype(jnp.float32)
    route_grad_part = jnp.where(mine_rows, jnp.sum(picked * upstream[:, None, :], axis=-1), 0.0)
    slot_weight = jnp.take(route_weight.reshape(-1), table, mode="fill", fill_value=0.0)
    grad_send = (
        jnp.take(cotangent, slot_token, axis=0, mode="fill", fill_value=0) * slot_weight[:, None]
    ).astype(jnp.bfloat16)
    grad_arrived = lax.all_to_all(
        grad_send.reshape(quarter, experts, width),
        "expert",
        split_axis=1,
        concat_axis=1,
        tiled=True,
    )
    grad_own = grad_arrived.reshape(quarter, sources, owned, width)
    down_part = jnp.einsum(
        "csjf,csjd->jfd", inner_low, grad_own, preferred_element_type=jnp.float32
    )
    inner_grad = jnp.einsum(
        "csjd,jfd->csjf", grad_own, down_full, preferred_element_type=jnp.float32
    )
    gate_grad_low = (
        inner_grad * up_val * sigmoid_gate * (1.0 + gate_val * (1.0 - sigmoid_gate))
    ).astype(jnp.bfloat16)
    up_grad_low = (inner_grad * activated).astype(jnp.bfloat16)
    gate_part = jnp.einsum(
        "csjd,csjf->jdf", rows_own, gate_grad_low, preferred_element_type=jnp.float32
    )
    up_part = jnp.einsum(
        "csjd,csjf->jdf", rows_own, up_grad_low, preferred_element_type=jnp.float32
    )
    rows_grad = jnp.einsum(
        "csjf,jdf->csjd", gate_grad_low, gate_full, preferred_element_type=jnp.float32
    )
    rows_grad = rows_grad + jnp.einsum(
        "csjf,jdf->csjd", up_grad_low, up_full, preferred_element_type=jnp.float32
    )
    gate_grad, up_grad, down_grad = (
        lax.psum_scatter(
            gate_part.astype(jnp.bfloat16), "tensor", scatter_dimension=2, tiled=True
        ).astype(jnp.float32),
        lax.psum_scatter(
            up_part.astype(jnp.bfloat16), "tensor", scatter_dimension=2, tiled=True
        ).astype(jnp.float32),
        lax.psum_scatter(
            down_part.astype(jnp.bfloat16), "tensor", scatter_dimension=1, tiled=True
        ).astype(jnp.float32),
    )
    rows_grad_low = rows_grad.astype(jnp.bfloat16).reshape(quarter, experts, width)
    returned_grad = lax.all_to_all(
        rows_grad_low, "expert", split_axis=1, concat_axis=1, tiled=True
    ).reshape(quarter * experts, width)
    route_rows = jnp.take(returned_grad, slot_index, axis=0, mode="fill", fill_value=0).reshape(
        count, top, width
    )
    xnorm2_part = jnp.sum(route_rows, axis=1, dtype=jnp.float32)
    xnorm2_moe, route_grad = (
        lax.psum(xnorm2_part.astype(jnp.bfloat16), "tensor").astype(jnp.float32),
        lax.psum(route_grad_part.astype(jnp.bfloat16), "tensor").astype(jnp.float32),
    )
    inner_total = jnp.sum(route_grad * route_weight, axis=1, keepdims=True)
    chosen_grad = (route_grad - inner_total) / chosen_total
    prob_grad = jnp.sum(jnp.where(onehot, chosen_grad[:, :, None], 0.0), axis=1)
    logit_low = (router * (prob_grad - jnp.sum(router * prob_grad, axis=1, keepdims=True))).astype(
        jnp.bfloat16
    )
    router_grad = contract(xnorm2, logit_low, 0, 0)
    xnorm2_grad = xnorm2_moe + contract(logit_low, router_weight, 1, 1)
    routing_gain_part = jnp.sum(xnorm2_grad * normed2, axis=0)
    inner2 = xnorm2_grad * routing_gain
    hidden_grad = upstream + scale2 * (
        inner2 - normed2 * jnp.mean(inner2 * normed2, axis=1, keepdims=True)
    )
    hidden_low = hidden_grad.astype(jnp.bfloat16)
    output_grad = contract(hidden_low, heads_low, 0, 0)
    heads_grad = jnp.where(
        valid,
        jnp.dot(hidden_low, output_weight, preferred_element_type=jnp.float32).astype(jnp.bfloat16),
        jnp.zeros((), jnp.bfloat16),
    )
    grad_blocks = heads_grad.reshape(blocks, block, local_groups, ratio, head_size)

    def backward_block(carry, item):
        key_acc, value_acc = carry
        qblock, dblock, lse_block, start = item
        query_piece, key_piece, value_piece = attend_back(
            qblock, dblock, lse_block, start, key_low, value_low, length
        )
        return ((key_acc + key_piece, value_acc + value_piece), query_piece)

    empty = jnp.zeros((count, local_groups, head_size), jnp.float32)
    (key_rot_grad, value_grad), query_rot_grad = lax.scan(
        backward_block, (empty, empty), (query_blocks, grad_blocks, lse, starts)
    )
    query_back, query_gain_part = head_norm_back(
        rotate_back(query_rot_grad.reshape(count, local_heads, head_size), cosine, sine),
        query_normed,
        query_scale,
        query_gain,
    )
    key_back, key_gain_part = head_norm_back(
        rotate_back(key_rot_grad, cosine, sine), key_normed, key_scale, key_gain
    )
    query_grad_low = query_back.reshape(count, local_heads * head_size).astype(jnp.bfloat16)
    key_grad_low = key_back.reshape(count, local_groups * head_size).astype(jnp.bfloat16)
    value_grad_low = value_grad.reshape(count, local_groups * head_size).astype(jnp.bfloat16)
    query_wgrad = contract(xnorm1, query_grad_low, 0, 0)
    key_wgrad = contract(xnorm1, key_grad_low, 0, 0)
    value_wgrad = contract(xnorm1, value_grad_low, 0, 0)
    xnorm1_part = contract(query_grad_low, query_weight, 1, 1) + contract(
        key_grad_low, key_weight, 1, 1
    )
    xnorm1_part = xnorm1_part + contract(value_grad_low, value_weight, 1, 1)
    xnorm1_grad, query_gain_sum, key_gain_sum = (
        lax.psum(xnorm1_part.astype(jnp.bfloat16), "tensor").astype(jnp.float32),
        lax.psum(query_gain_part.astype(jnp.bfloat16), "tensor").astype(jnp.float32),
        lax.psum(key_gain_part.astype(jnp.bfloat16), "tensor").astype(jnp.float32),
    )
    attention_gain_part = jnp.sum(xnorm1_grad * normed1, axis=0)
    inner1 = xnorm1_grad * attention_gain
    tokens_grad = (
        hidden_grad
        + scale1 * (inner1 - normed1 * jnp.mean(inner1 * normed1, axis=1, keepdims=True))
    ).astype(jnp.bfloat16)
    summed = (
        lax.psum_scatter(
            attention_gain_part.astype(jnp.bfloat16), "expert", scatter_dimension=0, tiled=True
        ).astype(jnp.float32),
        lax.psum_scatter(
            query_wgrad.astype(jnp.bfloat16), "expert", scatter_dimension=0, tiled=True
        ).astype(jnp.float32),
        lax.psum_scatter(
            key_wgrad.astype(jnp.bfloat16), "expert", scatter_dimension=0, tiled=True
        ).astype(jnp.float32),
        lax.psum_scatter(
            value_wgrad.astype(jnp.bfloat16), "expert", scatter_dimension=0, tiled=True
        ).astype(jnp.float32),
        lax.psum_scatter(
            query_gain_sum.astype(jnp.bfloat16), "expert", scatter_dimension=0, tiled=True
        ).astype(jnp.float32),
        lax.psum_scatter(
            key_gain_sum.astype(jnp.bfloat16), "expert", scatter_dimension=0, tiled=True
        ).astype(jnp.float32),
        lax.psum_scatter(
            output_grad.astype(jnp.bfloat16), "expert", scatter_dimension=0, tiled=True
        ).astype(jnp.float32),
        lax.psum_scatter(
            routing_gain_part.astype(jnp.bfloat16), "expert", scatter_dimension=0, tiled=True
        ).astype(jnp.float32),
        lax.psum_scatter(
            router_grad.astype(jnp.bfloat16), "expert", scatter_dimension=0, tiled=True
        ).astype(jnp.float32),
    )
    return (
        mixed,
        tokens_grad,
        summed[0],
        summed[1],
        summed[2],
        summed[3],
        summed[4],
        summed[5],
        summed[6],
        summed[7],
        summed[8],
        gate_grad,
        up_grad,
        down_grad,
    )


def solution(mesh):
    return jax.shard_map(
        shards,
        mesh=mesh,
        in_specs=(
            P("expert", None),
            P("expert"),
            P("expert", None),
            P(),
            P(None, "tensor"),
            P(None, "tensor"),
            P(None, "tensor"),
            P(),
            P(),
            P(None, "tensor"),
            P(),
            P(),
            P("expert", None, "tensor"),
            P("expert", None, "tensor"),
            P("expert", "tensor", None),
            P("expert", None),
        ),
        out_specs=(
            P("expert", None),
            P("expert", None),
            P("expert"),
            P("expert", "tensor"),
            P("expert", "tensor"),
            P("expert", "tensor"),
            P("expert"),
            P("expert"),
            P("expert", "tensor"),
            P("expert"),
            P("expert", None),
            P("expert", None, "tensor"),
            P("expert", None, "tensor"),
            P("expert", "tensor", None),
        ),
        check_vma=False,
    )
```

profile of v0, /device:TPU:0, one launch (start us, length us, event | category | flops | bytes accessed | tf_op | source)
XLA Modules:
  0.0 1200.8 jit_solution(10702286464317430164)
XLA Ops:
  52.1 8.3 scatter_custom_fusion
  60.4 38.0 %all-reduce.11.cloned.1.call-done = f32[256,2048]{1,0:T(8,128)} async-done(((f32[256,2048]{1,0:T(8,128)}), f32[256,2048]{1,0:T(8,128)}) %all-reduce.11.cloned.1.call-update) | async-done | bytes 2097168 | tf_op jit(solution)/shard_map/psum | solution.py:163
  109.7 64.8 %all_to_all.20 = bf16[40,16,2048]{2,0,1:T(8,128)(2,1)} all-to-all(bf16[40,16,2048]{2,0,1:T(8,128)(2,1)S(1)} %copy.216), channel_id=1, replica_groups=mesh['expert'=8,'tensor'=4] {'expert'}, dimensions={1} | all-to-all | bytes 5242880 | tf_op jit(solution)/shard_map/all_to_all | solution.py:190
  174.5 7.8 fusion.9
  182.3 12.1 %all-gather.6.cloned.1.call-done = bf16[2,2048,768]{1,2,0:T(8,128)(2,1)} async-done(((bf16[2,2048,192]{1,2,0:T(8,128)(2,1)}), bf16[2,2048,768]{1,2,0:T(8,128)(2,1)}) %all-gather.6.cloned.1.call-update) | async-done | bytes 6291472 | tf_op jit(solution)/shard_map/all_gather | solution.py:193
  194.4 8.4 fusion.50
  202.7 39.4 %all-gather.8.cloned.1.call-done = bf16[2,768,2048]{2,1,0:T(8,128)(2,1)} async-done(((bf16[2,192,2048]{2,1,0:T(8,128)(2,1)}), bf16[2,768,2048]{2,1,0:T(8,128)(2,1)}) %all-gather.8.cloned.1.call-update) | async-done | bytes 6291472 | tf_op jit(solution)/shard_map/all_gather | solution.py:194
  250.1 6.1 all-to-all-start.1
  264.9 51.2 %all-to-all-done.1 = bf16[40,16,2048]{2,0,1:T(8,128)(2,1)} async-done(((bf16[40,16,2048]{2,0,1:T(8,128)(2,1)}), bf16[40,16,2048]{2,0,1:T(8,128)(2,1)}, u32[]{:S(2)}, u32[]{:S(2)}) %all-to-all-start.1) | async-done | bytes 2621472 | tf_op jit(solution)/shard_map/all_to_all | solution.py:206
  319.3 11.0 gather_fusion.2
  330.3 6.1 fusion.2
  337.2 5.9 psum.52
  353.9 63.2 %all_to_all.21 = bf16[40,16,2048]{2,0,1:T(8,128)(2,1)S(1)} all-to-all(bf16[40,16,2048]{2,0,1:T(8,128)(2,1)S(1)} %copy.222), channel_id=1, replica_groups=mesh['expert'=8,'tensor'=4] {'expert'}, dimensions={1} | all-to-all | bytes 5242880 | tf_op jit(solution)/shard_map/all_to_all | solution.py:223
  417.1 8.5 fusion.48
  439.6 56.8 %all-to-all-done.3 = bf16[40,16,2048]{2,0,1:T(8,128)(2,1)} async-done(((bf16[40,16,2048]{2,0,1:T(8,128)(2,1)}), bf16[40,16,2048]{2,0,1:T(8,128)(2,1)}, u32[]{:S(2)}, u32[]{:S(2)}) %all-to-all-start.3) | async-done | bytes 2621472 | tf_op jit(solution)/shard_map/all_to_all | solution.py:265
  499.6 11.3 gather_fusion.4
  510.9 8.6 bitcast_reduce_fusion
  520.1 10.4 fusion.1
  530.6 23.5 %all-reduce.13.cloned.1.call-done = bf16[256,2048]{1,0:T(8,128)(2,1)} async-done(((bf16[256,2048]{1,0:T(8,128)(2,1)}), bf16[256,2048]{1,0:T(8,128)(2,1)}) %all-reduce.13.cloned.1.call-update) | async-done | bytes 1048592 | tf_op jit(solution)/shard_map/psum | solution.py:273
  587.9 7.2 bitcast_convert_fusion.2
  596.4 7.2 bitcast_convert_fusion.1
  604.8 8.2 bitcast_convert_fusion
  624.3 11.5 all-reduce.15.cloned.1.call-done
  638.2 22.0 %all-reduce.4 = (bf16[2048]{0:T(1024)(128)(2,1)S(1)}, bf16[128]{0:T(256)(128)(2,1)S(1)}, bf16[128]{0:T(256)(128)(2,1)S(1)}, bf16[2048]{0:T(1024)(128)(2,1)S(1)}) all-reduce(bf16[2048]{0:T(1024)(128)(2,1)S(1)} %get-tuple-element.71, bf16[128]{0:T(256)(128)(2,1)S(1)} %copy-done.103, ...), channel_id=2, replica_groups=mesh['expert'=8,'tensor'=4] {'expert'}, use_global_device_ids=true, to_apply=%region_31.34.clone | all-reduce | flops 4352 | bytes 17408
  660.4 34.0 %reduce-scatter.17.cloned.1.call-done = bf16[256,16]{0,1:T(8,128)(2,1)} async-done(((bf16[2048,16]{0,1:T(8,128)(2,1)}), bf16[256,16]{0,1:T(8,128)(2,1)}) %reduce-scatter.17.cloned.1.call-update) | async-done | bytes 8208 | tf_op jit(solution)/shard_map/reduce_scatter | solution.py:365
  702.4 57.6 %reduce-scatter.11.cloned.1.call-done = bf16[256,128]{1,0:T(8,128)(2,1)} async-done(((bf16[2048,128]{1,0:T(8,128)(2,1)}), bf16[256,128]{1,0:T(8,128)(2,1)}) %reduce-scatter.11.cloned.1.call-update) | async-done | bytes 65552 | tf_op jit(solution)/shard_map/reduce_scatter | solution.py:347
  761.5 64.0 %reduce-scatter.13.cloned.1.call-done = bf16[256,128]{1,0:T(8,128)(2,1)} async-done(((bf16[2048,128]{1,0:T(8,128)(2,1)}), bf16[256,128]{1,0:T(8,128)(2,1)}) %reduce-scatter.13.cloned.1.call-update) | async-done | bytes 65552 | tf_op jit(solution)/shard_map/reduce_scatter | solution.py:350
  832.6 53.1 %reduce-scatter.19.cloned.1.call-done = bf16[2,2048,192]{1,2,0:T(8,128)(2,1)} async-done(((bf16[2,2048,768]{1,2,0:T(8,128)(2,1)}), bf16[2,2048,192]{1,2,0:T(8,128)(2,1)}) %reduce-scatter.19.cloned.1.call-update) | async-done | bytes 1572880 | tf_op jit(solution)/shard_map/reduce_scatter | solution.py:254
  889.2 58.0 %reduce-scatter.21.cloned.1.call-done = bf16[2,2048,192]{1,2,0:T(8,128)(2,1)} async-done(((bf16[2,2048,768]{1,2,0:T(8,128)(2,1)}), bf16[2,2048,192]{1,2,0:T(8,128)(2,1)}) %reduce-scatter.21.cloned.1.call-update) | async-done | bytes 1572880 | tf_op jit(solution)/shard_map/reduce_scatter | solution.py:257
  950.6 57.8 %reduce-scatter.23.cloned.1.call-done = bf16[2,192,2048]{2,1,0:T(8,128)(2,1)} async-done(((bf16[2,768,2048]{2,1,0:T(8,128)(2,1)}), bf16[2,192,2048]{2,1,0:T(8,128)(2,1)}) %reduce-scatter.23.cloned.1.call-update) | async-done | bytes 1572880 | tf_op jit(solution)/shard_map/reduce_scatter | solution.py:260
  1011.9 88.6 %reduce-scatter.9.cloned.1.call-done = bf16[256,1024]{1,0:T(8,128)(2,1)} async-done(((bf16[2048,1024]{1,0:T(8,128)(2,1)}), bf16[256,1024]{1,0:T(8,128)(2,1)}) %reduce-scatter.9.cloned.1.call-update) | async-done | bytes 524304 | tf_op jit(solution)/shard_map/reduce_scatter | solution.py:344
  1102.6 89.3 %reduce-scatter.15.cloned.1.call-done = bf16[256,1024]{1,0:T(8,128)(2,1)} async-done(((bf16[2048,1024]{1,0:T(8,128)(2,1)}), bf16[256,1024]{1,0:T(8,128)(2,1)}) %reduce-scatter.15.cloned.1.call-update) | async-done | bytes 524304 | tf_op jit(solution)/shard_map/reduce_scatter | solution.py:359
  (401 shorter events, 183.1 us)
Async XLA Ops:
  7.2 91.2 %all-reduce.11.cloned.1.call-start = ((), (), s32[]{:S(2)}) async-start(), calls=%async_computation.12 | async-start | bytes 4194304 | tf_op jit(solution)/shard_map/psum | solution.py:163
  44.1 130.4 %all-gather.4.cloned.1.call-start = ((), (), s32[]{:S(2)}) async-start(), calls=%async_computation.13 | async-start | bytes 7864320 | tf_op jit(solution)/shard_map/all_gather | solution.py:192
  44.8 149.5 %all-gather.6.cloned.1.call-start = ((), (), s32[]{:S(2)}) async-start(), calls=%async_computation.14 | async-start | bytes 7864320 | tf_op jit(solution)/shard_map/all_gather | solution.py:193
  45.6 196.6 %all-gather.8.cloned.1.call-start = ((), (), s32[]{:S(2)}) async-start(), calls=%async_computation.15 | async-start | bytes 7864320 | tf_op jit(solution)/shard_map/all_gather | solution.py:194
  60.3 202.3 %copy-start.67 = (s32[640]{0:T(1024)}, s32[640]{0:T(1024)S(1)}, u32[]{:S(2)}) copy-start(s32[640]{0:T(1024)S(1)} %scatter_custom_fusion) | copy-start | bytes 7684
  60.4 45.6 %copy-start.91 = (pred[640]{0:T(1024)(128)(4,1)}, pred[640]{0:T(1024)(128)(4,1)S(1)}, u32[]{:S(2)}) copy-start(pred[640]{0:T(1024)(128)(4,1)S(1)} %get-tuple-element.92) | copy-start | bytes 1924
  60.4 41.3 %copy-start.54 = (f32[2048]{0:T(1024)S(1)}, f32[2048]{0:T(1024)}, u32[]{:S(2)}) copy-start(f32[2048]{0:T(1024)} %param.30) | copy-start | bytes 24580
  101.9 161.9 %copy-start.1 = (bf16[256,2048]{1,0:T(8,128)(2,1)}, bf16[256,2048]{1,0:T(8,128)(2,1)S(1)}, u32[]{:S(2)}) copy-start(bf16[256,2048]{1,0:T(8,128)(2,1)S(1)} %multiply_convert_fusion.1) | copy-start | bytes 3145732
  202.7 44.4 %copy-start.109 = (bf16[40,8,2,768]{3,1,0,2:T(8,128)(2,1)}, bf16[40,8,2,768]{3,1,0,2:T(8,128)(2,1)S(1)}, u32[]{:S(2)}) copy-start(bf16[40,8,2,768]{3,1,0,2:T(8,128)(2,1)S(1)} %get-tuple-element.120) | copy-start | bytes 2949124
  250.1 66.0 %all-to-all-start.1 = ((bf16[40,16,2048]{2,0,1:T(8,128)(2,1)}), bf16[40,16,2048]{2,0,1:T(8,128)(2,1)}, u32[]{:S(2)}, u32[]{:S(2)}) async-start(bf16[40,16,2048]{2,0,1:T(8,128)(2,1)} %bitcast.292), calls=%async_computation.1 | async-start | bytes 5242880 | tf_op jit(solution)/shard_map/all_to_all | solution.py:206
  263.8 55.5 %copy-start.58 = (s32[2048]{0:T(1024)}, s32[2048]{0:T(1024)S(1)}, u32[]{:S(2)}) copy-start(s32[2048]{0:T(1024)S(1)} %broadcast_clamp_fusion) | copy-start | bytes 24580
  353.9 71.7 %slice-start.2 = ((s8[6291456]{0:T(1024)(128)(4,1)}), s8[4194304]{0:T(1024)(128)(4,1)S(1)}, s32[]{:S(2)}) async-start(s8[6291456]{0:T(1024)(128)(4,1)} %bitcast.319), calls=%async_computation.28 | async-start | bytes 8388608
  353.9 74.1 %slice-start = ((s8[6291456]{0:T(1024)(128)(4,1)}), s8[4194304]{0:T(1024)(128)(4,1)S(1)}, s32[]{:S(2)}) async-start(s8[6291456]{0:T(1024)(128)(4,1)} %bitcast.299), calls=%async_computation.26 | async-start | bytes 8388608
  433.3 63.1 %all-to-all-start.3 = ((bf16[40,16,2048]{2,0,1:T(8,128)(2,1)}), bf16[40,16,2048]{2,0,1:T(8,128)(2,1)}, u32[]{:S(2)}, u32[]{:S(2)}) async-start(bf16[40,16,2048]{2,0,1:T(8,128)(2,1)} %bitcast.40), calls=%async_computation.3 | async-start | bytes 5242880 | tf_op jit(solution)/shard_map/all_to_all | solution.py:265
  437.8 116.3 %all-reduce.13.cloned.1.call-start = ((), (), s32[]{:S(2)}) async-start(), calls=%async_computation.16 | async-start | bytes 2097152 | tf_op jit(solution)/shard_map/psum | solution.py:273
  519.6 34.5 %copy-start.49 = (bf16[2048,16]{0,1:T(8,128)(2,1)S(1)}, bf16[2048,16]{0,1:T(8,128)(2,1)}, u32[]{:S(2)}) copy-start(bf16[2048,16]{0,1:T(8,128)(2,1)} %param.31) | copy-start | bytes 196612
  519.6 34.5 %copy-start.55 = (f32[2048]{0:T(1024)S(1)}, f32[2048]{0:T(1024)}, u32[]{:S(2)}) copy-start(f32[2048]{0:T(1024)} %param.30) | copy-start | bytes 24580
  519.6 34.5 %copy-start.88 = (f32[256]{0:T(256)S(1)}, f32[256]{0:T(256)}, u32[]{:S(2)}) copy-start(f32[256]{0:T(256)} %copy-done.87) | copy-start | bytes 3076
  519.6 116.2 %all-reduce.15.cloned.1.call-start = ((), (), s32[]{:S(2)}) async-start(), calls=%async_computation.25 | async-start | bytes 4194304 | tf_op jit(solution)/shard_map/psum | solution.py:215
  530.6 26.9 %copy-start.59 = (bf16[256,16]{0,1:T(8,128)(2,1)}, bf16[256,16]{0,1:T(8,128)(2,1)S(1)}, u32[]{:S(2)}) copy-start(bf16[256,16]{0,1:T(8,128)(2,1)S(1)} %multiply_convert_fusion.2) | copy-start | bytes 24580
  530.6 26.9 %copy-start.4 = (bf16[256,2048]{1,0:T(8,128)(2,1)S(1)}, bf16[256,2048]{1,0:T(8,128)(2,1)}, u32[]{:S(2)}) copy-start(bf16[256,2048]{1,0:T(8,128)(2,1)} %param.35) | copy-start | bytes 3145732
  583.8 110.7 %reduce-scatter.17.cloned.1.call-start = ((), (), s32[]{:S(2)}) async-start(), calls=%async_computation.21 | async-start | bytes 73728 | tf_op jit(solution)/shard_map/reduce_scatter | solution.py:365
  584.7 175.3 %reduce-scatter.11.cloned.1.call-start = ((), (), s32[]{:S(2)}) async-start(), calls=%async_computation.18 | async-start | bytes 589824 | tf_op jit(solution)/shard_map/reduce_scatter | solution.py:347
  586.4 239.1 %reduce-scatter.13.cloned.1.call-start = ((), (), s32[]{:S(2)}) async-start(), calls=%async_computation.19 | async-start | bytes 589824 | tf_op jit(solution)/shard_map/reduce_scatter | solution.py:350
  587.9 297.9 %reduce-scatter.19.cloned.1.call-start = ((), (), s32[]{:S(2)}) async-start(), calls=%async_computation.22 | async-start | bytes 7864320 | tf_op jit(solution)/shard_map/reduce_scatter | solution.py:254
  595.2 352.0 %reduce-scatter.21.cloned.1.call-start = ((), (), s32[]{:S(2)}) async-start(), calls=%async_computation.23 | async-start | bytes 7864320 | tf_op jit(solution)/shard_map/reduce_scatter | solution.py:257
  603.6 404.8 %reduce-scatter.23.cloned.1.call-start = ((), (), s32[]{:S(2)}) async-start(), calls=%async_computation.24 | async-start | bytes 7864320 | tf_op jit(solution)/shard_map/reduce_scatter | solution.py:260
  613.1 487.4 %reduce-scatter.9.cloned.1.call-start = ((), (), s32[]{:S(2)}) async-start(), calls=%async_computation.17 | async-start | bytes 4718592 | tf_op jit(solution)/shard_map/reduce_scatter | solution.py:344
  616.5 575.4 %reduce-scatter.15.cloned.1.call-start = ((), (), s32[]{:S(2)}) async-start(), calls=%async_computation.20 | async-start | bytes 4718592 | tf_op jit(solution)/shard_map/reduce_scatter | solution.py:359
  621.8 16.4 %copy-start.86 = (bf16[2048]{0:T(1024)(128)(2,1)S(1)}, bf16[2048]{0:T(1024)(128)(2,1)}, u32[]{:S(2)}) copy-start(bf16[2048]{0:T(1024)(128)(2,1)} %get-tuple-element.57) | copy-start | bytes 12292
  621.8 16.4 %copy-start.103 = (bf16[128]{0:T(256)(128)(2,1)S(1)}, bf16[128]{0:T(256)(128)(2,1)}, u32[]{:S(2)}) copy-start(bf16[128]{0:T(256)(128)(2,1)} %get-tuple-element.69) | copy-start | bytes 772
  621.8 206.5 %copy-start.7 = (f32[256,2048]{1,0:T(8,128)S(1)}, f32[256,2048]{1,0:T(8,128)}, u32[]{:S(2)}) copy-start(f32[256,2048]{1,0:T(8,128)} %copy-done.5) | copy-start | bytes 6291460
  (99 other events, 370.4 us)
Sparse Core Ops, SparseCore 0:
  44.2 54.1 all-reduce.10
  99.9 46.4 all-gather.3
  148.0 46.3 all-gather.5
  195.8 46.3 all-gather.7
  519.7 34.3 all-reduce.12
  583.9 51.8 all-reduce.14
  639.5 54.8 reduce-scatter.16
  698.3 61.6 reduce-scatter.10
  763.9 61.5 reduce-scatter.12
  827.9 57.8 reduce-scatter.18
  888.3 58.8 reduce-scatter.20
  949.6 58.8 reduce-scatter.22
  1012.1 88.3 reduce-scatter.8
  1104.0 87.9 reduce-scatter.14
where the time goes:
time: 1210 us; the launch traced here: 1200 us
  waiting for transfers between devices  737 us (61%)
  blocking collectives  162 us (13%)
  local copies, waits for them, and re-layouts  92.9 us (8%)
  matrix products  92.7 us (8%)
  other arithmetic  86.9 us (7%)
  between operations  17.6 us (1%)
    reduce_scatter x1, waiting for transfers between devices, shards(): lax.psum_scatter(output_grad.astype(jnp.bfloat16), 'expert', scatter_dime...  89.3 us
    reduce_scatter x1, waiting for transfers between devices, shards(): lax.psum_scatter(query_wgrad.astype(jnp.bfloat16), 'expert', scatter_dime...  88.6 us
    all_to_all x1, blocking collectives, shards(): lax.all_to_all(send_rows, 'expert', split_axis=1, concat_axis=1, tiled=True)  64.8 us
    reduce_scatter x1, waiting for transfers between devices, shards(): lax.psum_scatter(value_wgrad.astype(jnp.bfloat16), 'expert', scatter_dime...  64 us
    all_to_all x1, blocking collectives, shards(): lax.all_to_all(grad_send.reshape(quarter, experts, width), 'expert', spli...  63.2 us
    reduce_scatter x1, waiting for transfers between devices, shards(): lax.psum_scatter(up_part.astype(jnp.bfloat16), 'tensor', scatter_dimensio...  58 us
    reduce_scatter x1, waiting for transfers between devices, shards(): lax.psum_scatter(down_part.astype(jnp.bfloat16), 'tensor', scatter_dimens...  57.8 us
    reduce_scatter x1, waiting for transfers between devices, shards(): lax.psum_scatter(key_wgrad.astype(jnp.bfloat16), 'expert', scatter_dimens...  57.6 us
  transfers between devices with their start and end apart: 16, of which 15 were waited for; matrix products, arithmetic and copies ran while one was open for 10% of the time, Pallas kernels for 0%

commit v1 on v0

--- a/solution.py
+++ b/solution.py
@@ -1,6 +1,10 @@
+import functools
+
 import jax
 import jax.numpy as jnp
 from jax import lax
+from jax.experimental import pallas as pl
+from jax.experimental.pallas import tpu as pltpu
 from jax.sharding import PartitionSpec as P
 
 EPSILON = 1e-06
@@ -93,7 +97,7 @@
     return (query_grad, key_grad, value_grad)
 
 
-def shards(
+def routed_shards(
     tokens,
     seq_length,
     expert_routes,
@@ -384,9 +388,756 @@
     )
 
 
+MESH_ID = pl.DeviceIdType.MESH
+DEPTH = 4
+F32 = jnp.float32
+LOW = jnp.bfloat16
+
+
+class Place:
+    def __init__(self):
+        e, t = lax.axis_index("expert"), lax.axis_index("tensor")
+        self.e, self.t = e, t
+        self.z, self.y, self.x, self.c = e // 2, e % 2, t // 2, t % 2
+
+    def at(self, z=None, y=None, x=None, c=None):
+        z, y = self.z if z is None else z, self.y if y is None else y
+        x, c = self.x if x is None else x, self.c if c is None else c
+        return (z * 2 + y, x * 2 + c)
+
+    def block(self, **where):
+        e, t = self.at(**where)
+        return e * 4 + t
+
+    def near(self, k):
+        table = ((0, 1, 2, 3), (1, 2, 0, 3), (2, 1, 3, 0), (3, 2, 1, 0))
+        out = 0
+        for z in range(DEPTH):
+            if isinstance(k, int):
+                column = table[z][k]
+            else:
+                column = table[z][0]
+                for i in range(1, DEPTH):
+                    column = jnp.where(k == i, table[z][i], column)
+            out = jnp.where(self.z == z, column, out)
+        return out
+
+    def peers(self):
+        line = [self.at(z=(self.z + d) % DEPTH) for d in range(1, DEPTH)]
+        return line + [self.at(x=1 - self.x), self.at(y=1 - self.y), self.at(c=1 - self.c)]
+
+
+class Copies:
+    def __init__(self, send_sems, recv_sems):
+        self.send_sems, self.recv_sems, self.used, self.made = send_sems, recv_sems, 0, []
+
+    def make(self, src, dst, to):
+        i = self.used
+        self.used += 1
+        copy = pltpu.make_async_remote_copy(
+            src,
+            dst,
+            self.send_sems.at[i],
+            self.recv_sems.at[i],
+            device_id=to,
+            device_id_type=MESH_ID,
+        )
+        self.made.append(copy)
+        return copy
+
+    def along(self, pieces, to, mine):
+        base = self.used
+        self.used += DEPTH
+        out = []
+        for (peer, src, dst), device in zip(pieces, to):
+            there = pltpu.make_async_remote_copy(
+                src,
+                dst,
+                self.send_sems.at[base + peer],
+                self.recv_sems.at[base + mine],
+                device_id=device,
+                device_id_type=MESH_ID,
+            )
+            back = pltpu.make_async_remote_copy(
+                src,
+                dst,
+                self.send_sems.at[base + peer],
+                self.recv_sems.at[base + peer],
+                device_id=device,
+                device_id_type=MESH_ID,
+            )
+            self.made.append(there)
+            out.append((there, back))
+        return out
+
+    def finish(self):
+        for copy in self.made:
+            copy.wait_send()
+
+
+def enter(peers):
+    barrier = pltpu.get_barrier_semaphore()
+    for peer in peers:
+        pl.semaphore_signal(barrier, inc=1, device_id=peer, device_id_type=MESH_ID)
+    pl.semaphore_wait(barrier, len(peers))
+
+
+def pieces_of(ref, rows):
+    half = rows // 2
+
+    def whole(b):
+        return ref.at[pl.ds(pl.multiple_of(b * rows, rows), rows)]
+
+    def first(b):
+        return ref.at[pl.ds(pl.multiple_of(b * rows, rows), half)]
+
+    def second(b):
+        return ref.at[pl.ds(pl.multiple_of(b * rows + half, half), half)]
+
+    return whole, first, second
+
+
+GATHER_SEMS = DEPTH + 3 * DEPTH + 4 * DEPTH + 2 * DEPTH
+
+
+def gather_steps(p, copies, rows, own_ref, all_ref, own_copy):
+    whole, first, second = pieces_of(all_ref, rows)
+    me = p.block()
+    xn, yn, cn = p.at(x=1 - p.x), p.at(y=1 - p.y), p.at(c=1 - p.c)
+    order = [p.near(k) for k in range(DEPTH)]
+    line = copies.along(
+        [(z, own_ref, whole(me)) for z in order[1:]], [p.at(z=z) for z in order[1:]], p.z
+    )
+    to_x, to_y, near, far, diagonal = [], [], [], [], []
+    for d in range(DEPTH):
+        b = p.block(z=order[d])
+        src = own_ref if d == 0 else whole(b)
+        to_x.append(copies.make(src, whole(b), xn))
+        to_y.append(copies.make(src, whole(b), yn))
+        bx, by = p.block(z=order[d], x=1 - p.x), p.block(z=order[d], y=1 - p.y)
+        bd = p.block(z=order[d], x=1 - p.x, y=1 - p.y)
+        near.append([copies.make(src, whole(b), cn), copies.make(whole(bx), whole(bx), cn)])
+        diagonal.append(
+            (copies.make(first(bx), first(bx), yn), copies.make(second(by), second(by), xn))
+        )
+        far.append(
+            [
+                copies.make(whole(by), whole(by), cn),
+                copies.make(first(bd), first(bd), cn),
+                copies.make(second(bd), second(bd), cn),
+            ]
+        )
+
+    def onward(d):
+        if d:
+            line[d - 1][1].wait_recv()
+        to_x[d].start()
+        to_y[d].start()
+        near[d][0].start()
+
+    def pair(d):
+        to_x[d].wait_recv()
+        diagonal[d][0].start()
+        near[d][1].start()
+        to_y[d].wait_recv()
+        diagonal[d][1].start()
+        far[d][0].start()
+
+    def corner(d):
+        for i in range(2):
+            diagonal[d][i].wait_recv()
+            far[d][1 + i].start()
+
+    def arrived(group):
+        for copy in group:
+            copy.wait_recv()
+
+    def step0():
+        own_copy.start()
+        for there, _ in line:
+            there.start()
+        onward(0)
+        onward(1)
+        pair(0)
+        own_copy.wait()
+        arrived(near[0])
+
+    def step1():
+        onward(2)
+        pair(1)
+        corner(0)
+        arrived(far[0])
+
+    def step3():
+        onward(3)
+        pair(2)
+        corner(1)
+        arrived(far[1])
+
+    def step5():
+        pair(3)
+        corner(2)
+        arrived(far[2])
+
+    def step6():
+        corner(3)
+        arrived(near[3])
+
+    return [
+        step0,
+        step1,
+        lambda: arrived(near[1]),
+        step3,
+        lambda: arrived(near[2]),
+        step5,
+        step6,
+        lambda: arrived(far[3]),
+    ]
+
+
+SCATTER_SEMS = 16 + 8 + 8 + DEPTH
+
+
+def scatter_scratch(rows, width):
+    return [
+        pltpu.VMEM((16, rows, width), LOW),
+        pltpu.VMEM((2, DEPTH, rows // 2, width), LOW),
+        pltpu.VMEM((2, DEPTH, rows, width), LOW),
+        pltpu.VMEM((DEPTH, rows, width), LOW),
+    ]
+
+
+def scatter_steps(p, copies, rows, part, core_in, diag_in, side_in, line_in, out_ref):
+    whole, first, second = pieces_of(part, rows)
+    order = [p.near(k) for k in reversed(range(DEPTH))]
+    xn, yn, cn = p.at(x=1 - p.x), p.at(y=1 - p.y), p.at(c=1 - p.c)
+    kinds = [dict(y=1 - p.y, x=1 - p.x), dict(x=1 - p.x), dict(y=1 - p.y), dict()]
+    blocks = [[p.block(z=z, **kind) for kind in kinds] for z in order]
+    core = [
+        [
+            copies.make(whole(p.block(z=z, c=1 - p.c, **kind)), core_in.at[k * 4 + j], cn)
+            for j, kind in enumerate(kinds)
+        ]
+        for k, z in enumerate(order)
+    ]
+    corners = [
+        (
+            copies.make(first(blocks[k][0]), diag_in.at[0, k], yn),
+            copies.make(second(blocks[k][0]), diag_in.at[1, k], xn),
+        )
+        for k in range(DEPTH)
+    ]
+    sides = [
+        (
+            copies.make(whole(blocks[k][1]), side_in.at[0, k], xn),
+            copies.make(whole(blocks[k][2]), side_in.at[1, k], yn),
+        )
+        for k in range(DEPTH)
+    ]
+    line = copies.along(
+        [(order[k], whole(blocks[k][3]), line_in.at[p.z]) for k in range(DEPTH - 1)],
+        [p.at(z=order[k]) for k in range(DEPTH - 1)],
+        p.z,
+    )
+
+    def add(ref, *more):
+        total = ref[...].astype(F32)
+        for other in more:
+            total = total + other[...].astype(F32)
+        ref[...] = total.astype(LOW)
+
+    def corner(k):
+        core[k][0].wait_recv()
+        add(whole(blocks[k][0]), core_in.at[k * 4])
+        for copy in corners[k]:
+            copy.start()
+        for j in (1, 2):
+            core[k][j].wait_recv()
+            add(whole(blocks[k][j]), core_in.at[k * 4 + j])
+
+    def side(k):
+        corners[k][0].wait_recv()
+        add(first(blocks[k][1]), diag_in.at[0, k])
+        sides[k][0].start()
+        corners[k][1].wait_recv()
+        add(second(blocks[k][2]), diag_in.at[1, k])
+        sides[k][1].start()
+        core[k][3].wait_recv()
+
+    def close(k):
+        sides[k][0].wait_recv()
+        sides[k][1].wait_recv()
+        add(whole(blocks[k][3]), core_in.at[k * 4 + 3], side_in.at[0, k], side_in.at[1, k])
+        if k < DEPTH - 1:
+            line[k][0].start()
+
+    def step0():
+        for row in core:
+            for copy in row:
+                copy.start()
+        corner(0)
+
+    def step1():
+        corner(1)
+        side(0)
+
+    def step2():
+        corner(2)
+        side(1)
+
+    def step3():
+        corner(3)
+        side(2)
+        close(0)
+
+    def step4():
+        side(3)
+        close(1)
+
+    def step7():
+        total = whole(blocks[DEPTH - 1][3])[...].astype(F32)
+        for k in reversed(range(DEPTH - 1)):
+            line[k][1].wait_recv()
+            total = total + line_in[order[k]].astype(F32)
+        out_ref[...] = total
+
+    return [step0, step1, step2, step3, step4, lambda: close(2), lambda: close(3), step7]
+
+
+def dot(left, right, left_dim, right_dim):
+    return lax.dot_general(
+        left, right, (((left_dim,), (right_dim,)), ((), ())), preferred_element_type=F32
+    )
+
+
+def semaphores(*counts):
+    return [pltpu.SemaphoreType.DMA((n,)) for n in counts]
+
+
+VMEM_SPEC = pl.BlockSpec(memory_space=pltpu.VMEM)
+ANY_SPEC = pl.BlockSpec(memory_space=pl.ANY)
+
+
+def gather_kernel(rows, own_ref, all_ref, local_sem, send_sems, recv_sems):
+    p = Place()
+    enter(p.peers())
+    copies = Copies(send_sems, recv_sems)
+    whole, _, _ = pieces_of(all_ref, rows)
+    own_copy = pltpu.make_async_copy(own_ref, whole(p.block()), local_sem.at[0])
+    for step in gather_steps(p, copies, rows, own_ref, all_ref, own_copy):
+        step()
+    copies.finish()
+
+
+def gather_rows(own, collective_id):
+    rows, width = own.shape
+    devices = lax.axis_size("expert") * lax.axis_size("tensor")
+    return pl.pallas_call(
+        functools.partial(gather_kernel, rows),
+        out_shape=jax.ShapeDtypeStruct((devices * rows, width), own.dtype),
+        in_specs=[ANY_SPEC],
+        out_specs=ANY_SPEC,
+        scratch_shapes=semaphores(1, GATHER_SEMS, GATHER_SEMS),
+        compiler_params=pltpu.CompilerParams(collective_id=collective_id, has_side_effects=True),
+        name="gather_rows",
+    )(own)
+
+
+def scatter_kernel(
+    rows, part_ref, out_ref, part, core_in, diag_in, side_in, line_in, local_sem, ss, rs
+):
+    p = Place()
+    fetch = pltpu.make_async_copy(part_ref, part, local_sem.at[0])
+    fetch.start()
+    enter(p.peers())
+    fetch.wait()
+    copies = Copies(ss, rs)
+    for step in scatter_steps(p, copies, rows, part, core_in, diag_in, side_in, line_in, out_ref):
+        step()
+    copies.finish()
+
+
+def scatter_rows(part, collective_id):
+    total, width = part.shape
+    rows = total // (lax.axis_size("expert") * lax.axis_size("tensor"))
+    return pl.pallas_call(
+        functools.partial(scatter_kernel, rows),
+        out_shape=jax.ShapeDtypeStruct((rows, width), F32),
+        in_specs=[ANY_SPEC],
+        out_specs=VMEM_SPEC,
+        scratch_shapes=[pltpu.VMEM(part.shape, LOW)]
+        + scatter_scratch(rows, width)
+        + semaphores(1, SCATTER_SEMS, SCATTER_SEMS),
+        compiler_params=pltpu.CompilerParams(collective_id=collective_id, has_side_effects=True),
+        name="scatter_rows",
+    )(part)
+
+
+def experts_kernel(
+    rows,
+    width,
+    experts,
+    owned,
+    own_ref,
+    upstream_ref,
+    gate_up_ref,
+    down_ref,
+    grad_ref,
+    moe_ref,
+    columns_ref,
+    gate_up_grad_ref,
+    down_grad_ref,
+    all_ref,
+    upstream,
+    outgoing,
+    part,
+    back_rows,
+    core_in,
+    diag_in,
+    side_in,
+    line_in,
+    local_sems,
+    gather_send,
+    gather_recv,
+    scatter_send,
+    scatter_recv,
+):
+    p = Place()
+    group = rows * 4
+    units = down_ref.shape[0]
+    hidden = units // owned
+    extra = all_ref.shape[1] - width
+    enter(p.peers())
+    whole, _, _ = pieces_of(all_ref, rows)
+    own_copy = pltpu.make_async_copy(own_ref, whole(p.block()), local_sems.at[0])
+    gather_copies = Copies(gather_send, gather_recv)
+    scatter_copies = Copies(scatter_send, scatter_recv)
+    gathering = gather_steps(p, gather_copies, rows, own_ref, all_ref, own_copy)
+    scattering = scatter_steps(
+        p, scatter_copies, rows, part, core_in, diag_in, side_in, line_in, grad_ref
+    )
+    count = 2 * DEPTH
+
+    def rows_of(i):
+        side = jnp.where(i % 2 == 0, p.y, 1 - p.y)
+        return pl.ds(pl.multiple_of((p.near(i // 2) * 2 + side) * group, group), group)
+
+    def fetch(i):
+        return pltpu.make_async_copy(
+            upstream_ref.at[rows_of(i)], upstream.at[i % 2], local_sems.at[1 + i % 2]
+        )
+
+    def store(i):
+        return pltpu.make_async_copy(
+            outgoing.at[i % 2], moe_ref.at[rows_of(i)], local_sems.at[3 + i % 2]
+        )
+
+    fetch(0).start()
+    down_grad_ref[...] = jnp.zeros_like(down_grad_ref)
+    first = p.e * owned
+    lane = lax.broadcasted_iota(jnp.int32, (group, extra), 1)
+    unit = lax.broadcasted_iota(jnp.int32, (group, units), 1)
+
+    @pl.loop(0, count)
+    def _(i):
+        for k, step in enumerate(gathering):
+            pl.when(i == k)(step)
+        at = rows_of(i)
+        hid = dot(all_ref[at, :width], gate_up_ref[...], 1, 0)
+        gate, up = hid[:, :units], hid[:, units:]
+        tail = all_ref[at, width:].astype(F32)
+        weights = [
+            jnp.sum(
+                jnp.where((lane == first + j) | (lane == experts + first + j), tail, 0.0),
+                axis=1,
+                keepdims=True,
+            )
+            for j in range(owned)
+        ]
+        weight = weights[0]
+        for j in range(1, owned):
+            weight = jnp.where(unit >= j * hidden, weights[j], weight)
+        sigmoid = 1.0 / (1.0 + jnp.exp(-gate))
+        activated = gate * sigmoid
+        inner = activated * up
+        weighted = (inner * weight).astype(LOW)
+
+        @pl.when(i >= 2)
+        def _():
+            store(i - 2).wait()
+
+        outgoing[i % 2] = dot(weighted, down_ref[...], 1, 0).astype(LOW)
+        store(i).start()
+        fetch(i).wait()
+
+        @pl.when(i + 1 < count)
+        def _():
+            fetch(i + 1).start()
+
+        u = upstream[i % 2]
+        down_back = dot(u, down_ref[...], 1, 1)
+        down_grad_ref[...] += dot(weighted, u, 0, 0)
+        product = inner * down_back
+        note = jnp.zeros((group, extra), F32)
+        for j in range(owned):
+            mine = (unit >= j * hidden) & (unit < (j + 1) * hidden)
+            route_grad = jnp.sum(jnp.where(mine, product, 0.0), axis=1, keepdims=True)
+            note = jnp.where(lane == first + j, route_grad, note)
+        inner_grad = down_back * weight
+        gate_back = (inner_grad * up * sigmoid * (1.0 + gate * (1.0 - sigmoid))).astype(LOW)
+        up_back = (inner_grad * activated).astype(LOW)
+        back_rows[at, :units] = gate_back
+        back_rows[at, units:] = up_back
+        part[at, :width] = (
+            dot(gate_back, gate_up_ref[:, :units], 1, 1) + dot(up_back, gate_up_ref[:, units:], 1, 1)
+        ).astype(LOW)
+        part[at, width:] = note.astype(LOW)
+
+    share = columns_ref.shape[1]
+    columns = pltpu.make_async_copy(
+        all_ref.at[:, pl.ds(pl.multiple_of(p.e * share, share), share)],
+        columns_ref,
+        local_sems.at[0],
+    )
+    columns.start()
+    tile = width // count
+
+    @pl.loop(0, count)
+    def _(i):
+        for k, step in enumerate(scattering):
+            pl.when(i == k)(step)
+        at = pl.ds(pl.multiple_of(i * tile, tile), tile)
+        gate_up_grad_ref[at, :] = dot(all_ref[:, at], back_rows[...], 0, 0)
+
+    gather_copies.finish()
+    scatter_copies.finish()
+    store(count - 2).wait()
+    store(count - 1).wait()
+    columns.wait()
+
+
+def run_experts(own, upstream_all, gate_up, down, owned, experts, width, collective_id):
+    rows, full = own.shape
+    total = upstream_all.shape[0]
+    units = down.shape[0]
+    owners = lax.axis_size("expert")
+    group = rows * lax.axis_size("tensor")
+    return pl.pallas_call(
+        functools.partial(experts_kernel, rows, width, experts, owned),
+        out_shape=(
+            jax.ShapeDtypeStruct((rows, full), F32),
+            jax.ShapeDtypeStruct((total, width), LOW),
+            jax.ShapeDtypeStruct((total, width // owners), LOW),
+            jax.ShapeDtypeStruct((width, 2 * units), F32),
+            jax.ShapeDtypeStruct((units, width), F32),
+        ),
+        in_specs=[VMEM_SPEC, ANY_SPEC, VMEM_SPEC, VMEM_SPEC],
+        out_specs=(VMEM_SPEC, ANY_SPEC, ANY_SPEC, VMEM_SPEC, VMEM_SPEC),
+        scratch_shapes=[
+            pltpu.VMEM((total, full), LOW),
+            pltpu.VMEM((2, group, width), LOW),
+            pltpu.VMEM((2, group, width), LOW),
+            pltpu.VMEM((total, full), LOW),
+            pltpu.VMEM((total, 2 * units), LOW),
+        ]
+        + scatter_scratch(rows, full)
+        + semaphores(6, GATHER_SEMS, GATHER_SEMS, SCATTER_SEMS, SCATTER_SEMS),
+        compiler_params=pltpu.CompilerParams(
+            collective_id=collective_id, has_side_effects=True, vmem_limit_bytes=64000000
+        ),
+        name="experts",
+    )(own, upstream_all, gate_up, down)
+
+
+def gathered_shards(
+    tokens,
+    seq_length,
+    expert_routes,
+    attention_gain,
+    query_weight,
+    key_weight,
+    value_weight,
+    query_gain,
+    key_gain,
+    output_weight,
+    routing_gain,
+    router_weight,
+    gate_weight,
+    up_weight,
+    down_weight,
+    cotangent,
+):
+    count, width = tokens.shape
+    head_size = query_gain.shape[0]
+    local_heads = query_weight.shape[1] // head_size
+    local_groups = key_weight.shape[1] // head_size
+    ratio = local_heads // local_groups
+    length = seq_length[0]
+    experts = router_weight.shape[1]
+    owned = gate_weight.shape[0]
+    parts = lax.axis_size("tensor")
+    part = lax.axis_index("tensor")
+    owner = lax.axis_index("expert")
+    rows = count // parts
+    everywhere = ("expert", "tensor")
+    low = jnp.bfloat16
+
+    def own_rows(values):
+        return lax.dynamic_slice_in_dim(values, part * rows, rows, 0)
+
+    upstream_all = gather_rows(own_rows(cotangent), 0)
+    inputs = tokens.astype(jnp.float32)
+    scale1 = rms_scale(inputs)
+    normed1 = inputs * scale1
+    xnorm1 = (normed1 * attention_gain).astype(low)
+    xnorm1_columns = lax.all_to_all(xnorm1, "expert", split_axis=1, concat_axis=0, tiled=True)
+    query_raw = jnp.dot(xnorm1, query_weight, preferred_element_type=jnp.float32).reshape(
+        count, local_heads, head_size
+    )
+    key_raw = jnp.dot(xnorm1, key_weight, preferred_element_type=jnp.float32).reshape(
+        count, local_groups, head_size
+    )
+    value_low = (
+        jnp.dot(xnorm1, value_weight, preferred_element_type=jnp.float32)
+        .astype(low)
+        .reshape(count, local_groups, head_size)
+    )
+    query_gained, query_normed, query_scale = head_norm(query_raw, query_gain)
+    key_gained, key_normed, key_scale = head_norm(key_raw, key_gain)
+    cosine, sine = rope_tables(count, head_size)
+    query_low = rotate(query_gained, cosine, sine).astype(low)
+    key_low = rotate(key_gained, cosine, sine).astype(low)
+    query_block = query_low.reshape(count, local_groups, ratio, head_size)
+    outputs, lse = attend_block(query_block, 0, key_low, value_low, length)
+    valid = (jnp.arange(count, dtype=jnp.int32) < length)[:, None]
+    heads_low = jnp.where(valid, outputs.reshape(count, local_heads * head_size), 0.0).astype(low)
+    attention_part = contract(heads_low, output_weight, 1, 1)
+    attention = lax.psum_scatter(
+        attention_part.astype(low), "tensor", scatter_dimension=0, tiled=True
+    ).astype(jnp.float32)
+    heads_all = lax.all_gather(heads_low, "expert", axis=0, tiled=True)
+
+    hidden = own_rows(inputs) + attention
+    scale2 = rms_scale(hidden)
+    normed2 = hidden * scale2
+    xnorm2 = (normed2 * routing_gain).astype(low)
+    logits = jnp.dot(xnorm2, router_weight, preferred_element_type=jnp.float32)
+    peak = jnp.max(logits, axis=1, keepdims=True)
+    expo = jnp.exp(logits - peak)
+    router = expo / jnp.sum(expo, axis=1, keepdims=True)
+    routes = own_rows(expert_routes)
+    named = jnp.any(
+        routes[:, :, None] == jnp.arange(experts, dtype=jnp.int32)[None, None, :], axis=1
+    )
+    chosen = jnp.where(named, router, 0.0)
+    chosen_total = jnp.sum(chosen, axis=1, keepdims=True)
+    route_weight = chosen / chosen_total
+
+    high = route_weight.astype(low)
+    rest = (route_weight - high.astype(jnp.float32)).astype(low)
+    spare = jnp.zeros((rows, 128 - 2 * experts), low)
+    own = jnp.concatenate([xnorm2, high, rest, spare], axis=1)
+    gate_up = jnp.concatenate([*gate_weight, *up_weight], axis=1)
+    summed, moe_part, columns, gate_up_grad, down_grad = run_experts(
+        own, upstream_all, gate_up, down_weight.reshape(-1, width), owned, experts, width, 1
+    )
+    units = gate_up.shape[1] // (2 * owned)
+    split = [gate_up_grad[:, j * units : (j + 1) * units] for j in range(2 * owned)]
+    gate_grad, up_grad = jnp.stack(split[:owned]), jnp.stack(split[owned:])
+    down_grad = down_grad.reshape(down_weight.shape)
+    moe = scatter_rows(moe_part, 2)
+    mixed = lax.all_gather((hidden + moe).astype(low), "tensor", axis=0, tiled=True)
+    xnorm2_moe, route_grad = summed[:, :width], summed[:, width : width + experts]
+
+    upstream = own_rows(cotangent).astype(jnp.float32)
+    inner_total = jnp.sum(route_grad * route_weight, axis=1, keepdims=True)
+    prob_grad = jnp.where(named, (route_grad - inner_total) / chosen_total, 0.0)
+    logit_low = (router * (prob_grad - jnp.sum(router * prob_grad, axis=1, keepdims=True))).astype(
+        low
+    )
+    logit_all = lax.all_gather(logit_low, everywhere, axis=0, tiled=True)
+    router_grad = contract(columns, logit_all, 0, 0)
+    xnorm2_grad = xnorm2_moe + contract(logit_low, router_weight, 1, 1)
+    routing_gain_part = jnp.sum(xnorm2_grad * normed2, axis=0)
+    inner2 = xnorm2_grad * routing_gain
+    hidden_grad = upstream + scale2 * (
+        inner2 - normed2 * jnp.mean(inner2 * normed2, axis=1, keepdims=True)
+    )
+    hidden_low = lax.all_gather(hidden_grad.astype(low), "tensor", axis=0, tiled=True)
+    hidden_columns = lax.all_to_all(hidden_low, "expert", split_axis=1, concat_axis=0, tiled=True)
+    output_grad = contract(hidden_columns, heads_all, 0, 0)
+    heads_grad = jnp.where(
+        valid,
+        jnp.dot(hidden_low, output_weight, preferred_element_type=jnp.float32).astype(low),
+        jnp.zeros((), low),
+    ).reshape(count, local_groups, ratio, head_size)
+    query_rot_grad, key_rot_grad, value_grad = attend_back(
+        query_block, heads_grad, lse, 0, key_low, value_low, length
+    )
+    query_back, query_gain_part = head_norm_back(
+        rotate_back(query_rot_grad.reshape(count, local_heads, head_size), cosine, sine),
+        query_normed,
+        query_scale,
+        query_gain,
+    )
+    key_back, key_gain_part = head_norm_back(
+        rotate_back(key_rot_grad, cosine, sine), key_normed, key_scale, key_gain
+    )
+    query_grad_low = query_back.reshape(count, local_heads * head_size).astype(low)
+    key_grad_low = key_back.reshape(count, local_groups * head_size).astype(low)
+    value_grad_low = value_grad.reshape(count, local_groups * head_size).astype(low)
+    packed = jnp.concatenate([query_grad_low, key_grad_low, value_grad_low], axis=1)
+    packed_all = lax.all_gather(packed, "expert", axis=0, tiled=True)
+    packed_grad = contract(xnorm1_columns, packed_all, 0, 0)
+    query_end = local_heads * head_size
+    key_end = query_end + local_groups * head_size
+    xnorm1_part = contract(query_grad_low, query_weight, 1, 1) + contract(
+        key_grad_low, key_weight, 1, 1
+    )
+    xnorm1_part = xnorm1_part + contract(value_grad_low, value_weight, 1, 1)
+    xnorm1_grad = lax.psum_scatter(
+        xnorm1_part.astype(low), "tensor", scatter_dimension=0, tiled=True
+    ).astype(jnp.float32)
+    normed1_own = own_rows(normed1)
+    attention_gain_part = jnp.sum(xnorm1_grad * normed1_own, axis=0)
+    inner1 = xnorm1_grad * attention_gain
+    tokens_grad = (
+        hidden_grad
+        + own_rows(scale1)
+        * (inner1 - normed1_own * jnp.mean(inner1 * normed1_own, axis=1, keepdims=True))
+    ).astype(low)
+    tokens_grad = lax.all_gather(tokens_grad, "tensor", axis=0, tiled=True)
+    gains = lax.psum(
+        jnp.concatenate([attention_gain_part, routing_gain_part, query_gain_part, key_gain_part]),
+        everywhere,
+    )
+
+    def own_share(start, size):
+        share = size // lax.axis_size("expert")
+        return lax.dynamic_slice_in_dim(gains, start + owner * share, share, 0)
+
+    return (
+        mixed,
+        tokens_grad,
+        own_share(0, width),
+        packed_grad[:, :query_end],
+        packed_grad[:, query_end:key_end],
+        packed_grad[:, key_end:],
+        own_share(2 * width, head_size),
+        own_share(2 * width + head_size, head_size),
+        output_grad,
+        own_share(width, width),
+        router_grad,
+        gate_grad,
+        up_grad,
+        down_grad,
+    )
+
 def solution(mesh):
+    sizes = dict(mesh.shape)
+    fits = sizes["expert"] == 2 * DEPTH and sizes["tensor"] == 4
     return jax.shard_map(
-        shards,
+        gathered_shards if fits else routed_shards,
         mesh=mesh,
         in_specs=(
             P("expert", None),

time: 1210 us -> 588 us (0.49)
  waiting for transfers between devices: 737 us -> 88.7 us
  Pallas kernels: 0 us -> 219 us
  matrix products: 92.7 us -> 32.9 us
  blocking collectives: 162 us -> 105 us
  other arithmetic: 86.9 us -> 41.2 us
  local copies, waits for them, and re-layouts: 92.9 us -> 66.9 us
    reduce_scatter x8 -> x2, waiting for transfers between devices: 503 us -> 0.02 us  [the longest x1 0.02 us: gathered_shards(): lax.psum_scatter(xnorm1_part.astype(low), 'tensor', scatter_dimension=0,...]
    pallas_call x0 -> x3, Pallas kernels: none -> 219 us  [the longest x1 118 us: run_experts(): pl.pallas_call(functools.partial(experts_kernel, rows, width, experts, ow...]
    all_to_all x2 -> x0, blocking collectives: 128 us -> none  [the longest x1 64.8 us: shards(): lax.all_to_all(send_rows, 'expert', split_axis=1, concat_axis=1, tiled=True)]
    all_to_all x2, waiting for transfers between devices: 108 us -> 0.01 us  [the longest x1 0.01 us: gathered_shards(): lax.all_to_all(xnorm1, 'expert', split_axis=1, concat_axis=0, tiled=True)]
    psum x3 -> x0, waiting for transfers between devices: 72.9 us -> none  [the longest x1 38 us: shards(): attention_full = lax.psum(attention_part, 'tensor')]
    dot_general x14 -> x5, matrix products: 64.1 us -> 7.16 us  [the longest x1 3.76 us: gathered_shards(): jnp.dot(hidden_low, output_weight, preferred_element_type=jnp.float32)]
    all_gather x0 -> x1, blocking collectives: none -> 51.3 us  [gathered_shards(): logit_all = lax.all_gather(logit_low, everywhere, axis=0, tiled=True)]
    psum x2 -> x1, blocking collectives: 11.6 us -> 53.4 us  [gathered_shards(): lax.psum(jnp.concatenate([attention_gain_part, routing_gain_part, query_g...]
  transfers between devices with their start and end apart: 16 -> 9, of which waited for: 15 -> 2; matrix products, arithmetic and copies ran while one was open for 10% -> 9% of each run, Pallas kernels for 0% -> 17%
where the time goes in v1:
time: 588 us; the launch traced here: 580 us
  Pallas kernels  219 us (37%)
  blocking collectives  105 us (18%)
  waiting for transfers between devices  88.7 us (15%)
  local copies, waits for them, and re-layouts  66.9 us (11%)
  other arithmetic  41.2 us (7%)
  matrix products  32.9 us (6%)
  between operations  16.2 us (3%)
  starting transfers between devices  10.9 us (2%)
    pallas_call x1, Pallas kernels, run_experts(): pl.pallas_call(functools.partial(experts_kernel, rows, width, experts, ow...  118 us
    all_gather x1, waiting for transfers between devices, gathered_shards(): packed_all = lax.all_gather(packed, 'expert', axis=0, tiled=True)  69.6 us
    psum x1, blocking collectives, gathered_shards(): lax.psum(jnp.concatenate([attention_gain_part, routing_gain_part, query_g...  53.4 us
    pallas_call x1, Pallas kernels, gather_rows(): pl.pallas_call(functools.partial(gather_kernel, rows), out_shape=jax.Shap...  53.2 us
    all_gather x1, blocking collectives, gathered_shards(): logit_all = lax.all_gather(logit_low, everywhere, axis=0, tiled=True)  51.3 us
    pallas_call x1, Pallas kernels, scatter_rows(): pl.pallas_call(functools.partial(scatter_kernel, rows), out_shape=jax.Sha...  47.6 us
    unnamed x133, local copies, waits for them, and re-layouts  31.8 us
    dot_general x8, matrix products, contract(): lax.dot_general(left, right, (((left_dim,), (right_dim,)), ((), ())), pre...  22.1 us
  transfers between devices with their start and end apart: 9, of which 2 were waited for; matrix products, arithmetic and copies ran while one was open for 9% of the time, Pallas kernels for 17%

profile of v1, /device:TPU:0, one launch (start us, length us, event | category | flops | bytes accessed | tf_op | source)
XLA Modules:
  0.0 580.5 jit_solution(14762356694145736122)
XLA Ops:
  8.8 3.0 broadcast_multiply_fusion
  17.7 2.5 copy.250
  25.6 2.5 copy.251
  30.5 3.3 fusion.27
  40.1 4.6 convolution_convert_fusion
  45.0 2.8 convert_element_type.99
  49.6 53.2 %gather_rows.1.upstream_ref = bf16[2048,2048]{1,0:T(8,128)(2,1)} custom-call(bf16[64,2048]{1,0:T(8,128)(2,1)} %constant_dynamic-slice_fusion.own_ref), custom_call_target="tpu_custom_call" | custom-call | tf_op jit(solution)/shard_map/gather_rows/pallas_call | solution.py:735
  102.8 2.7 fusion.53
  105.6 2.2 copy.259
  107.8 2.2 copy.258
  110.0 2.7 fusion.52
  112.7 2.2 copy.257
  114.9 2.2 copy.256
  117.2 4.7 pad_maximum_fusion.2.gate_up_ref
  126.1 117.9 %experts.1 = (f32[64,2176]{1,0:T(8,128)}, bf16[2048,2048]{1,0:T(8,128)(2,1)}, bf16[2048,256]{1,0:T(8,128)(2,1)}, f32[2048,768]{1,0:T(8,128)}, f32[384,2048]{1,0:T(8,128)}) custom-call(bf16[64,2176]{1,0:T(8,128)(2,1)} %concatenate.46.own_ref, bf16[2048,2048]{1,0:T(8,128)(2,1)} %gather_rows.1.upstream_ref, bf16[2048,768]{1,0:T(8,128)(2,1)} %pad_maximum_fusion.2.gate_up_ref, ...), custom_call_target="tpu_custom_call" | custom-call | tf_op jit(solution)/shard_map/experts/pallas_call | solution.py:925
  251.6 18.0 %all-gather.9.cloned.1.call-done = bf16[256,2048]{1,0:T(8,128)(2,1)} async-done(((bf16[64,2048]{1,0:T(8,128)(2,1)}), bf16[256,2048]{1,0:T(8,128)(2,1)}) %all-gather.9.cloned.1.call-update) | async-done | bytes 1048592 | tf_op jit(solution)/shard_map/all_gather | solution.py:1066
  269.6 3.8 fusion.6
  282.0 3.1 fusion.16
  285.4 2.6 fusion.62
  294.7 47.6 %scatter_rows.1 = f32[64,2048]{1,0:T(8,128)} custom-call(bf16[2048,2048]{1,0:T(8,128)(2,1)} %get-tuple-element.19.part_ref), custom_call_target="tpu_custom_call" | custom-call | tf_op jit(solution)/shard_map/scatter_rows/pallas_call | solution.py:763
  343.6 2.4 fusion.25
  350.4 6.7 %all-to-all-start.1 = ((bf16[256,8,256]{2,0,1:T(8,128)(2,1)}), bf16[256,8,256]{2,0,1:T(8,128)(2,1)S(1)}, u32[]{:S(2)}, u32[]{:S(2)}) async-start(bf16[256,8,256]{2,0,1:T(8,128)(2,1)} %bitcast.201), calls=%async_computation.3 | async-start | bytes 2097152 | tf_op jit(solution)/shard_map/all_to_all | solution.py:1067
  358.2 51.3 %all-gather = bf16[32,64,16]{1,2,0:T(8,128)(2,1)S(1)} all-gather(bf16[1,64,16]{1,2,0:T(8,128)(2,1)S(1)} %copy.238), channel_id=1, replica_groups=mesh['expert'=8,'tensor'=4] {'expert','tensor'}, dimensions={0}, use_global_device_ids=true | all-gather | bytes 67584 | tf_op jit(solution)/shard_map/all_gather | solution.py:1058
  409.8 3.6 all-to-all-start
  413.4 5.1 slice_bitcast_fusion.1
  418.5 4.0 pad_maximum_fusion
  422.5 5.2 copy.240
  427.8 5.3 copy.241
  433.9 53.4 %psum.7 = f32[4352]{0:T(1024)S(1)} all-reduce(f32[4352]{0:T(1024)S(1)} %pad_maximum_fusion.7), channel_id=1, replica_groups=mesh['expert'=8,'tensor'=4] {'expert','tensor'}, use_global_device_ids=true, to_apply=%region_23.24 | all-reduce | flops 4352 | bytes 34816 | tf_op jit(solution)/shard_map/psum | solution.py:1110
  488.6 4.8 fusion.64
  493.4 69.6 %all-gather.13.cloned.1.call-done = bf16[2048,1280]{1,0:T(8,128)(2,1)} async-done(((bf16[256,1280]{1,0:T(8,128)(2,1)}), bf16[2048,1280]{1,0:T(8,128)(2,1)}) %all-gather.13.cloned.1.call-update) | async-done | bytes 5242896 | tf_op jit(solution)/shard_map/all_gather | solution.py:1090
  563.0 4.0 fusion.63
  (231 shorter events, 64.7 us)
Async XLA Ops:
  7.2 14.6 %copy-start = (bf16[2048,128]{1,0:T(8,128)(2,1)S(1)}, bf16[2048,128]{1,0:T(8,128)(2,1)}, u32[]{:S(2)}) copy-start(bf16[2048,128]{1,0:T(8,128)(2,1)} %param.21) | copy-start | bytes 1572868
  7.2 114.6 %reduce-scatter.3.cloned.1.call-start = ((), (), s32[]{:S(2)}) async-start(), calls=%async_computation.4 | async-start | bytes 1310720 | tf_op jit(solution)/shard_map/reduce_scatter | solution.py:1015
  11.8 17.2 %copy-start.1 = (bf16[256,2048]{1,0:T(8,128)(2,1)}, bf16[256,2048]{1,0:T(8,128)(2,1)S(1)}, u32[]{:S(2)}) copy-start(bf16[256,2048]{1,0:T(8,128)(2,1)S(1)} %get-tuple-element.148) | copy-start | bytes 3145732
  16.3 4.1 copy-start.6
  16.3 3.8 copy-start.51
  23.2 4.9 copy-start.10
  28.9 9.2 %copy-start.55 = (pred[256]{0:T(512)(128)(4,1)}, pred[256]{0:T(512)(128)(4,1)S(1)}, u32[]{:S(2)}) copy-start(pred[256]{0:T(512)(128)(4,1)S(1)} %iota_compare_fusion.2) | copy-start | bytes 772
  30.5 4.2 copy-start.36
  30.5 3.3 copy-start.32
  44.7 224.8 %all-gather.9.cloned.1.call-start = ((), (), s32[]{:S(2)}) async-start(), calls=%async_computation.6 | async-start | bytes 1310720 | tf_op jit(solution)/shard_map/all_gather | solution.py:1066
  117.2 6.8 %copy-start.39 = (f32[2048]{0:T(1024)S(1)}, f32[2048]{0:T(1024)}, u32[]{:S(2)}) copy-start(f32[2048]{0:T(1024)} %param.26) | copy-start | bytes 24580
  126.1 118.0 %copy-start.44 = (f32[64]{0:T(128)S(1)}, f32[64]{0:T(128)}, u32[]{:S(2)}) copy-start(f32[64]{0:T(128)} %copy-done.43) | copy-start | bytes 772
  126.1 118.0 %copy-start.46 = (f32[64]{0:T(128)S(1)}, f32[64]{0:T(128)}, u32[]{:S(2)}) copy-start(f32[64]{0:T(128)} %copy-done.45) | copy-start | bytes 772
  244.1 5.3 copy-start.4
  244.1 7.5 %copy-start.42 = (f32[8,256]{1,0:T(8,128)S(1)}, f32[8,256]{1,0:T(8,128)}, u32[]{:S(2)}) copy-start(f32[8,256]{1,0:T(8,128)} %copy-done.41) | copy-start | bytes 24580
  244.1 25.5 %copy-start.56 = (pred[256]{0:T(512)(128)(4,1)S(1)}, pred[256]{0:T(512)(128)(4,1)}, u32[]{:S(2)}) copy-start(pred[256]{0:T(512)(128)(4,1)} %copy-done.55) | copy-start | bytes 772
  251.3 91.1 %reduce-scatter.5.cloned.1.call-start = ((), (), s32[]{:S(2)}) async-start(), calls=%async_computation.7 | async-start | bytes 1310720 | tf_op jit(solution)/shard_map/reduce_scatter | solution.py:1098
  251.6 21.8 %copy-start.37 = (bf16[256,128,1]{1,0,2:T(8,128)(2,1)S(1)}, bf16[256,128,1]{1,0,2:T(8,128)(2,1)}, u32[]{:S(2)}) copy-start(bf16[256,128,1]{1,0,2:T(8,128)(2,1)} %copy-done.36) | copy-start | bytes 196612
  282.0 3.5 copy-start.59
  294.6 194.0 %all-gather.7.cloned.1.call-start = ((), (), s32[]{:S(2)}) async-start(), calls=%async_computation.5 | async-start | bytes 1310720 | tf_op jit(solution)/shard_map/all_gather | solution.py:1049
  294.7 47.7 %copy-start.15 = (f32[256,2048]{1,0:T(8,128)S(1)}, f32[256,2048]{1,0:T(8,128)}, u32[]{:S(2)}) copy-start(f32[256,2048]{1,0:T(8,128)} %get-tuple-element.147) | copy-start | bytes 6291460
  294.7 47.7 %copy-start.40 = (f32[2048]{0:T(1024)S(1)}, f32[2048]{0:T(1024)}, u32[]{:S(2)}) copy-start(f32[2048]{0:T(1024)} %param.19) | copy-start | bytes 24580
  294.7 48.9 %copy-start.5 = (f32[64,2048]{1,0:T(8,128)S(1)}, f32[64,2048]{1,0:T(8,128)}, u32[]{:S(2)}) copy-start(f32[64,2048]{1,0:T(8,128)} %copy-done.3) | copy-start | bytes 1572868
  294.7 48.9 %copy-start.48 = (f32[64]{0:T(128)S(1)}, f32[64]{0:T(128)}, u32[]{:S(2)}) copy-start(f32[64]{0:T(128)} %copy-done.47) | copy-start | bytes 772
  346.0 142.6 %all-gather.11.cloned.1.call-start = ((), (), s32[]{:S(2)}) async-start(), calls=%async_computation.8 | async-start | bytes 1310720 | tf_op jit(solution)/shard_map/all_gather | solution.py:1109
  346.6 142.0 %all-gather.15.cloned.1.call-start = ((), (), s32[]{:S(2)}) async-start(), calls=%async_computation.10 | async-start | bytes 4718592 | tf_op jit(solution)/shard_map/all_gather | solution.py:1018
  347.2 215.8 %all-gather.13.cloned.1.call-start = ((), (), s32[]{:S(2)}) async-start(), calls=%async_computation.9 | async-start | bytes 5898240 | tf_op jit(solution)/shard_map/all_gather | solution.py:1090
  349.3 7.8 %copy-start.2 = (bf16[256,2048]{1,0:T(8,128)(2,1)S(1)}, bf16[256,2048]{1,0:T(8,128)(2,1)}, u32[]{:S(2)}) copy-start(bf16[256,2048]{1,0:T(8,128)(2,1)} %copy-done.1) | copy-start | bytes 3145732
  350.4 59.4 %all-to-all-start.1 = ((bf16[256,8,256]{2,0,1:T(8,128)(2,1)}), bf16[256,8,256]{2,0,1:T(8,128)(2,1)S(1)}, u32[]{:S(2)}, u32[]{:S(2)}) async-start(bf16[256,8,256]{2,0,1:T(8,128)(2,1)} %bitcast.201), calls=%async_computation.3 | async-start | bytes 2097152 | tf_op jit(solution)/shard_map/all_to_all | solution.py:1067
  409.8 8.7 %copy-start.31 = (bf16[256,8,256]{2,0,1:T(8,128)(2,1)}, bf16[256,8,256]{2,0,1:T(8,128)(2,1)S(1)}, u32[]{:S(2)}) copy-start(bf16[256,8,256]{2,0,1:T(8,128)(2,1)S(1)} %all-to-all-done.1) | copy-start | bytes 3145732
  409.8 83.6 %all-to-all-start = ((bf16[256,8,256]{2,0,1:T(8,128)(2,1)}), bf16[256,8,256]{2,0,1:T(8,128)(2,1)S(1)}, u32[]{:S(2)}, u32[]{:S(2)}) async-start(bf16[256,8,256]{2,0,1:T(8,128)(2,1)} %bitcast.202), calls=%async_computation.2 | async-start | bytes 2097152 | tf_op jit(solution)/shard_map/all_to_all | solution.py:993
  427.8 5.3 copy-start.27
  (37 other events, 66.0 us)
Sparse Core Ops, SparseCore 0:
  44.9 32.1 reduce-scatter.2
  251.4 18.0 all-gather.8
  294.7 30.6 reduce-scatter.4
  346.2 18.8 all-gather.6
  367.0 16.6 all-gather.10
  385.8 89.3 all-gather.14
  477.9 85.0 all-gather.12

commit v2 on v1

--- a/solution.py
+++ b/solution.py
@@ -782,9 +782,10 @@
     upstream_ref,
     gate_up_ref,
     down_ref,
+    heads_ref,
     grad_ref,
     moe_ref,
-    columns_ref,
+    line_heads_ref,
     gate_up_grad_ref,
     down_grad_ref,
     all_ref,
@@ -801,6 +802,8 @@
     gather_recv,
     scatter_send,
     scatter_recv,
+    heads_send,
+    heads_recv,
 ):
     p = Place()
     group = rows * 4
@@ -815,6 +818,11 @@
     gathering = gather_steps(p, gather_copies, rows, own_ref, all_ref, own_copy)
     scattering = scatter_steps(
         p, scatter_copies, rows, part, core_in, diag_in, side_in, line_in, grad_ref
+    )
+    heads_copies = Copies(heads_send, heads_recv)
+    others = [p.near(k) for k in range(1, DEPTH)]
+    heads_line = heads_copies.along(
+        [(z, heads_ref, line_heads_ref.at[p.z]) for z in others], [p.at(z=z) for z in others], p.z
     )
     count = 2 * DEPTH
 
@@ -893,13 +901,8 @@
         ).astype(LOW)
         part[at, width:] = note.astype(LOW)
 
-    share = columns_ref.shape[1]
-    columns = pltpu.make_async_copy(
-        all_ref.at[:, pl.ds(pl.multiple_of(p.e * share, share), share)],
-        columns_ref,
-        local_sems.at[0],
-    )
-    columns.start()
+    for there, _ in heads_line:
+        there.start()
     tile = width // count
 
     @pl.loop(0, count)
@@ -913,25 +916,26 @@
     scatter_copies.finish()
     store(count - 2).wait()
     store(count - 1).wait()
-    columns.wait()
-
-
-def run_experts(own, upstream_all, gate_up, down, owned, experts, width, collective_id):
+    for _, back in heads_line:
+        back.wait_recv()
+    heads_copies.finish()
+
+
+def run_experts(own, upstream_all, gate_up, down, heads, owned, experts, width, collective_id):
     rows, full = own.shape
     total = upstream_all.shape[0]
     units = down.shape[0]
-    owners = lax.axis_size("expert")
     group = rows * lax.axis_size("tensor")
     return pl.pallas_call(
         functools.partial(experts_kernel, rows, width, experts, owned),
         out_shape=(
             jax.ShapeDtypeStruct((rows, full), F32),
             jax.ShapeDtypeStruct((total, width), LOW),
-            jax.ShapeDtypeStruct((total, width // owners), LOW),
+            jax.ShapeDtypeStruct((DEPTH, *heads.shape), LOW),
             jax.ShapeDtypeStruct((width, 2 * units), F32),
             jax.ShapeDtypeStruct((units, width), F32),
         ),
-        in_specs=[VMEM_SPEC, ANY_SPEC, VMEM_SPEC, VMEM_SPEC],
+        in_specs=[VMEM_SPEC, ANY_SPEC, VMEM_SPEC, VMEM_SPEC, ANY_SPEC],
         out_specs=(VMEM_SPEC, ANY_SPEC, ANY_SPEC, VMEM_SPEC, VMEM_SPEC),
         scratch_shapes=[
             pltpu.VMEM((total, full), LOW),
@@ -941,12 +945,477 @@
             pltpu.VMEM((total, 2 * units), LOW),
         ]
         + scatter_scratch(rows, full)
-        + semaphores(6, GATHER_SEMS, GATHER_SEMS, SCATTER_SEMS, SCATTER_SEMS),
+        + semaphores(5, GATHER_SEMS, GATHER_SEMS, SCATTER_SEMS, SCATTER_SEMS, DEPTH, DEPTH),
         compiler_params=pltpu.CompilerParams(
             collective_id=collective_id, has_side_effects=True, vmem_limit_bytes=64000000
         ),
         name="experts",
-    )(own, upstream_all, gate_up, down)
+    )(own, upstream_all, gate_up, down, heads)
+
+
+def normed_rows(values):
+    scale = lax.rsqrt(jnp.mean(values * values, axis=-1, keepdims=True) + EPSILON)
+    return values * scale, scale
+
+
+def turned(values):
+    return pltpu.roll(values, values.shape[-1] // 2, values.ndim - 1)
+
+
+def allowed_keys(count, length):
+    row = lax.broadcasted_iota(jnp.int32, (count, count), 0)
+    column = lax.broadcasted_iota(jnp.int32, (count, count), 1)
+    return (column <= row) & (column < length)
+
+
+def attention_probs(query, key, allowed):
+    factor = query.shape[-1] ** (-0.5)
+    scores = jnp.where(allowed, dot(query, key, 1, 1) * factor, NEGATIVE)
+    expo = jnp.exp(scores - jnp.max(scores, axis=-1, keepdims=True))
+    return expo / jnp.sum(expo, axis=-1, keepdims=True)
+
+
+class Spread:
+    def __init__(self, p, copies, slot):
+        other = (1 - p.x) * 2 + p.c
+        self.to_x = copies.make(slot(p.t), slot(p.t), p.at(x=1 - p.x))
+        self.to_c = copies.make(slot(p.t), slot(p.t), p.at(c=1 - p.c))
+        self.onward = copies.make(slot(other), slot(other), p.at(c=1 - p.c))
+
+    def start(self):
+        self.to_x.start()
+        self.to_c.start()
+
+    def forward(self):
+        self.to_x.wait_recv()
+        self.onward.start()
+
+    def finish(self):
+        self.to_c.wait_recv()
+        self.onward.wait_recv()
+
+
+SPREAD_SEMS = 3
+TAIL_SEMS = 4 * SPREAD_SEMS + DEPTH + DEPTH + 2 + 2 * DEPTH + 1 + 3 + 3 + DEPTH
+
+
+def tail_kernel(
+    rows,
+    length_ref,
+    hidden_low_ref,
+    hidden_grad_ref,
+    hidden_ref,
+    tokens_ref,
+    xnorm1_ref,
+    small_ref,
+    moe_ref,
+    heads_ref,
+    line_heads_ref,
+    query_ref,
+    key_ref,
+    value_ref,
+    cosine_ref,
+    sine_ref,
+    attention_gain_ref,
+    query_gain_ref,
+    key_gain_ref,
+    query_weight_ref,
+    key_weight_ref,
+    value_weight_ref,
+    output_weight_ref,
+    mixed_ref,
+    tokens_grad_ref,
+    output_grad_ref,
+    packed_grad_ref,
+    small_out_ref,
+    hidden_all,
+    hidden_line,
+    line_heads,
+    heads_grad,
+    packed,
+    packed_in,
+    xnorm_in,
+    weight_out,
+    weight_in,
+    output_out,
+    output_in,
+    key_sum,
+    value_sum,
+    back_part,
+    back_in,
+    moe,
+    moe_own,
+    small,
+    small_in,
+    small_side,
+    small_line,
+    core_in,
+    diag_in,
+    side_in,
+    line_in,
+    local_sems,
+    send_sems,
+    recv_sems,
+    scatter_send,
+    scatter_recv,
+):
+    p = Place()
+    group, width = xnorm1_ref.shape
+    units = query_ref.shape[1]
+    size = cosine_ref.shape[1]
+    count = units // size
+    packed_width = packed.shape[1]
+    share = width // (2 * DEPTH)
+    length = length_ref[0]
+    fetch = [
+        pltpu.make_async_copy(moe_ref, moe, local_sems.at[0]),
+        *[
+            pltpu.make_async_copy(
+                line_heads_ref.at[p.near(k)], line_heads.at[p.near(k)], local_sems.at[k]
+            )
+            for k in range(1, DEPTH)
+        ],
+    ]
+    for copy in fetch:
+        copy.start()
+    enter(p.peers())
+    copies = Copies(send_sems, recv_sems)
+    scatter_copies = Copies(scatter_send, scatter_recv)
+    scattering = scatter_steps(
+        p, scatter_copies, rows, moe, core_in, diag_in, side_in, line_in, moe_own
+    )
+    xn, yn, cn = p.at(x=1 - p.x), p.at(y=1 - p.y), p.at(c=1 - p.c)
+    order = [p.near(k) for k in reversed(range(DEPTH))]
+    along = [p.at(z=z) for z in order[: DEPTH - 1]]
+
+    def columns(z, y):
+        return pl.ds(pl.multiple_of((z * 2 + y) * share, share), share)
+
+    def block(ref, t):
+        return ref.at[pl.ds(pl.multiple_of(t * rows, rows), rows)]
+
+    hidden_spread = Spread(p, copies, lambda t: block(hidden_all, t))
+    line_spread = Spread(p, copies, lambda t: hidden_line.at[t])
+    hidden_to = copies.along(
+        [
+            (
+                z,
+                hidden_low_ref.at[:, pl.ds(pl.multiple_of(z * 2 * share, share), 2 * share)],
+                hidden_line.at[p.t, p.z],
+            )
+            for z in order[: DEPTH - 1]
+        ],
+        along,
+        p.z,
+    )
+    xnorm_to = [
+        copies.make(xnorm1_ref.at[:, columns(z, 1 - p.y)], xnorm_in.at[z], yn) for z in range(DEPTH)
+    ]
+    cuts = [(0, units // 2), (units // 2, packed_width)]
+    packed_to = [copies.make(packed.at[:, a:b], packed_in.at[:, a:b], yn) for a, b in cuts]
+    weight_to = [
+        copies.along(
+            [
+                (order[k], weight_out.at[k, :, a:b], weight_in.at[p.z, :, a:b])
+                for k in range(DEPTH - 1)
+            ],
+            along,
+            p.z,
+        )
+        for a, b in cuts
+    ]
+    output_to = copies.make(output_out, output_in, yn)
+    other = (1 - p.x) * 2 + p.c
+    back_to_c = [
+        copies.make(block(back_part, (1 - p.x) * 2 + 1 - p.c), back_in.at[0], cn),
+        copies.make(block(back_part, p.x * 2 + 1 - p.c), back_in.at[1], cn),
+    ]
+    back_to_x = copies.make(block(back_part, other), back_in.at[2], xn)
+    tokens_spread = Spread(p, copies, lambda t: block(tokens_grad_ref, t))
+    mixed_spread = Spread(p, copies, lambda t: block(mixed_ref, t))
+    small_to_c = copies.make(small, small_in.at[0], cn)
+    small_to_x = copies.make(small, small_in.at[1], xn)
+    small_to_y = copies.make(small_side.at[0], small_side.at[1], yn)
+    small_to = copies.along(
+        [(z, small_side.at[2, z], small_line.at[p.z]) for z in order[: DEPTH - 1]], along, p.z
+    )
+
+    block(hidden_all, p.t)[...] = hidden_low_ref[...]
+    hidden_line[p.t, p.z] = hidden_low_ref[
+        :, pl.ds(pl.multiple_of(p.z * 2 * share, share), 2 * share)
+    ]
+    for there, _ in hidden_to:
+        there.start()
+    hidden_spread.start()
+    for copy in xnorm_to:
+        copy.start()
+    small[...] = small_ref[...]
+    key_sum[...] = jnp.zeros_like(key_sum)
+    value_sum[...] = jnp.zeros_like(value_sum)
+    fetch[0].wait()
+    scattering[0]()
+    hidden_spread.forward()
+    scattering[1]()
+    hidden_spread.finish()
+
+    valid = lax.broadcasted_iota(jnp.int32, (group, 1), 0) < length
+    allowed = allowed_keys(group, length)
+    heads_grad[...] = jnp.where(
+        valid, dot(hidden_all[...], output_weight_ref[...], 1, 0), 0.0
+    ).astype(LOW)
+    cosine, sine = cosine_ref[...], sine_ref[...]
+    query_gain, key_gain = query_gain_ref[...], key_gain_ref[...]
+    factor = size ** (-0.5)
+    key_hat, key_scale = normed_rows(key_ref[...])
+    key_gained = key_hat * key_gain
+    key_low = (key_gained * cosine + turned(key_gained) * sine).astype(LOW)
+    gain_row = 2 * DEPTH * 2 + 2
+
+    def norm_back(grad, hat, scale, gain):
+        grad = grad * cosine - turned(grad) * sine
+        gain_part = jnp.sum(grad * hat, axis=0, keepdims=True)
+        inner = grad * gain
+        return scale * (inner - hat * jnp.mean(inner * hat, axis=-1, keepdims=True)), gain_part
+
+    def one_head(h):
+        at = pl.ds(pl.multiple_of(h * size, size), size)
+        hat, scale = normed_rows(query_ref[:, at])
+        gained = hat * query_gain
+        query_low = (gained * cosine + turned(gained) * sine).astype(LOW)
+        probs = attention_probs(query_low, key_low, allowed)
+        grad = heads_grad[:, at]
+        probs_grad = dot(grad, value_ref[...], 1, 1)
+        delta = jnp.sum(probs * probs_grad, axis=-1, keepdims=True)
+        score_grad = (probs * (probs_grad - delta)).astype(LOW)
+        key_sum[...] += dot(score_grad, query_low, 0, 0)
+        value_sum[...] += dot(probs.astype(LOW), grad, 0, 0)
+        back, gain_part = norm_back(
+            dot(score_grad, key_low, 1, 0) * factor, hat, scale, query_gain
+        )
+        packed[:, at] = back.astype(LOW)
+        small[gain_row : gain_row + 1, :size] += gain_part
+
+    pl.loop(0, count // 2)(one_head)
+    packed_to[0].start()
+    scattering[2]()
+    for _, back in hidden_to:
+        back.wait_recv()
+    line_spread.start()
+    pl.loop(count // 2, count)(one_head)
+    key_back, key_part = norm_back(key_sum[...] * factor, key_hat, key_scale, key_gain)
+    packed[:, units : units + size] = key_back.astype(LOW)
+    packed[:, units + size :] = value_sum[...].astype(LOW)
+    packed_to[1].start()
+    small[gain_row + 1 : gain_row + 2, :size] = key_part
+    for row in (gain_row, gain_row + 1):
+        part = small[row : row + 1, :size]
+        for i in range(1, width // size):
+            small[row : row + 1, i * size : (i + 1) * size] = part
+    line_spread.forward()
+    scattering[3]()
+    back_part[...] = (
+        dot(packed[:, :units], query_weight_ref[...], 1, 1)
+        + dot(packed[:, units : units + size], key_weight_ref[...], 1, 1)
+        + dot(packed[:, units + size :], value_weight_ref[...], 1, 1)
+    ).astype(LOW)
+    for copy in back_to_c:
+        copy.start()
+    for copy in xnorm_to:
+        copy.wait_recv()
+
+    def weight_piece(i):
+        a, b = cuts[i]
+        packed_to[i].wait_recv()
+        for k, z in enumerate(order):
+            grad = dot(xnorm1_ref[:, columns(z, p.y)], packed[:, a:b], 0, 0) + dot(
+                xnorm_in[z], packed_in[:, a:b], 0, 0
+            )
+            if k < DEPTH - 1:
+                weight_out[k, :, a:b] = grad.astype(LOW)
+                weight_to[i][k][0].start()
+            else:
+                packed_grad_ref[:, a:b] = grad
+
+    weight_piece(0)
+    back_to_c[0].wait_recv()
+    there = block(back_part, other)
+    there[...] = (there[...].astype(F32) + back_in[0].astype(F32)).astype(LOW)
+    back_to_x.start()
+    scattering[4]()
+    weight_piece(1)
+    scattering[5]()
+
+    back_to_c[1].wait_recv()
+    back_to_x.wait_recv()
+    xnorm1_grad = (
+        block(back_part, p.t)[...].astype(F32) + back_in[1].astype(F32) + back_in[2].astype(F32)
+    )
+    normed1, scale1 = normed_rows(tokens_ref[...].astype(F32))
+    small[gain_row - 1 : gain_row, :] = jnp.sum(xnorm1_grad * normed1, axis=0, keepdims=True)
+    small_to_c.start()
+    inner = xnorm1_grad * attention_gain_ref[...]
+    block(tokens_grad_ref, p.t)[...] = (
+        hidden_grad_ref[...]
+        + scale1 * (inner - normed1 * jnp.mean(inner * normed1, axis=-1, keepdims=True))
+    ).astype(LOW)
+    tokens_spread.start()
+
+    line_spread.finish()
+    for copy in fetch[1:]:
+        copy.wait()
+
+    def output_piece(y):
+        at = pl.ds(pl.multiple_of(y * share, share), share)
+        grad = dot(hidden_line[:, p.z, :, at].reshape(group, share), heads_ref[...], 0, 0)
+        for k in range(1, DEPTH):
+            z = p.near(k)
+            grad += dot(hidden_line[:, z, :, at].reshape(group, share), line_heads[z], 0, 0)
+        return grad
+
+    output_out[...] = output_piece(1 - p.y).astype(LOW)
+    output_to.start()
+    output_grad_ref[...] = output_piece(p.y)
+    scattering[6]()
+    small_to_c.wait_recv()
+    small_to_c.wait_send()
+    small[...] += small_in[0]
+    small_to_x.start()
+    tokens_spread.forward()
+    scattering[7]()
+    block(mixed_ref, p.t)[...] = (hidden_ref[...] + moe_own[...]).astype(LOW)
+    mixed_spread.start()
+    small_to_x.wait_recv()
+    small_to_x.wait_send()
+    small[...] += small_in[1]
+    for z in range(DEPTH):
+        small_side[0, z] = small[:, columns(z, 1 - p.y)]
+        small_side[2, z] = small[:, columns(z, p.y)]
+    small_to_y.start()
+    output_to.wait_recv()
+    output_grad_ref[...] += output_in[...].astype(F32)
+    small_to_y.wait_recv()
+    small_side[2] += small_side[1]
+    for there, _ in small_to:
+        there.start()
+    mixed_spread.forward()
+    tokens_spread.finish()
+    small_total = small_side[2, p.z]
+    for (_, back), z in zip(small_to, order):
+        back.wait_recv()
+        small_total += small_line[z]
+    small_out_ref[...] = small_total
+    mixed_spread.finish()
+    for i, (a, b) in enumerate(cuts):
+        grad = packed_grad_ref[:, a:b]
+        for (_, back), z in zip(weight_to[i], order):
+            back.wait_recv()
+            grad += weight_in[z, :, a:b].astype(F32)
+        packed_grad_ref[:, a:b] = grad
+    for copy in copies.made:
+        if copy is not small_to_c and copy is not small_to_x:
+            copy.wait_send()
+    scatter_copies.finish()
+
+
+def run_tail(
+    length,
+    hidden_low,
+    hidden_grad,
+    hidden,
+    tokens,
+    xnorm1,
+    small,
+    moe,
+    heads,
+    line_heads,
+    query,
+    key,
+    value,
+    cosine,
+    sine,
+    attention_gain,
+    query_gain,
+    key_gain,
+    query_weight,
+    key_weight,
+    value_weight,
+    output_weight,
+    collective_id,
+):
+    group, width = xnorm1.shape
+    rows = hidden_low.shape[0]
+    units, size = query.shape[1], cosine.shape[1]
+    packed_width = units + 2 * size
+    share = width // (2 * DEPTH)
+    tensors = group // rows
+    vmem = pltpu.VMEM
+    return pl.pallas_call(
+        functools.partial(tail_kernel, rows),
+        out_shape=(
+            jax.ShapeDtypeStruct((group, width), LOW),
+            jax.ShapeDtypeStruct((group, width), LOW),
+            jax.ShapeDtypeStruct((share, units), F32),
+            jax.ShapeDtypeStruct((share, packed_width), F32),
+            jax.ShapeDtypeStruct((small.shape[0], share), F32),
+        ),
+        in_specs=[pl.BlockSpec(memory_space=pltpu.SMEM)]
+        + [VMEM_SPEC] * 6
+        + [ANY_SPEC, VMEM_SPEC, ANY_SPEC]
+        + [VMEM_SPEC] * 12,
+        out_specs=[VMEM_SPEC] * 5,
+        scratch_shapes=[
+            vmem((group, width), LOW),
+            vmem((tensors, DEPTH, rows, 2 * share), LOW),
+            vmem((DEPTH, group, units), LOW),
+            vmem((group, units), LOW),
+            vmem((group, packed_width), LOW),
+            vmem((group, packed_width), LOW),
+            vmem((DEPTH, group, share), LOW),
+            vmem((DEPTH - 1, share, packed_width), LOW),
+            vmem((DEPTH, share, packed_width), LOW),
+            vmem((share, units), LOW),
+            vmem((share, units), LOW),
+            vmem((group, size), F32),
+            vmem((group, size), F32),
+            vmem((group, width), LOW),
+            vmem((3, rows, width), LOW),
+            vmem(moe.shape, LOW),
+            vmem((rows, width), F32),
+            vmem(small.shape, F32),
+            vmem((2, *small.shape), F32),
+            vmem((3, DEPTH, small.shape[0], share), F32),
+            vmem((DEPTH, small.shape[0], share), F32),
+        ]
+        + scatter_scratch(rows, width)
+        + semaphores(DEPTH, TAIL_SEMS, TAIL_SEMS, SCATTER_SEMS, SCATTER_SEMS),
+        compiler_params=pltpu.CompilerParams(
+            collective_id=collective_id, has_side_effects=True, vmem_limit_bytes=64000000
+        ),
+        name="tail",
+    )(
+        length,
+        hidden_low,
+        hidden_grad,
+        hidden,
+        tokens,
+        xnorm1,
+        small,
+        moe,
+        heads,
+        line_heads,
+        query,
+        key,
+        value,
+        cosine,
+        sine,
+        attention_gain,
+        query_gain,
+        key_gain,
+        query_weight,
+        key_weight,
+        value_weight,
+        output_weight,
+    )
 
 
 def gathered_shards(
@@ -990,32 +1459,25 @@
     scale1 = rms_scale(inputs)
     normed1 = inputs * scale1
     xnorm1 = (normed1 * attention_gain).astype(low)
-    xnorm1_columns = lax.all_to_all(xnorm1, "expert", split_axis=1, concat_axis=0, tiled=True)
-    query_raw = jnp.dot(xnorm1, query_weight, preferred_element_type=jnp.float32).reshape(
-        count, local_heads, head_size
-    )
-    key_raw = jnp.dot(xnorm1, key_weight, preferred_element_type=jnp.float32).reshape(
-        count, local_groups, head_size
-    )
-    value_low = (
-        jnp.dot(xnorm1, value_weight, preferred_element_type=jnp.float32)
-        .astype(low)
-        .reshape(count, local_groups, head_size)
-    )
+    query_flat = jnp.dot(xnorm1, query_weight, preferred_element_type=jnp.float32)
+    key_flat = jnp.dot(xnorm1, key_weight, preferred_element_type=jnp.float32)
+    value_flat = jnp.dot(xnorm1, value_weight, preferred_element_type=jnp.float32).astype(low)
+    query_raw = query_flat.reshape(count, local_heads, head_size)
+    key_raw = key_flat.reshape(count, local_groups, head_size)
+    value_low = value_flat.reshape(count, local_groups, head_size)
     query_gained, query_normed, query_scale = head_norm(query_raw, query_gain)
     key_gained, key_normed, key_scale = head_norm(key_raw, key_gain)
     cosine, sine = rope_tables(count, head_size)
     query_low = rotate(query_gained, cosine, sine).astype(low)
     key_low = rotate(key_gained, cosine, sine).astype(low)
     query_block = query_low.reshape(count, local_groups, ratio, head_size)
-    outputs, lse = attend_block(query_block, 0, key_low, value_low, length)
+    outputs, _ = attend_block(query_block, 0, key_low, value_low, length)
     valid = (jnp.arange(count, dtype=jnp.int32) < length)[:, None]
     heads_low = jnp.where(valid, outputs.reshape(count, local_heads * head_size), 0.0).astype(low)
     attention_part = contract(heads_low, output_weight, 1, 1)
     attention = lax.psum_scatter(
         attention_part.astype(low), "tensor", scatter_dimension=0, tiled=True
     ).astype(jnp.float32)
-    heads_all = lax.all_gather(heads_low, "expert", axis=0, tiled=True)
 
     hidden = own_rows(inputs) + attention
     scale2 = rms_scale(hidden)
@@ -1038,15 +1500,21 @@
     spare = jnp.zeros((rows, 128 - 2 * experts), low)
     own = jnp.concatenate([xnorm2, high, rest, spare], axis=1)
     gate_up = jnp.concatenate([*gate_weight, *up_weight], axis=1)
-    summed, moe_part, columns, gate_up_grad, down_grad = run_experts(
-        own, upstream_all, gate_up, down_weight.reshape(-1, width), owned, experts, width, 1
+    summed, moe_part, line_heads, gate_up_grad, down_grad = run_experts(
+        own,
+        upstream_all,
+        gate_up,
+        down_weight.reshape(-1, width),
+        heads_low,
+        owned,
+        experts,
+        width,
+        1,
     )
     units = gate_up.shape[1] // (2 * owned)
     split = [gate_up_grad[:, j * units : (j + 1) * units] for j in range(2 * owned)]
     gate_grad, up_grad = jnp.stack(split[:owned]), jnp.stack(split[owned:])
     down_grad = down_grad.reshape(down_weight.shape)
-    moe = scatter_rows(moe_part, 2)
-    mixed = lax.all_gather((hidden + moe).astype(low), "tensor", axis=0, tiled=True)
     xnorm2_moe, route_grad = summed[:, :width], summed[:, width : width + experts]
 
     upstream = own_rows(cotangent).astype(jnp.float32)
@@ -1055,83 +1523,66 @@
     logit_low = (router * (prob_grad - jnp.sum(router * prob_grad, axis=1, keepdims=True))).astype(
         low
     )
-    logit_all = lax.all_gather(logit_low, everywhere, axis=0, tiled=True)
-    router_grad = contract(columns, logit_all, 0, 0)
+    router_part = contract(logit_low, xnorm2, 0, 0)
     xnorm2_grad = xnorm2_moe + contract(logit_low, router_weight, 1, 1)
     routing_gain_part = jnp.sum(xnorm2_grad * normed2, axis=0)
     inner2 = xnorm2_grad * routing_gain
     hidden_grad = upstream + scale2 * (
         inner2 - normed2 * jnp.mean(inner2 * normed2, axis=1, keepdims=True)
     )
-    hidden_low = lax.all_gather(hidden_grad.astype(low), "tensor", axis=0, tiled=True)
-    hidden_columns = lax.all_to_all(hidden_low, "expert", split_axis=1, concat_axis=0, tiled=True)
-    output_grad = contract(hidden_columns, heads_all, 0, 0)
-    heads_grad = jnp.where(
-        valid,
-        jnp.dot(hidden_low, output_weight, preferred_element_type=jnp.float32).astype(low),
-        jnp.zeros((), low),
-    ).reshape(count, local_groups, ratio, head_size)
-    query_rot_grad, key_rot_grad, value_grad = attend_back(
-        query_block, heads_grad, lse, 0, key_low, value_low, length
-    )
-    query_back, query_gain_part = head_norm_back(
-        rotate_back(query_rot_grad.reshape(count, local_heads, head_size), cosine, sine),
-        query_normed,
-        query_scale,
-        query_gain,
-    )
-    key_back, key_gain_part = head_norm_back(
-        rotate_back(key_rot_grad, cosine, sine), key_normed, key_scale, key_gain
-    )
-    query_grad_low = query_back.reshape(count, local_heads * head_size).astype(low)
-    key_grad_low = key_back.reshape(count, local_groups * head_size).astype(low)
-    value_grad_low = value_grad.reshape(count, local_groups * head_size).astype(low)
-    packed = jnp.concatenate([query_grad_low, key_grad_low, value_grad_low], axis=1)
-    packed_all = lax.all_gather(packed, "expert", axis=0, tiled=True)
-    packed_grad = contract(xnorm1_columns, packed_all, 0, 0)
+    small = jnp.concatenate(
+        [router_part, routing_gain_part[None], jnp.zeros((7, width), jnp.float32)], axis=0
+    )
+    half = head_size // 2
+    mixed, tokens_grad, output_grad, packed_grad, small_sum = run_tail(
+        seq_length,
+        hidden_grad.astype(low),
+        hidden_grad,
+        hidden,
+        own_rows(tokens),
+        xnorm1,
+        small,
+        moe_part,
+        heads_low,
+        line_heads,
+        query_flat,
+        key_flat,
+        value_flat,
+        cosine,
+        jnp.concatenate([-sine[:, :half], sine[:, half:]], axis=1),
+        attention_gain[None],
+        query_gain[None],
+        key_gain[None],
+        query_weight,
+        key_weight,
+        value_weight,
+        output_weight,
+        2,
+    )
     query_end = local_heads * head_size
     key_end = query_end + local_groups * head_size
-    xnorm1_part = contract(query_grad_low, query_weight, 1, 1) + contract(
-        key_grad_low, key_weight, 1, 1
-    )
-    xnorm1_part = xnorm1_part + contract(value_grad_low, value_weight, 1, 1)
-    xnorm1_grad = lax.psum_scatter(
-        xnorm1_part.astype(low), "tensor", scatter_dimension=0, tiled=True
-    ).astype(jnp.float32)
-    normed1_own = own_rows(normed1)
-    attention_gain_part = jnp.sum(xnorm1_grad * normed1_own, axis=0)
-    inner1 = xnorm1_grad * attention_gain
-    tokens_grad = (
-        hidden_grad
-        + own_rows(scale1)
-        * (inner1 - normed1_own * jnp.mean(inner1 * normed1_own, axis=1, keepdims=True))
-    ).astype(low)
-    tokens_grad = lax.all_gather(tokens_grad, "tensor", axis=0, tiled=True)
-    gains = lax.psum(
-        jnp.concatenate([attention_gain_part, routing_gain_part, query_gain_part, key_gain_part]),
-        everywhere,
-    )
-
-    def own_share(start, size):
-        share = size // lax.axis_size("expert")
-        return lax.dynamic_slice_in_dim(gains, start + owner * share, share, 0)
+    share = head_size // lax.axis_size("expert")
+
+    def own_gain(row):
+        return lax.dynamic_slice_in_dim(small_sum[row], owner * share, share, 0)
 
     return (
         mixed,
         tokens_grad,
-        own_share(0, width),
+        small_sum[experts + 1],
         packed_grad[:, :query_end],
         packed_grad[:, query_end:key_end],
         packed_grad[:, key_end:],
-        own_share(2 * width, head_size),
-        own_share(2 * width + head_size, head_size),
+        own_gain(experts + 2),
+        own_gain(experts + 3),
         output_grad,
-        own_share(width, width),
-        router_grad,
+        small_sum[experts],
+        small_sum[:experts].T,
         gate_grad,
         up_grad,
         down_grad,
     )
+
 
 def solution(mesh):
     sizes = dict(mesh.shape)

time: 588 us -> 435 us (0.74)
  Pallas kernels: 219 us -> 334 us
  blocking collectives: 105 us -> 0 us
  waiting for transfers between devices: 88.7 us -> 0.02 us
  local copies, waits for them, and re-layouts: 66.9 us -> 42.4 us
  matrix products: 32.9 us -> 14.7 us
  other arithmetic: 41.2 us -> 25.7 us
  starting transfers between devices: 10.9 us -> 0.04 us
    pallas_call x1, Pallas kernels: 47.6 us -> 140 us  [run_tail(): pl.pallas_call(functools.partial(tail_kernel, rows), out_shape=(jax.Shape...]
    all_gather x5 -> x0, waiting for transfers between devices: 87.6 us -> none  [the longest x1 69.6 us: gathered_shards(): packed_all = lax.all_gather(packed, 'expert', axis=0, tiled=True)]
    psum x1 -> x0, blocking collectives: 53.4 us -> none  [gathered_shards(): lax.psum(jnp.concatenate([attention_gain_part, routing_gain_part, query_g...]
    all_gather x1 -> x0, blocking collectives: 51.3 us -> none  [gathered_shards(): logit_all = lax.all_gather(logit_low, everywhere, axis=0, tiled=True)]
    pallas_call x1, Pallas kernels: 118 us -> 141 us  [run_experts(): pl.pallas_call(functools.partial(experts_kernel, rows, width, experts, ow...]
    dot_general x8 -> x3, matrix products: 22.1 us -> 7.25 us  [contract(): lax.dot_general(left, right, (((left_dim,), (right_dim,)), ((), ())), pre...]
    all_to_all x2 -> x0, starting transfers between devices: 10.3 us -> none  [the longest x1 6.71 us: gathered_shards(): lax.all_to_all(hidden_low, 'expert', split_axis=1, concat_axis=0, tiled=T...]
    unnamed x133 -> x65, local copies, waits for them, and re-layouts: 31.8 us -> 21.6 us
  transfers between devices with their start and end apart: 9 -> 1, of which waited for: 2 -> 0; matrix products, arithmetic and copies ran while one was open for 9% -> 4% of each run, Pallas kernels for 17% -> 12%
where the time goes in v2:
time: 435 us; the launch traced here: 433 us
  Pallas kernels  334 us (77%)
  local copies, waits for them, and re-layouts  42.4 us (10%)
  other arithmetic  25.7 us (6%)
  between operations  15.5 us (4%)
  matrix products  14.7 us (3%)
    pallas_call x1, Pallas kernels, run_experts(): pl.pallas_call(functools.partial(experts_kernel, rows, width, experts, ow...  141 us
    pallas_call x1, Pallas kernels, run_tail(): pl.pallas_call(functools.partial(tail_kernel, rows), out_shape=(jax.Shape...  140 us
    pallas_call x1, Pallas kernels, gather_rows(): pl.pallas_call(functools.partial(gather_kernel, rows), out_shape=jax.Shap...  53.2 us
    unnamed x65, local copies, waits for them, and re-layouts  21.6 us
  transfers between devices with their start and end apart: 1, of which 0 were waited for; matrix products, arithmetic and copies ran while one was open for 4% of the time, Pallas kernels for 12%

profile of v2, /device:TPU:0, one launch (start us, length us, event | category | flops | bytes accessed | tf_op | source)
XLA Modules:
  0.0 432.8 jit_solution(9486747413840841148)
XLA Ops:
  7.3 1.5 multiply_reduce_fusion
  8.8 1.6 multiply_convert_fusion.xnorm1_ref
  10.3 3.8 fusion.37.query_ref
  15.3 1.3 slice_negate_fusion
  16.7 1.2 fusion.21
  19.8 1.5 convolution_convert_fusion.1.value_ref
  23.4 1.0 fusion.35
  25.7 4.7 %convolution_convert_fusion = bf16[256,2048]{1,0:T(8,128)(2,1)} fusion(bf16[256,1024]{1,0:T(8,128)(2,1)S(1)} %select_convert_fusion.heads_ref, bf16[2048,1024]{1,0:T(8,128)(2,1)} %output_weight_ref.1), kind=kOutput, calls=%fused_computation.3 | convolution fusion | flops 1074266112 | bytes 5767168 | tf_op jit(solution)/shard_map/dot_general | solution.py:55
  30.4 1.6 convert_element_type.55
  32.1 1.8 constant_dynamic-slice_fusion.2
  33.9 53.2 %gather_rows.1.upstream_ref = bf16[2048,2048]{1,0:T(8,128)(2,1)} custom-call(bf16[64,2048]{1,0:T(8,128)(2,1)} %get-tuple-element.130.own_ref), custom_call_target="tpu_custom_call" | custom-call | tf_op jit(solution)/shard_map/gather_rows/pallas_call | solution.py:735
  87.2 1.5 fusion.31
  89.9 2.7 fusion.32
  92.5 1.4 copy.92
  94.0 2.2 copy.93
  96.3 4.2 pad_maximum_fusion.2.gate_up_ref
  100.5 1.3 multiply_reduce_fusion.4
  103.6 141.4 %experts.1 = (f32[64,2176]{1,0:T(8,128)}, bf16[2048,2048]{1,0:T(8,128)(2,1)}, bf16[4,256,1024]{2,1,0:T(8,128)(2,1)}, f32[2048,768]{1,0:T(8,128)}, f32[384,2048]{1,0:T(8,128)}) custom-call(bf16[64,2176]{1,0:T(8,128)(2,1)} %concatenate.37.own_ref, bf16[2048,2048]{1,0:T(8,128)(2,1)} %gather_rows.1.upstream_ref, ...), custom_call_target="tpu_custom_call" | custom-call | tf_op jit(solution)/shard_map/experts/pallas_call | solution.py:929
  245.0 1.0 multiply_reduce_fusion.7
  246.0 1.0 multiply_reduce_fusion.6
  247.0 1.1 fusion.29
  248.1 1.5 multiply_reduce_fusion.2
  249.6 1.1 fusion.30
  251.5 139.8 %tail.1 = (bf16[256,2048]{1,0:T(8,128)(2,1)}, bf16[256,2048]{1,0:T(8,128)(2,1)}, f32[256,1024]{1,0:T(8,128)}, f32[256,1280]{1,0:T(8,128)}, f32[24,256]{1,0:T(8,128)}) custom-call(s32[1]{0:T(128)} %copy.130.length_ref, bf16[64,2048]{1,0:T(8,128)(2,1)} %get-tuple-element.92.hidden_low_ref, f32[64,2048]{1,0:T(8,128)} %get-tuple-element.93.hidden_grad_ref, ...), custom_call_target="tpu_custom_call" | custom-call | tf_op jit(solution)/shard_map/tail/pallas_call | solution.py:1352
  391.2 2.3 slice.61
  393.6 1.7 fusion.33
  396.4 6.5 %slice_bitcast_fusion.1 = (f32[1,2048,192]{2,1,0:T(8,128)S(1)}, f32[1,2048,192]{2,1,0:T(8,128)S(1)}, f32[1,2048,192]{2,1,0:T(8,128)S(1)}, f32[1,2048,192]{2,1,0:T(8,128)}) fusion(f32[2048,768]{1,0:T(8,128)} %get-tuple-element.32), kind=kLoop, calls=%fused_computation.7 | loop fusion | bytes 12582912 | tf_op jit(solution)/shard_map/stack | solution.py:1516
  402.9 2.2 pad_maximum_fusion.1
  405.1 5.2 %copy.87 = f32[2,2048,192]{1,2,0:T(8,128)} copy(f32[2,2048,192]{2,1,0:T(8,128)} %pad_maximum_fusion.1) | data formatting | bytes 6291456
  410.3 3.8 pad_maximum_fusion
  414.1 5.3 %copy.86 = f32[2,2048,192]{1,2,0:T(8,128)} copy(f32[2,2048,192]{2,1,0:T(8,128)} %pad_maximum_fusion) | data formatting | bytes 6291456
  424.3 1.7 copy.134
  (106 shorter events, 15.4 us)
Async XLA Ops:
  7.2 94.8 %copy-start = (bf16[2048,16]{0,1:T(8,128)(2,1)S(1)}, bf16[2048,16]{0,1:T(8,128)(2,1)}, u32[]{:S(2)}) copy-start(bf16[2048,16]{0,1:T(8,128)(2,1)} %param.27) | copy-start | bytes 196612
  7.2 93.3 %reduce-scatter.2.cloned.1.call-start = ((), (), s32[]{:S(2)}) async-start(), calls=%async_computation.1 | async-start | bytes 1310720 | tf_op jit(solution)/shard_map/reduce_scatter | solution.py:1478
  10.3 9.5 %copy-start.2 = (bf16[256,2048]{1,0:T(8,128)(2,1)}, bf16[256,2048]{1,0:T(8,128)(2,1)S(1)}, u32[]{:S(2)}) copy-start(bf16[256,2048]{1,0:T(8,128)(2,1)S(1)} %multiply_convert_fusion.xnorm1_ref) | copy-start | bytes 3145732
  14.2 9.2 %copy-start.4 = (f32[256,1024]{1,0:T(8,128)}, f32[256,1024]{1,0:T(8,128)S(1)}, u32[]{:S(2)}) copy-start(f32[256,1024]{1,0:T(8,128)S(1)} %fusion.37.query_ref) | copy-start | bytes 3145732
  14.2 0.8 copy-start.25
  15.0 1.7 copy-start.13
  15.3 2.6 copy-start.11
  16.6 1.9 copy-start.24
  18.5 4.9 %copy-start.10 = (f32[256,128]{1,0:T(8,128)}, f32[256,128]{1,0:T(8,128)S(1)}, u32[]{:S(2)}) copy-start(f32[256,128]{1,0:T(8,128)S(1)} %copy.72.key_ref) | copy-start | bytes 393220
  18.5 2.8 copy-start.15
  18.5 2.8 copy-start.16
  18.5 2.8 copy-start.20
  18.5 3.6 copy-start.7
  21.3 3.4 copy-start.21
  22.1 0.7 copy-start.12
  22.1 1.0 copy-start.14
  25.7 4.7 %copy-start.6 = (bf16[256,1024]{1,0:T(8,128)(2,1)}, bf16[256,1024]{1,0:T(8,128)(2,1)S(1)}, u32[]{:S(2)}) copy-start(bf16[256,1024]{1,0:T(8,128)(2,1)S(1)} %select_convert_fusion.heads_ref) | copy-start | bytes 1572868
  25.7 4.7 %copy-start.3 = (bf16[256,2048]{1,0:T(8,128)(2,1)S(1)}, bf16[256,2048]{1,0:T(8,128)(2,1)}, u32[]{:S(2)}) copy-start(bf16[256,2048]{1,0:T(8,128)(2,1)} %param.16) | copy-start | bytes 3145732
  30.3 1.6 copy-start.26
  96.3 5.6 %copy-start.22 = (f32[2048]{0:T(1024)S(1)}, f32[2048]{0:T(1024)}, u32[]{:S(2)}) copy-start(f32[2048]{0:T(1024)} %param.26) | copy-start | bytes 24580
  101.8 147.8 %copy-start.5 = (f32[64,2048]{1,0:T(8,128)}, f32[64,2048]{1,0:T(8,128)S(1)}, u32[]{:S(2)}) copy-start(f32[64,2048]{1,0:T(8,128)S(1)} %get-tuple-element.95.hidden_ref) | copy-start | bytes 1572868
  245.0 4.6 %copy-start.9 = (bf16[64,2048]{1,0:T(8,128)(2,1)S(1)}, bf16[64,2048]{1,0:T(8,128)(2,1)}, u32[]{:S(2)}) copy-start(bf16[64,2048]{1,0:T(8,128)(2,1)} %get-tuple-element.130.own_ref) | copy-start | bytes 786436
  391.2 4.0 copy-start.23
  414.1 6.5 %copy-start.19 = (bf16[256,2048]{1,0:T(8,128)(2,1)S(1)}, bf16[256,2048]{1,0:T(8,128)(2,1)}, u32[]{:S(2)}) copy-start(bf16[256,2048]{1,0:T(8,128)(2,1)} %get-tuple-element.145) | copy-start | bytes 3145732
  419.4 2.1 copy-start.18
  420.6 1.9 copy-start.17
  421.5 2.7 copy-start.8
  422.5 3.4 copy-start.1
Sparse Core Ops, SparseCore 0:
  30.5 31.4 reduce-scatter.1

commit v3 on v2

--- a/solution.py
+++ b/solution.py
@@ -552,11 +552,13 @@
         for copy in group:
             copy.wait_recv()
 
-    def step0():
+    def begin():
         own_copy.start()
         for there, _ in line:
             there.start()
         onward(0)
+
+    def step0():
         onward(1)
         pair(0)
         own_copy.wait()
@@ -584,6 +586,7 @@
         arrived(near[3])
 
     return [
+        begin,
         step0,
         step1,
         lambda: arrived(near[1]),
@@ -718,61 +721,6 @@
 ANY_SPEC = pl.BlockSpec(memory_space=pl.ANY)
 
 
-def gather_kernel(rows, own_ref, all_ref, local_sem, send_sems, recv_sems):
-    p = Place()
-    enter(p.peers())
-    copies = Copies(send_sems, recv_sems)
-    whole, _, _ = pieces_of(all_ref, rows)
-    own_copy = pltpu.make_async_copy(own_ref, whole(p.block()), local_sem.at[0])
-    for step in gather_steps(p, copies, rows, own_ref, all_ref, own_copy):
-        step()
-    copies.finish()
-
-
-def gather_rows(own, collective_id):
-    rows, width = own.shape
-    devices = lax.axis_size("expert") * lax.axis_size("tensor")
-    return pl.pallas_call(
-        functools.partial(gather_kernel, rows),
-        out_shape=jax.ShapeDtypeStruct((devices * rows, width), own.dtype),
-        in_specs=[ANY_SPEC],
-        out_specs=ANY_SPEC,
-        scratch_shapes=semaphores(1, GATHER_SEMS, GATHER_SEMS),
-        compiler_params=pltpu.CompilerParams(collective_id=collective_id, has_side_effects=True),
-        name="gather_rows",
-    )(own)
-
-
-def scatter_kernel(
-    rows, part_ref, out_ref, part, core_in, diag_in, side_in, line_in, local_sem, ss, rs
-):
-    p = Place()
-    fetch = pltpu.make_async_copy(part_ref, part, local_sem.at[0])
-    fetch.start()
-    enter(p.peers())
-    fetch.wait()
-    copies = Copies(ss, rs)
-    for step in scatter_steps(p, copies, rows, part, core_in, diag_in, side_in, line_in, out_ref):
-        step()
-    copies.finish()
-
-
-def scatter_rows(part, collective_id):
-    total, width = part.shape
-    rows = total // (lax.axis_size("expert") * lax.axis_size("tensor"))
-    return pl.pallas_call(
-        functools.partial(scatter_kernel, rows),
-        out_shape=jax.ShapeDtypeStruct((rows, width), F32),
-        in_specs=[ANY_SPEC],
-        out_specs=VMEM_SPEC,
-        scratch_shapes=[pltpu.VMEM(part.shape, LOW)]
-        + scatter_scratch(rows, width)
-        + semaphores(1, SCATTER_SEMS, SCATTER_SEMS),
-        compiler_params=pltpu.CompilerParams(collective_id=collective_id, has_side_effects=True),
-        name="scatter_rows",
-    )(part)
-
-
 def experts_kernel(
     rows,
     width,
@@ -780,13 +728,15 @@
     owned,
     own_ref,
     upstream_ref,
-    gate_up_ref,
+    gate_ref,
+    up_ref,
     down_ref,
     heads_ref,
     grad_ref,
     moe_ref,
     line_heads_ref,
-    gate_up_grad_ref,
+    gate_grad_ref,
+    up_grad_ref,
     down_grad_ref,
     all_ref,
     upstream,
@@ -841,6 +791,7 @@
         )
 
     fetch(0).start()
+    gathering[0]()
     down_grad_ref[...] = jnp.zeros_like(down_grad_ref)
     first = p.e * owned
     lane = lax.broadcasted_iota(jnp.int32, (group, extra), 1)
@@ -848,11 +799,12 @@
 
     @pl.loop(0, count)
     def _(i):
-        for k, step in enumerate(gathering):
+        for k, step in enumerate(gathering[1:]):
             pl.when(i == k)(step)
         at = rows_of(i)
-        hid = dot(all_ref[at, :width], gate_up_ref[...], 1, 0)
-        gate, up = hid[:, :units], hid[:, units:]
+        x = all_ref[at, :width]
+        gate = dot(x, gate_ref[...], 1, 1)
+        up = dot(x, up_ref[...], 1, 1)
         tail = all_ref[at, width:].astype(F32)
         weights = [
             jnp.sum(
@@ -897,7 +849,7 @@
         back_rows[at, :units] = gate_back
         back_rows[at, units:] = up_back
         part[at, :width] = (
-            dot(gate_back, gate_up_ref[:, :units], 1, 1) + dot(up_back, gate_up_ref[:, units:], 1, 1)
+            dot(gate_back, gate_ref[...], 1, 0) + dot(up_back, up_ref[...], 1, 0)
         ).astype(LOW)
         part[at, width:] = note.astype(LOW)
 
@@ -910,7 +862,9 @@
         for k, step in enumerate(scattering):
             pl.when(i == k)(step)
         at = pl.ds(pl.multiple_of(i * tile, tile), tile)
-        gate_up_grad_ref[at, :] = dot(all_ref[:, at], back_rows[...], 0, 0)
+        x = all_ref[:, at]
+        gate_grad_ref[:, at] = dot(back_rows[:, :units], x, 0, 0)
+        up_grad_ref[:, at] = dot(back_rows[:, units:], x, 0, 0)
 
     gather_copies.finish()
     scatter_copies.finish()
@@ -921,7 +875,7 @@
     heads_copies.finish()
 
 
-def run_experts(own, upstream_all, gate_up, down, heads, owned, experts, width, collective_id):
+def run_experts(own, upstream_all, gate, up, down, heads, owned, experts, width, collective_id):
     rows, full = own.shape
     total = upstream_all.shape[0]
     units = down.shape[0]
@@ -932,11 +886,10 @@
             jax.ShapeDtypeStruct((rows, full), F32),
             jax.ShapeDtypeStruct((total, width), LOW),
             jax.ShapeDtypeStruct((DEPTH, *heads.shape), LOW),
-            jax.ShapeDtypeStruct((width, 2 * units), F32),
-            jax.ShapeDtypeStruct((units, width), F32),
+            *[jax.ShapeDtypeStruct((units, width), F32)] * 3,
         ),
-        in_specs=[VMEM_SPEC, ANY_SPEC, VMEM_SPEC, VMEM_SPEC, ANY_SPEC],
-        out_specs=(VMEM_SPEC, ANY_SPEC, ANY_SPEC, VMEM_SPEC, VMEM_SPEC),
+        in_specs=[VMEM_SPEC, ANY_SPEC, VMEM_SPEC, VMEM_SPEC, VMEM_SPEC, ANY_SPEC],
+        out_specs=(VMEM_SPEC, ANY_SPEC, ANY_SPEC, VMEM_SPEC, VMEM_SPEC, VMEM_SPEC),
         scratch_shapes=[
             pltpu.VMEM((total, full), LOW),
             pltpu.VMEM((2, group, width), LOW),
@@ -950,7 +903,7 @@
             collective_id=collective_id, has_side_effects=True, vmem_limit_bytes=64000000
         ),
         name="experts",
-    )(own, upstream_all, gate_up, down, heads)
+    )(own, upstream_all, gate, up, down, heads)
 
 
 def normed_rows(values):
@@ -995,19 +948,228 @@
         self.onward.wait_recv()
 
 
+class Fold:
+    def __init__(self, p, copies, rows, part, arrived):
+        def block(t):
+            return part.at[pl.ds(pl.multiple_of(t * rows, rows), rows)]
+
+        cn, xn = p.at(c=1 - p.c), p.at(x=1 - p.x)
+        self.arrived, self.own, self.other = arrived, block(p.t), block((1 - p.x) * 2 + p.c)
+        self.to_c = [
+            copies.make(block((1 - p.x) * 2 + 1 - p.c), arrived.at[0], cn),
+            copies.make(block(p.x * 2 + 1 - p.c), arrived.at[1], cn),
+        ]
+        self.to_x = copies.make(self.other, arrived.at[2], xn)
+
+    def start(self):
+        for copy in self.to_c:
+            copy.start()
+
+    def forward(self):
+        self.to_c[0].wait_recv()
+        self.other[...] = (self.other[...].astype(F32) + self.arrived[0].astype(F32)).astype(LOW)
+        self.to_x.start()
+
+    def finish(self):
+        self.to_c[1].wait_recv()
+        self.to_x.wait_recv()
+        return (
+            self.own[...].astype(F32) + self.arrived[1].astype(F32) + self.arrived[2].astype(F32)
+        )
+
+
+FOLD_SEMS = 3
+
+
+def front_kernel(
+    rows,
+    experts,
+    length_ref,
+    tokens_ref,
+    cotangent_ref,
+    routes_ref,
+    attention_gain_ref,
+    query_gain_ref,
+    key_gain_ref,
+    routing_gain_ref,
+    cosine_ref,
+    sine_ref,
+    query_weight_ref,
+    key_weight_ref,
+    value_weight_ref,
+    output_weight_ref,
+    router_weight_ref,
+    upstream_ref,
+    xnorm1_ref,
+    query_ref,
+    key_ref,
+    value_ref,
+    heads_ref,
+    hidden_ref,
+    own_ref,
+    router_ref,
+    part,
+    part_in,
+    local_sems,
+    gather_send,
+    gather_recv,
+    send_sems,
+    recv_sems,
+):
+    p = Place()
+    group, width = tokens_ref.shape
+    units = query_ref.shape[1]
+    size = cosine_ref.shape[1]
+    count = units // size
+    length = length_ref[0]
+    enter(p.peers())
+    copies = Copies(send_sems, recv_sems)
+    gather_copies = Copies(gather_send, gather_recv)
+    mine = pl.ds(pl.multiple_of(p.t * rows, rows), rows)
+    whole, _, _ = pieces_of(upstream_ref, rows)
+    own_cotangent = cotangent_ref.at[mine]
+    own_copy = pltpu.make_async_copy(own_cotangent, whole(p.block()), local_sems.at[0])
+    gathering = gather_steps(p, gather_copies, rows, own_cotangent, upstream_ref, own_copy)
+    fold = Fold(p, copies, rows, part, part_in)
+    gathering[0]()
+
+    normed1, _ = normed_rows(tokens_ref[...].astype(F32))
+    xnorm1_ref[...] = (normed1 * attention_gain_ref[...]).astype(LOW)
+    query_ref[...] = dot(xnorm1_ref[...], query_weight_ref[...], 1, 0)
+    key_ref[...] = dot(xnorm1_ref[...], key_weight_ref[...], 1, 0)
+    value_ref[...] = dot(xnorm1_ref[...], value_weight_ref[...], 1, 0).astype(LOW)
+    gathering[1]()
+    cosine, sine = cosine_ref[...], sine_ref[...]
+    query_gain = query_gain_ref[...]
+    valid = lax.broadcasted_iota(jnp.int32, (group, 1), 0) < length
+    allowed = allowed_keys(group, length)
+    key_hat, _ = normed_rows(key_ref[...])
+    key_gained = key_hat * key_gain_ref[...]
+    key_low = (key_gained * cosine + turned(key_gained) * sine).astype(LOW)
+
+    @pl.loop(0, count)
+    def _(h):
+        for k in (2, 3):
+            pl.when(h == 2 * k)(gathering[k])
+        at = pl.ds(pl.multiple_of(h * size, size), size)
+        hat, _ = normed_rows(query_ref[:, at])
+        gained = hat * query_gain
+        query_low = (gained * cosine + turned(gained) * sine).astype(LOW)
+        probs = attention_probs(query_low, key_low, allowed).astype(LOW)
+        heads_ref[:, at] = jnp.where(valid, dot(probs, value_ref[...], 1, 0), 0.0).astype(LOW)
+
+    part[...] = dot(heads_ref[...], output_weight_ref[...], 1, 1).astype(LOW)
+    fold.start()
+    gathering[4]()
+    fold.forward()
+    gathering[5]()
+    hidden = tokens_ref[mine, :].astype(F32) + fold.finish()
+    hidden_ref[...] = hidden
+    normed2, _ = normed_rows(hidden)
+    xnorm2 = (normed2 * routing_gain_ref[...]).astype(LOW)
+    own_ref[:, :width] = xnorm2
+    gathering[6]()
+    logits = dot(xnorm2, router_weight_ref[...], 1, 1)
+    lanes = logits.shape[1]
+    lane = lax.broadcasted_iota(jnp.int32, logits.shape, 1)
+    peak = jnp.max(jnp.where(lane < experts, logits, NEGATIVE), axis=1, keepdims=True)
+    expo = jnp.where(lane < experts, jnp.exp(jnp.minimum(logits - peak, 0.0)), 0.0)
+    router = expo / jnp.sum(expo, axis=1, keepdims=True)
+    named = jnp.zeros(logits.shape, F32)
+    for k in range(routes_ref.shape[1]):
+        named = jnp.where(routes_ref[:, k : k + 1] == lane, 1.0, named)
+    chosen = router * named
+    route_weight = chosen / jnp.sum(chosen, axis=1, keepdims=True)
+    high = route_weight.astype(LOW).astype(F32)
+    own_ref[:, width:] = (high + pltpu.roll(route_weight - high, experts, 1)).astype(LOW)
+    router_ref[:, :lanes] = router
+    router_ref[:, lanes : 2 * lanes] = route_weight
+    router_ref[:, 2 * lanes :] = named
+    for step in gathering[7:]:
+        step()
+    gather_copies.finish()
+    copies.finish()
+
+
+def run_front(
+    length,
+    tokens,
+    cotangent,
+    routes,
+    attention_gain,
+    query_gain,
+    key_gain,
+    routing_gain,
+    cosine,
+    sine,
+    query_weight,
+    key_weight,
+    value_weight,
+    output_weight,
+    router_weight,
+    experts,
+    collective_id,
+):
+    group, width = tokens.shape
+    rows = routes.shape[0]
+    lanes = router_weight.shape[0]
+    total = group * lax.axis_size("expert")
+    struct = jax.ShapeDtypeStruct
+    return pl.pallas_call(
+        functools.partial(front_kernel, rows, experts),
+        out_shape=(
+            struct((total, width), LOW),
+            struct((group, width), LOW),
+            struct((group, query_weight.shape[1]), F32),
+            struct((group, key_weight.shape[1]), F32),
+            struct((group, value_weight.shape[1]), LOW),
+            struct((group, query_weight.shape[1]), LOW),
+            struct((rows, width), F32),
+            struct((rows, width + lanes), LOW),
+            struct((rows, 3 * lanes), F32),
+        ),
+        in_specs=[pl.BlockSpec(memory_space=pltpu.SMEM), VMEM_SPEC, ANY_SPEC] + [VMEM_SPEC] * 12,
+        out_specs=[ANY_SPEC] + [VMEM_SPEC] * 8,
+        scratch_shapes=[pltpu.VMEM((group, width), LOW), pltpu.VMEM((3, rows, width), LOW)]
+        + semaphores(1, GATHER_SEMS, GATHER_SEMS, FOLD_SEMS, FOLD_SEMS),
+        compiler_params=pltpu.CompilerParams(
+            collective_id=collective_id, has_side_effects=True, vmem_limit_bytes=60000000
+        ),
+        name="front",
+    )(
+        length,
+        tokens,
+        cotangent,
+        routes,
+        attention_gain,
+        query_gain,
+        key_gain,
+        routing_gain,
+        cosine,
+        sine,
+        query_weight,
+        key_weight,
+        value_weight,
+        output_weight,
+        router_weight,
+    )
+
+
 SPREAD_SEMS = 3
 TAIL_SEMS = 4 * SPREAD_SEMS + DEPTH + DEPTH + 2 + 2 * DEPTH + 1 + 3 + 3 + DEPTH
 
 
 def tail_kernel(
     rows,
+    experts,
     length_ref,
-    hidden_low_ref,
-    hidden_grad_ref,
+    summed_ref,
+    own_ref,
+    router_ref,
     hidden_ref,
+    cotangent_ref,
     tokens_ref,
     xnorm1_ref,
-    small_ref,
     moe_ref,
     heads_ref,
     line_heads_ref,
@@ -1017,17 +1179,21 @@
     cosine_ref,
     sine_ref,
     attention_gain_ref,
+    routing_gain_ref,
     query_gain_ref,
     key_gain_ref,
     query_weight_ref,
     key_weight_ref,
     value_weight_ref,
     output_weight_ref,
+    router_weight_ref,
     mixed_ref,
     tokens_grad_ref,
     output_grad_ref,
     packed_grad_ref,
     small_out_ref,
+    hidden_grad_ref,
+    hidden_low_ref,
     hidden_all,
     hidden_line,
     line_heads,
@@ -1125,12 +1291,7 @@
         for a, b in cuts
     ]
     output_to = copies.make(output_out, output_in, yn)
-    other = (1 - p.x) * 2 + p.c
-    back_to_c = [
-        copies.make(block(back_part, (1 - p.x) * 2 + 1 - p.c), back_in.at[0], cn),
-        copies.make(block(back_part, p.x * 2 + 1 - p.c), back_in.at[1], cn),
-    ]
-    back_to_x = copies.make(block(back_part, other), back_in.at[2], xn)
+    fold = Fold(p, copies, rows, back_part, back_in)
     tokens_spread = Spread(p, copies, lambda t: block(tokens_grad_ref, t))
     mixed_spread = Spread(p, copies, lambda t: block(mixed_ref, t))
     small_to_c = copies.make(small, small_in.at[0], cn)
@@ -1140,6 +1301,28 @@
         [(z, small_side.at[2, z], small_line.at[p.z]) for z in order[: DEPTH - 1]], along, p.z
     )
 
+    lanes = router_weight_ref.shape[0]
+    gain_row = experts + 2
+    route_grad = summed_ref[:, width:]
+    router = router_ref[:, :lanes]
+    route_weight = router_ref[:, lanes : 2 * lanes]
+    named = router_ref[:, 2 * lanes :]
+    chosen_total = jnp.sum(router * named, axis=1, keepdims=True)
+    inner_total = jnp.sum(route_grad * route_weight, axis=1, keepdims=True)
+    prob_grad = named * (route_grad - inner_total) / chosen_total
+    logit_low = (router * (prob_grad - jnp.sum(router * prob_grad, axis=1, keepdims=True))).astype(
+        LOW
+    )
+    small[...] = jnp.zeros_like(small)
+    small[:experts, :] = dot(logit_low, own_ref[:, :width], 0, 0)[:experts]
+    xnorm2_grad = summed_ref[:, :width] + dot(logit_low, router_weight_ref[...], 1, 0)
+    normed2, scale2 = normed_rows(hidden_ref[...])
+    small[experts : experts + 1, :] = jnp.sum(xnorm2_grad * normed2, axis=0, keepdims=True)
+    inner2 = xnorm2_grad * routing_gain_ref[...]
+    hidden_grad_ref[...] = cotangent_ref[...].astype(F32) + scale2 * (
+        inner2 - normed2 * jnp.mean(inner2 * normed2, axis=-1, keepdims=True)
+    )
+    hidden_low_ref[...] = hidden_grad_ref[...].astype(LOW)
     block(hidden_all, p.t)[...] = hidden_low_ref[...]
     hidden_line[p.t, p.z] = hidden_low_ref[
         :, pl.ds(pl.multiple_of(p.z * 2 * share, share), 2 * share)
@@ -1149,7 +1332,6 @@
     hidden_spread.start()
     for copy in xnorm_to:
         copy.start()
-    small[...] = small_ref[...]
     key_sum[...] = jnp.zeros_like(key_sum)
     value_sum[...] = jnp.zeros_like(value_sum)
     fetch[0].wait()
@@ -1169,7 +1351,6 @@
     key_hat, key_scale = normed_rows(key_ref[...])
     key_gained = key_hat * key_gain
     key_low = (key_gained * cosine + turned(key_gained) * sine).astype(LOW)
-    gain_row = 2 * DEPTH * 2 + 2
 
     def norm_back(grad, hat, scale, gain):
         grad = grad * cosine - turned(grad) * sine
@@ -1218,8 +1399,7 @@
         + dot(packed[:, units : units + size], key_weight_ref[...], 1, 1)
         + dot(packed[:, units + size :], value_weight_ref[...], 1, 1)
     ).astype(LOW)
-    for copy in back_to_c:
-        copy.start()
+    fold.start()
     for copy in xnorm_to:
         copy.wait_recv()
 
@@ -1237,19 +1417,12 @@
                 packed_grad_ref[:, a:b] = grad
 
     weight_piece(0)
-    back_to_c[0].wait_recv()
-    there = block(back_part, other)
-    there[...] = (there[...].astype(F32) + back_in[0].astype(F32)).astype(LOW)
-    back_to_x.start()
+    fold.forward()
     scattering[4]()
     weight_piece(1)
     scattering[5]()
 
-    back_to_c[1].wait_recv()
-    back_to_x.wait_recv()
-    xnorm1_grad = (
-        block(back_part, p.t)[...].astype(F32) + back_in[1].astype(F32) + back_in[2].astype(F32)
-    )
+    xnorm1_grad = fold.finish()
     normed1, scale1 = normed_rows(tokens_ref[...].astype(F32))
     small[gain_row - 1 : gain_row, :] = jnp.sum(xnorm1_grad * normed1, axis=0, keepdims=True)
     small_to_c.start()
@@ -1319,12 +1492,13 @@
 
 def run_tail(
     length,
-    hidden_low,
-    hidden_grad,
+    summed,
+    own,
+    router,
     hidden,
+    cotangent,
     tokens,
     xnorm1,
-    small,
     moe,
     heads,
     line_heads,
@@ -1334,36 +1508,42 @@
     cosine,
     sine,
     attention_gain,
+    routing_gain,
     query_gain,
     key_gain,
     query_weight,
     key_weight,
     value_weight,
     output_weight,
+    router_weight,
+    experts,
     collective_id,
 ):
     group, width = xnorm1.shape
-    rows = hidden_low.shape[0]
+    rows = hidden.shape[0]
     units, size = query.shape[1], cosine.shape[1]
     packed_width = units + 2 * size
     share = width // (2 * DEPTH)
     tensors = group // rows
+    smalls = (experts + 4 + 7) // 8 * 8
     vmem = pltpu.VMEM
     return pl.pallas_call(
-        functools.partial(tail_kernel, rows),
+        functools.partial(tail_kernel, rows, experts),
         out_shape=(
             jax.ShapeDtypeStruct((group, width), LOW),
             jax.ShapeDtypeStruct((group, width), LOW),
             jax.ShapeDtypeStruct((share, units), F32),
             jax.ShapeDtypeStruct((share, packed_width), F32),
-            jax.ShapeDtypeStruct((small.shape[0], share), F32),
+            jax.ShapeDtypeStruct((smalls, share), F32),
         ),
         in_specs=[pl.BlockSpec(memory_space=pltpu.SMEM)]
-        + [VMEM_SPEC] * 6
+        + [VMEM_SPEC] * 7
         + [ANY_SPEC, VMEM_SPEC, ANY_SPEC]
-        + [VMEM_SPEC] * 12,
+        + [VMEM_SPEC] * 14,
         out_specs=[VMEM_SPEC] * 5,
         scratch_shapes=[
+            vmem((rows, width), F32),
+            vmem((rows, width), LOW),
             vmem((group, width), LOW),
             vmem((tensors, DEPTH, rows, 2 * share), LOW),
             vmem((DEPTH, group, units), LOW),
@@ -1381,10 +1561,10 @@
             vmem((3, rows, width), LOW),
             vmem(moe.shape, LOW),
             vmem((rows, width), F32),
-            vmem(small.shape, F32),
-            vmem((2, *small.shape), F32),
-            vmem((3, DEPTH, small.shape[0], share), F32),
-            vmem((DEPTH, small.shape[0], share), F32),
+            vmem((smalls, width), F32),
+            vmem((2, smalls, width), F32),
+            vmem((3, DEPTH, smalls, share), F32),
+            vmem((DEPTH, smalls, share), F32),
         ]
         + scatter_scratch(rows, width)
         + semaphores(DEPTH, TAIL_SEMS, TAIL_SEMS, SCATTER_SEMS, SCATTER_SEMS),
@@ -1394,12 +1574,13 @@
         name="tail",
     )(
         length,
-        hidden_low,
-        hidden_grad,
+        summed,
+        own,
+        router,
         hidden,
+        cotangent,
         tokens,
         xnorm1,
-        small,
         moe,
         heads,
         line_heads,
@@ -1409,12 +1590,14 @@
         cosine,
         sine,
         attention_gain,
+        routing_gain,
         query_gain,
         key_gain,
         query_weight,
         key_weight,
         value_weight,
         output_weight,
+        router_weight,
     )
 
 
@@ -1438,129 +1621,88 @@
 ):
     count, width = tokens.shape
     head_size = query_gain.shape[0]
-    local_heads = query_weight.shape[1] // head_size
-    local_groups = key_weight.shape[1] // head_size
-    ratio = local_heads // local_groups
-    length = seq_length[0]
     experts = router_weight.shape[1]
     owned = gate_weight.shape[0]
-    parts = lax.axis_size("tensor")
     part = lax.axis_index("tensor")
     owner = lax.axis_index("expert")
-    rows = count // parts
-    everywhere = ("expert", "tensor")
-    low = jnp.bfloat16
+    rows = count // lax.axis_size("tensor")
 
     def own_rows(values):
         return lax.dynamic_slice_in_dim(values, part * rows, rows, 0)
 
-    upstream_all = gather_rows(own_rows(cotangent), 0)
-    inputs = tokens.astype(jnp.float32)
-    scale1 = rms_scale(inputs)
-    normed1 = inputs * scale1
-    xnorm1 = (normed1 * attention_gain).astype(low)
-    query_flat = jnp.dot(xnorm1, query_weight, preferred_element_type=jnp.float32)
-    key_flat = jnp.dot(xnorm1, key_weight, preferred_element_type=jnp.float32)
-    value_flat = jnp.dot(xnorm1, value_weight, preferred_element_type=jnp.float32).astype(low)
-    query_raw = query_flat.reshape(count, local_heads, head_size)
-    key_raw = key_flat.reshape(count, local_groups, head_size)
-    value_low = value_flat.reshape(count, local_groups, head_size)
-    query_gained, query_normed, query_scale = head_norm(query_raw, query_gain)
-    key_gained, key_normed, key_scale = head_norm(key_raw, key_gain)
     cosine, sine = rope_tables(count, head_size)
-    query_low = rotate(query_gained, cosine, sine).astype(low)
-    key_low = rotate(key_gained, cosine, sine).astype(low)
-    query_block = query_low.reshape(count, local_groups, ratio, head_size)
-    outputs, _ = attend_block(query_block, 0, key_low, value_low, length)
-    valid = (jnp.arange(count, dtype=jnp.int32) < length)[:, None]
-    heads_low = jnp.where(valid, outputs.reshape(count, local_heads * head_size), 0.0).astype(low)
-    attention_part = contract(heads_low, output_weight, 1, 1)
-    attention = lax.psum_scatter(
-        attention_part.astype(low), "tensor", scatter_dimension=0, tiled=True
-    ).astype(jnp.float32)
-
-    hidden = own_rows(inputs) + attention
-    scale2 = rms_scale(hidden)
-    normed2 = hidden * scale2
-    xnorm2 = (normed2 * routing_gain).astype(low)
-    logits = jnp.dot(xnorm2, router_weight, preferred_element_type=jnp.float32)
-    peak = jnp.max(logits, axis=1, keepdims=True)
-    expo = jnp.exp(logits - peak)
-    router = expo / jnp.sum(expo, axis=1, keepdims=True)
-    routes = own_rows(expert_routes)
-    named = jnp.any(
-        routes[:, :, None] == jnp.arange(experts, dtype=jnp.int32)[None, None, :], axis=1
-    )
-    chosen = jnp.where(named, router, 0.0)
-    chosen_total = jnp.sum(chosen, axis=1, keepdims=True)
-    route_weight = chosen / chosen_total
-
-    high = route_weight.astype(low)
-    rest = (route_weight - high.astype(jnp.float32)).astype(low)
-    spare = jnp.zeros((rows, 128 - 2 * experts), low)
-    own = jnp.concatenate([xnorm2, high, rest, spare], axis=1)
-    gate_up = jnp.concatenate([*gate_weight, *up_weight], axis=1)
-    summed, moe_part, line_heads, gate_up_grad, down_grad = run_experts(
+    half = head_size // 2
+    sine = jnp.concatenate([-sine[:, :half], sine[:, half:]], axis=1)
+    router_wide = jnp.pad(router_weight.T, ((0, 128 - experts), (0, 0)))
+    upstream_all, xnorm1, query, key, value, heads, hidden, own, router = run_front(
+        seq_length,
+        tokens,
+        cotangent,
+        own_rows(expert_routes),
+        attention_gain[None],
+        query_gain[None],
+        key_gain[None],
+        routing_gain[None],
+        cosine,
+        sine,
+        query_weight,
+        key_weight,
+        value_weight,
+        output_weight,
+        router_wide,
+        experts,
+        0,
+    )
+
+    def by_unit(weight):
+        return weight.transpose(0, 2, 1).reshape(-1, width)
+
+    def from_units(grad):
+        return grad.reshape(owned, -1, width).transpose(0, 2, 1)
+
+    summed, moe_part, line_heads, gate_grad, up_grad, down_grad = run_experts(
         own,
         upstream_all,
-        gate_up,
+        by_unit(gate_weight),
+        by_unit(up_weight),
         down_weight.reshape(-1, width),
-        heads_low,
+        heads,
         owned,
         experts,
         width,
         1,
     )
-    units = gate_up.shape[1] // (2 * owned)
-    split = [gate_up_grad[:, j * units : (j + 1) * units] for j in range(2 * owned)]
-    gate_grad, up_grad = jnp.stack(split[:owned]), jnp.stack(split[owned:])
-    down_grad = down_grad.reshape(down_weight.shape)
-    xnorm2_moe, route_grad = summed[:, :width], summed[:, width : width + experts]
-
-    upstream = own_rows(cotangent).astype(jnp.float32)
-    inner_total = jnp.sum(route_grad * route_weight, axis=1, keepdims=True)
-    prob_grad = jnp.where(named, (route_grad - inner_total) / chosen_total, 0.0)
-    logit_low = (router * (prob_grad - jnp.sum(router * prob_grad, axis=1, keepdims=True))).astype(
-        low
-    )
-    router_part = contract(logit_low, xnorm2, 0, 0)
-    xnorm2_grad = xnorm2_moe + contract(logit_low, router_weight, 1, 1)
-    routing_gain_part = jnp.sum(xnorm2_grad * normed2, axis=0)
-    inner2 = xnorm2_grad * routing_gain
-    hidden_grad = upstream + scale2 * (
-        inner2 - normed2 * jnp.mean(inner2 * normed2, axis=1, keepdims=True)
-    )
-    small = jnp.concatenate(
-        [router_part, routing_gain_part[None], jnp.zeros((7, width), jnp.float32)], axis=0
-    )
-    half = head_size // 2
     mixed, tokens_grad, output_grad, packed_grad, small_sum = run_tail(
         seq_length,
-        hidden_grad.astype(low),
-        hidden_grad,
+        summed,
+        own,
+        router,
         hidden,
+        own_rows(cotangent),
         own_rows(tokens),
         xnorm1,
-        small,
         moe_part,
-        heads_low,
+        heads,
         line_heads,
-        query_flat,
-        key_flat,
-        value_flat,
+        query,
+        key,
+        value,
         cosine,
-        jnp.concatenate([-sine[:, :half], sine[:, half:]], axis=1),
+        sine,
         attention_gain[None],
+        routing_gain[None],
         query_gain[None],
         key_gain[None],
         query_weight,
         key_weight,
         value_weight,
         output_weight,
+        router_wide,
+        experts,
         2,
     )
-    query_end = local_heads * head_size
-    key_end = query_end + local_groups * head_size
+    query_end = query_weight.shape[1]
+    key_end = query_end + key_weight.shape[1]
     share = head_size // lax.axis_size("expert")
 
     def own_gain(row):
@@ -1578,9 +1720,9 @@
         output_grad,
         small_sum[experts],
         small_sum[:experts].T,
-        gate_grad,
-        up_grad,
-        down_grad,
+        from_units(gate_grad),
+        from_units(up_grad),
+        down_grad.reshape(down_weight.shape),
     )
 
 

time: 435 us -> 375 us (0.86)
  other arithmetic: 25.7 us -> 1.36 us
  local copies, waits for them, and re-layouts: 42.4 us -> 23.7 us
  matrix products: 14.7 us -> 0 us
  between operations: 15.5 us -> 1.38 us
  Pallas kernels: 334 us -> 347 us
    pallas_call x2, Pallas kernels: 193 us -> 215 us  [the longest x1 148 us: run_tail(): pl.pallas_call(functools.partial(tail_kernel, rows, experts), out_shape=(...]
    dot_general x9 -> x0, matrix products: 14.7 us -> none  [the longest x3 7.25 us: contract(): lax.dot_general(left, right, (((left_dim,), (right_dim,)), ((), ())), pre...]
    another operation x3 -> x0, local copies, waits for them, and re-layouts: 10.6 us -> none  [the longest x1 6.46 us: gathered_shards(): gate_grad, up_grad = (jnp.stack(split[:owned]), jnp.stack(split[owned:]))]
    unnamed x65 -> x23, local copies, waits for them, and re-layouts: 21.6 us -> 12 us
    pallas_call x1, Pallas kernels: 141 us -> 132 us  [run_experts(): pl.pallas_call(functools.partial(experts_kernel, rows, width, experts, ow...]
    another operation x2 -> x0, other arithmetic: 6 us -> none  [gathered_shards(): gate_grad, up_grad = (jnp.stack(split[:owned]), jnp.stack(split[owned:]))]
    reduce_sum x8 -> x0, other arithmetic: 5.81 us -> none  [the longest x3 3.15 us: rms_scale(): jnp.mean(values * values, axis=-1, keepdims=True) + EPSILON]
    concatenate x4 -> x1, other arithmetic: 5.87 us -> 0.84 us  [rope_tables(): cosine = jnp.concatenate([jnp.cos(angles), jnp.cos(angles)], axis=1)]
  transfers between devices with their start and end apart: 1 -> 0, of which waited for: 0 -> 0; matrix products, arithmetic and copies ran while one was open for 4% -> 0% of each run, Pallas kernels for 12% -> 0%
where the time goes in v3:
time: 375 us; the launch traced here: 373 us
  Pallas kernels  347 us (93%)
  local copies, waits for them, and re-layouts  23.7 us (6%)
    pallas_call x1, Pallas kernels, run_tail(): pl.pallas_call(functools.partial(tail_kernel, rows, experts), out_shape=(...  148 us
    pallas_call x1, Pallas kernels, run_experts(): pl.pallas_call(functools.partial(experts_kernel, rows, width, experts, ow...  132 us
    pallas_call x1, Pallas kernels, run_front(): pl.pallas_call(functools.partial(front_kernel, rows, experts), out_shape=...  67.1 us
    unnamed x23, local copies, waits for them, and re-layouts  12 us

profile of v3, /device:TPU:0, one launch (start us, length us, event | category | flops | bytes accessed | tf_op | source)
XLA Modules:
  0.0 373.1 jit_solution(12416447818616780605)
XLA Ops:
  0.6 0.0 copy-start
  0.7 0.7 copy-done
  1.3 0.1 constant_dynamic-slice_fusion.4
  1.4 0.7 copy.31.routes_ref
  2.1 0.5 fusion.2
  2.6 0.8 pad_maximum_fusion
  3.5 1.7 pad.4.router_weight_ref
  5.8 67.1 %front.1 = (bf16[2048,2048]{1,0:T(8,128)(2,1)}, bf16[256,2048]{1,0:T(8,128)(2,1)}, f32[256,1024]{1,0:T(8,128)}, f32[256,128]{1,0:T(8,128)}, bf16[256,128]{1,0:T(...) custom-call(s32[1]{0:T(128)S(6)} %copy.38.length_ref, ...), custom_call_target="tpu_custom_call" | custom-call | tf_op jit(solution)/shard_map/front/pallas_call | solution.py:1118
  72.9 132.0 %experts.1 = (f32[64,2176]{1,0:T(8,128)}, bf16[2048,2048]{1,0:T(8,128)(2,1)}, bf16[4,256,1024]{2,1,0:T(8,128)(2,1)}, f32[384,2048]{1,0:T(8,128)}, f32[384,2048]{1,0:T(8,128)}, /*index=5*/f32[384,2048]{1,0:T(8,128)}) custom-call(bf16[64,2176]{1,0:T(8,128)(2,1)} %get-tuple-element.34.own_ref, bf16[2048,2048]{1,0:T(8,128)(2,1)} %get-tuple-element.35.upstream_ref, ...), custom_call_target="tpu_custom_call" | custom-call | tf_op jit(solution)/shard_map/experts/pallas_call | solution.py:883
  204.9 1.9 constant_dynamic-slice_fusion.2
  206.8 147.6 %tail.1 = (bf16[256,2048]{1,0:T(8,128)(2,1)}, bf16[256,2048]{1,0:T(8,128)(2,1)}, f32[256,1024]{1,0:T(8,128)}, f32[256,1280]{1,0:T(8,128)}, f32[24,256]{1,0:T(8,128)}) custom-call(s32[1]{0:T(128)S(6)} %copy.38.length_ref, f32[64,2176]{1,0:T(8,128)} %get-tuple-element.37.summed_ref, bf16[64,2176]{1,0:T(8,128)(2,1)} %get-tuple-element.34.own_ref, ...), custom_call_target="tpu_custom_call" | custom-call | tf_op jit(solution)/shard_map/tail/pallas_call | solution.py:1530
  354.4 0.0 copy-start.7
  354.4 0.0 copy-start.6
  354.4 0.0 copy-start.5
  354.4 2.5 slice.25
  356.9 1.7 fusion.5
  358.5 1.3 slice_bitcast_fusion
  359.9 1.4 fusion.6
  361.3 0.6 fusion.3
  361.9 0.6 fusion.4
  362.4 0.0 copy-done.7
  362.4 1.0 copy.39
  363.4 0.0 copy-done.6
  363.4 1.0 copy.40
  364.4 0.0 copy-done.5
  364.4 1.0 copy.41
  365.4 0.0 copy-done.4
  365.4 1.7 copy.42
  367.0 1.4 copy-done.3
  368.4 1.7 copy.43
  370.1 1.4 copy-done.2
  371.4 1.7 copy.44
  (6 shorter events, 0.0 us)
Async XLA Ops:
  0.6 0.7 copy-start
  354.4 8.1 %copy-start.7 = (bf16[256,2048]{1,0:T(8,128)(2,1)S(1)}, bf16[256,2048]{1,0:T(8,128)(2,1)}, u32[]{:S(2)}) copy-start(bf16[256,2048]{1,0:T(8,128)(2,1)} %get-tuple-element.81) | copy-start | bytes 3145732
  354.4 9.0 %copy-start.6 = (bf16[256,2048]{1,0:T(8,128)(2,1)S(1)}, bf16[256,2048]{1,0:T(8,128)(2,1)}, u32[]{:S(2)}) copy-start(bf16[256,2048]{1,0:T(8,128)(2,1)} %get-tuple-element.82) | copy-start | bytes 3145732
  354.4 10.0 %copy-start.5 = (f32[256,1024]{1,0:T(8,128)S(1)}, f32[256,1024]{1,0:T(8,128)}, u32[]{:S(2)}) copy-start(f32[256,1024]{1,0:T(8,128)} %get-tuple-element.89) | copy-start | bytes 3145732
  362.4 2.9 copy-start.4
  365.4 3.0 copy-start.3
  368.4 3.0 copy-start.2
  368.4 4.7 %copy-start.1 = (s32[256,8]{0,1:T(8,128)S(1)}, s32[256,8]{0,1:T(8,128)}, u32[]{:S(2)}) copy-start(s32[256,8]{0,1:T(8,128)} %param.18) | copy-start | bytes 24580

commit v4 on v3

--- a/solution.py
+++ b/solution.py
@@ -470,9 +470,105 @@
             out.append((there, back))
         return out
 
+    def between(self, src, dst, to, send, recv):
+        return pltpu.make_async_remote_copy(
+            src,
+            dst,
+            self.send_sems.at[send],
+            self.recv_sems.at[recv],
+            device_id=to,
+            device_id_type=MESH_ID,
+        )
+
     def finish(self):
         for copy in self.made:
             copy.wait_send()
+
+
+class LineSend:
+    SEMS = DEPTH
+
+    def __init__(self, p, copies, src, slot):
+        others = [p.near(k) for k in range(1, DEPTH)]
+        self.pairs = copies.along(
+            [(z, src, slot(p.z)) for z in others], [p.at(z=z) for z in others], p.z
+        )
+
+    def start(self):
+        for there, _ in self.pairs:
+            there.start()
+
+    def wait(self, k):
+        self.pairs[k - 1][1].wait_recv()
+
+
+class LineSum:
+    SEMS = 4
+
+    def __init__(self, p, copies, terms, arrived):
+        base = copies.used
+        copies.used += self.SEMS
+        near = {k: p.at(z=p.near(k)) for k in range(1, DEPTH)}
+        self.inner = (p.z == 1) | (p.z == 2)
+        arrived = [arrived.at[i] for i in range(DEPTH)]
+        self.terms, self.arrived = terms, arrived
+        self.outer_to = {
+            1: copies.between(terms[1], arrived[0], near[1], base, base),
+            2: copies.between(terms[2], arrived[2], near[1], base + 1, base + 2),
+            3: copies.between(terms[3], arrived[3], near[1], base + 2, base + 3),
+        }
+        self.inner_to = {
+            2: copies.between(terms[2], arrived[0], near[2], base, base),
+            1: copies.between(terms[1], arrived[1], near[1], base + 1, base + 1),
+            3: copies.between(terms[3], arrived[1], near[3], base + 2, base + 1),
+        }
+        copies.made += self.outer_to.values()
+
+    def send(self, k):
+        pl.when(jnp.logical_not(self.inner))(self.outer_to[k].start)
+        if k == 2:
+            pl.when(self.inner)(self.inner_to[2].start)
+
+    def relay(self):
+        @pl.when(self.inner)
+        def _():
+            for k, behind in ((3, 3), (1, 2)):
+                self.outer_to[behind].wait_recv()
+                term = self.terms[k]
+                term[...] = (term[...].astype(F32) + self.arrived[behind][...].astype(F32)).astype(
+                    LOW
+                )
+                self.inner_to[k].start()
+
+    def wait(self):
+        self.inner_to[2].wait_recv()
+        self.inner_to[1].wait_recv()
+        return self.arrived[:2]
+
+
+class StraightSum:
+    SEMS = DEPTH
+
+    def __init__(self, p, copies, terms, arrived):
+        others = [p.near(k) for k in range(1, DEPTH)]
+        slots = [arrived.at[p.near(k)] for k in range(1, DEPTH)]
+        self.slots = slots
+        self.pairs = copies.along(
+            [(z, terms[k], arrived.at[p.z]) for k, z in enumerate(others, 1)],
+            [p.at(z=z) for z in others],
+            p.z,
+        )
+
+    def send(self, k):
+        self.pairs[k - 1][0].start()
+
+    def relay(self):
+        pass
+
+    def wait(self):
+        for _, back in self.pairs:
+            back.wait_recv()
+        return self.slots
 
 
 def enter(peers):
@@ -497,7 +593,7 @@
     return whole, first, second
 
 
-GATHER_SEMS = DEPTH + 3 * DEPTH + 4 * DEPTH + 2 * DEPTH
+GATHER_SEMS = LineSend.SEMS + 3 * DEPTH + 4 * DEPTH + 2 * DEPTH
 
 
 def gather_steps(p, copies, rows, own_ref, all_ref, own_copy):
@@ -505,9 +601,7 @@
     me = p.block()
     xn, yn, cn = p.at(x=1 - p.x), p.at(y=1 - p.y), p.at(c=1 - p.c)
     order = [p.near(k) for k in range(DEPTH)]
-    line = copies.along(
-        [(z, own_ref, whole(me)) for z in order[1:]], [p.at(z=z) for z in order[1:]], p.z
-    )
+    line = LineSend(p, copies, own_ref, lambda z: whole(p.block(z=z)))
     to_x, to_y, near, far, diagonal = [], [], [], [], []
     for d in range(DEPTH):
         b = p.block(z=order[d])
@@ -530,7 +624,7 @@
 
     def onward(d):
         if d:
-            line[d - 1][1].wait_recv()
+            line.wait(d)
         to_x[d].start()
         to_y[d].start()
         near[d][0].start()
@@ -554,8 +648,7 @@
 
     def begin():
         own_copy.start()
-        for there, _ in line:
-            there.start()
+        line.start()
         onward(0)
 
     def step0():
@@ -598,7 +691,7 @@
     ]
 
 
-SCATTER_SEMS = 16 + 8 + 8 + DEPTH
+SCATTER_SEMS = 16 + 8 + 8 + LineSum.SEMS
 
 
 def scatter_scratch(rows, width):
@@ -610,101 +703,91 @@
     ]
 
 
-def scatter_steps(p, copies, rows, part, core_in, diag_in, side_in, line_in, out_ref):
-    whole, first, second = pieces_of(part, rows)
-    order = [p.near(k) for k in reversed(range(DEPTH))]
-    xn, yn, cn = p.at(x=1 - p.x), p.at(y=1 - p.y), p.at(c=1 - p.c)
-    kinds = [dict(y=1 - p.y, x=1 - p.x), dict(x=1 - p.x), dict(y=1 - p.y), dict()]
-    blocks = [[p.block(z=z, **kind) for kind in kinds] for z in order]
-    core = [
-        [
-            copies.make(whole(p.block(z=z, c=1 - p.c, **kind)), core_in.at[k * 4 + j], cn)
-            for j, kind in enumerate(kinds)
+class Scatter:
+    def __init__(self, p, copies, rows, part, core_in, diag_in, side_in, line_in, order, kind):
+        whole, first, second = pieces_of(part, rows)
+        positions = [p.near(k) for k in order]
+        xn, yn, cn = p.at(x=1 - p.x), p.at(y=1 - p.y), p.at(c=1 - p.c)
+        kinds = [dict(y=1 - p.y, x=1 - p.x), dict(x=1 - p.x), dict(y=1 - p.y), dict()]
+        self.core_in, self.diag_in, self.side_in = core_in, diag_in, side_in
+        self.order = order
+        blocks = [[p.block(z=z, **kind) for kind in kinds] for z in positions]
+        self.wholes = [[whole(b) for b in row] for row in blocks]
+        self.first = [first(row[1]) for row in blocks]
+        self.second = [second(row[2]) for row in blocks]
+        self.core = [
+            [
+                copies.make(whole(p.block(z=z, c=1 - p.c, **kind)), core_in.at[k * 4 + j], cn)
+                for j, kind in enumerate(kinds)
+            ]
+            for k, z in enumerate(positions)
         ]
-        for k, z in enumerate(order)
-    ]
-    corners = [
-        (
-            copies.make(first(blocks[k][0]), diag_in.at[0, k], yn),
-            copies.make(second(blocks[k][0]), diag_in.at[1, k], xn),
+        self.corners = [
+            (
+                copies.make(first(row[0]), diag_in.at[0, k], yn),
+                copies.make(second(row[0]), diag_in.at[1, k], xn),
+            )
+            for k, row in enumerate(blocks)
+        ]
+        self.sides = [
+            (
+                copies.make(whole(row[1]), side_in.at[0, k], xn),
+                copies.make(whole(row[2]), side_in.at[1, k], yn),
+            )
+            for k, row in enumerate(blocks)
+        ]
+        self.line = kind(
+            p, copies, {order[k]: self.wholes[k][3] for k in range(DEPTH)}, line_in
         )
-        for k in range(DEPTH)
-    ]
-    sides = [
-        (
-            copies.make(whole(blocks[k][1]), side_in.at[0, k], xn),
-            copies.make(whole(blocks[k][2]), side_in.at[1, k], yn),
-        )
-        for k in range(DEPTH)
-    ]
-    line = copies.along(
-        [(order[k], whole(blocks[k][3]), line_in.at[p.z]) for k in range(DEPTH - 1)],
-        [p.at(z=order[k]) for k in range(DEPTH - 1)],
-        p.z,
-    )
-
-    def add(ref, *more):
+
+    def add(self, ref, *more):
         total = ref[...].astype(F32)
         for other in more:
             total = total + other[...].astype(F32)
         ref[...] = total.astype(LOW)
 
-    def corner(k):
-        core[k][0].wait_recv()
-        add(whole(blocks[k][0]), core_in.at[k * 4])
-        for copy in corners[k]:
+    def start(self, k):
+        for copy in self.core[k]:
+            copy.start()
+
+    def corner(self, k):
+        self.core[k][0].wait_recv()
+        self.add(self.wholes[k][0], self.core_in.at[k * 4])
+        for copy in self.corners[k]:
             copy.start()
         for j in (1, 2):
-            core[k][j].wait_recv()
-            add(whole(blocks[k][j]), core_in.at[k * 4 + j])
-
-    def side(k):
-        corners[k][0].wait_recv()
-        add(first(blocks[k][1]), diag_in.at[0, k])
-        sides[k][0].start()
-        corners[k][1].wait_recv()
-        add(second(blocks[k][2]), diag_in.at[1, k])
-        sides[k][1].start()
-        core[k][3].wait_recv()
-
-    def close(k):
-        sides[k][0].wait_recv()
-        sides[k][1].wait_recv()
-        add(whole(blocks[k][3]), core_in.at[k * 4 + 3], side_in.at[0, k], side_in.at[1, k])
-        if k < DEPTH - 1:
-            line[k][0].start()
-
-    def step0():
-        for row in core:
-            for copy in row:
-                copy.start()
-        corner(0)
-
-    def step1():
-        corner(1)
-        side(0)
-
-    def step2():
-        corner(2)
-        side(1)
-
-    def step3():
-        corner(3)
-        side(2)
-        close(0)
-
-    def step4():
-        side(3)
-        close(1)
-
-    def step7():
-        total = whole(blocks[DEPTH - 1][3])[...].astype(F32)
-        for k in reversed(range(DEPTH - 1)):
-            line[k][1].wait_recv()
-            total = total + line_in[order[k]].astype(F32)
-        out_ref[...] = total
-
-    return [step0, step1, step2, step3, step4, lambda: close(2), lambda: close(3), step7]
+            self.core[k][j].wait_recv()
+            self.add(self.wholes[k][j], self.core_in.at[k * 4 + j])
+
+    def side(self, k):
+        self.corners[k][0].wait_recv()
+        self.add(self.first[k], self.diag_in.at[0, k])
+        self.sides[k][0].start()
+        self.corners[k][1].wait_recv()
+        self.add(self.second[k], self.diag_in.at[1, k])
+        self.sides[k][1].start()
+        self.core[k][3].wait_recv()
+
+    def close(self, k):
+        for copy in self.sides[k]:
+            copy.wait_recv()
+        self.add(
+            self.wholes[k][3],
+            self.core_in.at[k * 4 + 3],
+            self.side_in.at[0, k],
+            self.side_in.at[1, k],
+        )
+        if self.order[k]:
+            self.line.send(self.order[k])
+
+    def relay(self, _):
+        self.line.relay()
+
+    def finish(self):
+        total = self.wholes[self.order.index(0)][3][...].astype(F32)
+        for term in self.line.wait():
+            total = total + term[...].astype(F32)
+        return total
 
 
 def dot(left, right, left_dim, right_dim):
@@ -731,10 +814,8 @@
     gate_ref,
     up_ref,
     down_ref,
-    heads_ref,
     grad_ref,
     moe_ref,
-    line_heads_ref,
     gate_grad_ref,
     up_grad_ref,
     down_grad_ref,
@@ -752,8 +833,6 @@
     gather_recv,
     scatter_send,
     scatter_recv,
-    heads_send,
-    heads_recv,
 ):
     p = Place()
     group = rows * 4
@@ -766,14 +845,41 @@
     gather_copies = Copies(gather_send, gather_recv)
     scatter_copies = Copies(scatter_send, scatter_recv)
     gathering = gather_steps(p, gather_copies, rows, own_ref, all_ref, own_copy)
-    scattering = scatter_steps(
-        p, scatter_copies, rows, part, core_in, diag_in, side_in, line_in, grad_ref
-    )
-    heads_copies = Copies(heads_send, heads_recv)
-    others = [p.near(k) for k in range(1, DEPTH)]
-    heads_line = heads_copies.along(
-        [(z, heads_ref, line_heads_ref.at[p.z]) for z in others], [p.at(z=z) for z in others], p.z
-    )
+    sums = Scatter(
+        p,
+        scatter_copies,
+        rows,
+        part,
+        core_in,
+        diag_in,
+        side_in,
+        line_in,
+        list(range(DEPTH)),
+        StraightSum,
+    )
+
+    def finish():
+        grad_ref[...] = sums.finish()
+
+    beside_work = {
+        2: [(sums.start, 0)],
+        3: [(sums.corner, 0)],
+        4: [(sums.start, 1)],
+        5: [(sums.corner, 1), (sums.side, 0)],
+        6: [(sums.start, 2)],
+        7: [(sums.corner, 2), (sums.side, 1), (sums.close, 0)],
+    }
+    beside_tiles = {
+        0: [(sums.start, 3), (sums.side, 2), (sums.close, 1), (sums.corner, 3)],
+        2: [(sums.side, 3)],
+        3: [(sums.close, 2)],
+        5: [(sums.close, 3)],
+    }
+
+    def run(actions):
+        for stage, k in actions:
+            stage(k)
+
     count = 2 * DEPTH
 
     def rows_of(i):
@@ -799,6 +905,8 @@
 
     @pl.loop(0, count)
     def _(i):
+        for k, actions in beside_work.items():
+            pl.when(i == k)(functools.partial(run, actions))
         for k, step in enumerate(gathering[1:]):
             pl.when(i == k)(step)
         at = rows_of(i)
@@ -853,29 +961,25 @@
         ).astype(LOW)
         part[at, width:] = note.astype(LOW)
 
-    for there, _ in heads_line:
-        there.start()
     tile = width // count
 
     @pl.loop(0, count)
     def _(i):
-        for k, step in enumerate(scattering):
-            pl.when(i == k)(step)
+        for k, actions in beside_tiles.items():
+            pl.when(i == k)(functools.partial(run, actions))
         at = pl.ds(pl.multiple_of(i * tile, tile), tile)
         x = all_ref[:, at]
         gate_grad_ref[:, at] = dot(back_rows[:, :units], x, 0, 0)
         up_grad_ref[:, at] = dot(back_rows[:, units:], x, 0, 0)
 
+    finish()
     gather_copies.finish()
     scatter_copies.finish()
     store(count - 2).wait()
     store(count - 1).wait()
-    for _, back in heads_line:
-        back.wait_recv()
-    heads_copies.finish()
-
-
-def run_experts(own, upstream_all, gate, up, down, heads, owned, experts, width, collective_id):
+
+
+def run_experts(own, upstream_all, gate, up, down, owned, experts, width, collective_id):
     rows, full = own.shape
     total = upstream_all.shape[0]
     units = down.shape[0]
@@ -885,11 +989,10 @@
         out_shape=(
             jax.ShapeDtypeStruct((rows, full), F32),
             jax.ShapeDtypeStruct((total, width), LOW),
-            jax.ShapeDtypeStruct((DEPTH, *heads.shape), LOW),
             *[jax.ShapeDtypeStruct((units, width), F32)] * 3,
         ),
-        in_specs=[VMEM_SPEC, ANY_SPEC, VMEM_SPEC, VMEM_SPEC, VMEM_SPEC, ANY_SPEC],
-        out_specs=(VMEM_SPEC, ANY_SPEC, ANY_SPEC, VMEM_SPEC, VMEM_SPEC, VMEM_SPEC),
+        in_specs=[VMEM_SPEC, ANY_SPEC, VMEM_SPEC, VMEM_SPEC, VMEM_SPEC],
+        out_specs=(VMEM_SPEC, ANY_SPEC, VMEM_SPEC, VMEM_SPEC, VMEM_SPEC),
         scratch_shapes=[
             pltpu.VMEM((total, full), LOW),
             pltpu.VMEM((2, group, width), LOW),
@@ -898,12 +1001,12 @@
             pltpu.VMEM((total, 2 * units), LOW),
         ]
         + scatter_scratch(rows, full)
-        + semaphores(5, GATHER_SEMS, GATHER_SEMS, SCATTER_SEMS, SCATTER_SEMS, DEPTH, DEPTH),
+        + semaphores(5, GATHER_SEMS, GATHER_SEMS, SCATTER_SEMS, SCATTER_SEMS),
         compiler_params=pltpu.CompilerParams(
             collective_id=collective_id, has_side_effects=True, vmem_limit_bytes=64000000
         ),
         name="experts",
-    )(own, upstream_all, gate, up, down, heads)
+    )(own, upstream_all, gate, up, down)
 
 
 def normed_rows(values):
@@ -979,6 +1082,7 @@
 
 
 FOLD_SEMS = 3
+FRONT_SEMS = FOLD_SEMS + 2 * LineSend.SEMS
 
 
 def front_kernel(
@@ -1005,6 +1109,7 @@
     key_ref,
     value_ref,
     heads_ref,
+    line_heads_ref,
     hidden_ref,
     own_ref,
     router_ref,
@@ -1031,6 +1136,19 @@
     own_copy = pltpu.make_async_copy(own_cotangent, whole(p.block()), local_sems.at[0])
     gathering = gather_steps(p, gather_copies, rows, own_cotangent, upstream_ref, own_copy)
     fold = Fold(p, copies, rows, part, part_in)
+    line = [
+        LineSend(
+            p,
+            copies,
+            heads_ref.at[:, a:b],
+            lambda z, a=a, b=b: line_heads_ref.at[z, :, a:b],
+        )
+        for a, b in ((0, units // 2), (units // 2, units))
+    ]
+
+    def send_heads(i):
+        line[i].start()
+
     gathering[0]()
 
     normed1, _ = normed_rows(tokens_ref[...].astype(F32))
@@ -1049,6 +1167,7 @@
 
     @pl.loop(0, count)
     def _(h):
+        pl.when(h == count // 2)(functools.partial(send_heads, 0))
         for k in (2, 3):
             pl.when(h == 2 * k)(gathering[k])
         at = pl.ds(pl.multiple_of(h * size, size), size)
@@ -1058,6 +1177,7 @@
         probs = attention_probs(query_low, key_low, allowed).astype(LOW)
         heads_ref[:, at] = jnp.where(valid, dot(probs, value_ref[...], 1, 0), 0.0).astype(LOW)
 
+    send_heads(1)
     part[...] = dot(heads_ref[...], output_weight_ref[...], 1, 1).astype(LOW)
     fold.start()
     gathering[4]()
@@ -1085,8 +1205,11 @@
     router_ref[:, :lanes] = router
     router_ref[:, lanes : 2 * lanes] = route_weight
     router_ref[:, 2 * lanes :] = named
-    for step in gathering[7:]:
-        step()
+    gathering[7]()
+    gathering[8]()
+    for half in line:
+        for k in range(1, DEPTH):
+            half.wait(k)
     gather_copies.finish()
     copies.finish()
 
@@ -1124,14 +1247,15 @@
             struct((group, key_weight.shape[1]), F32),
             struct((group, value_weight.shape[1]), LOW),
             struct((group, query_weight.shape[1]), LOW),
+            struct((DEPTH, group, query_weight.shape[1]), LOW),
             struct((rows, width), F32),
             struct((rows, width + lanes), LOW),
             struct((rows, 3 * lanes), F32),
         ),
         in_specs=[pl.BlockSpec(memory_space=pltpu.SMEM), VMEM_SPEC, ANY_SPEC] + [VMEM_SPEC] * 12,
-        out_specs=[ANY_SPEC] + [VMEM_SPEC] * 8,
+        out_specs=[ANY_SPEC] + [VMEM_SPEC] * 5 + [ANY_SPEC] + [VMEM_SPEC] * 3,
         scratch_shapes=[pltpu.VMEM((group, width), LOW), pltpu.VMEM((3, rows, width), LOW)]
-        + semaphores(1, GATHER_SEMS, GATHER_SEMS, FOLD_SEMS, FOLD_SEMS),
+        + semaphores(1, GATHER_SEMS, GATHER_SEMS, FRONT_SEMS, FRONT_SEMS),
         compiler_params=pltpu.CompilerParams(
             collective_id=collective_id, has_side_effects=True, vmem_limit_bytes=60000000
         ),
@@ -1156,7 +1280,7 @@
 
 
 SPREAD_SEMS = 3
-TAIL_SEMS = 4 * SPREAD_SEMS + DEPTH + DEPTH + 2 + 2 * DEPTH + 1 + 3 + 3 + DEPTH
+TAIL_SEMS = 4 * SPREAD_SEMS + DEPTH + DEPTH + 2 + 2 * LineSum.SEMS + 1 + 3 + 3 + DEPTH
 
 
 def tail_kernel(
@@ -1210,7 +1334,6 @@
     back_part,
     back_in,
     moe,
-    moe_own,
     small,
     small_in,
     small_side,
@@ -1247,8 +1370,17 @@
     enter(p.peers())
     copies = Copies(send_sems, recv_sems)
     scatter_copies = Copies(scatter_send, scatter_recv)
-    scattering = scatter_steps(
-        p, scatter_copies, rows, moe, core_in, diag_in, side_in, line_in, moe_own
+    sums = Scatter(
+        p,
+        scatter_copies,
+        rows,
+        moe,
+        core_in,
+        diag_in,
+        side_in,
+        line_in,
+        [3, 2, 1, 0],
+        LineSum,
     )
     xn, yn, cn = p.at(x=1 - p.x), p.at(y=1 - p.y), p.at(c=1 - p.c)
     order = [p.near(k) for k in reversed(range(DEPTH))]
@@ -1279,14 +1411,12 @@
     ]
     cuts = [(0, units // 2), (units // 2, packed_width)]
     packed_to = [copies.make(packed.at[:, a:b], packed_in.at[:, a:b], yn) for a, b in cuts]
-    weight_to = [
-        copies.along(
-            [
-                (order[k], weight_out.at[k, :, a:b], weight_in.at[p.z, :, a:b])
-                for k in range(DEPTH - 1)
-            ],
-            along,
-            p.z,
+    weight_sums = [
+        LineSum(
+            p,
+            copies,
+            {k: weight_out.at[k - 1, :, a:b] for k in range(1, DEPTH)},
+            weight_in.at[:, :, a:b],
         )
         for a, b in cuts
     ]
@@ -1315,6 +1445,9 @@
     )
     small[...] = jnp.zeros_like(small)
     small[:experts, :] = dot(logit_low, own_ref[:, :width], 0, 0)[:experts]
+    fetch[0].wait()
+    for k in range(DEPTH):
+        sums.start(k)
     xnorm2_grad = summed_ref[:, :width] + dot(logit_low, router_weight_ref[...], 1, 0)
     normed2, scale2 = normed_rows(hidden_ref[...])
     small[experts : experts + 1, :] = jnp.sum(xnorm2_grad * normed2, axis=0, keepdims=True)
@@ -1334,10 +1467,10 @@
         copy.start()
     key_sum[...] = jnp.zeros_like(key_sum)
     value_sum[...] = jnp.zeros_like(value_sum)
-    fetch[0].wait()
-    scattering[0]()
+    sums.corner(0)
     hidden_spread.forward()
-    scattering[1]()
+    sums.corner(1)
+    sums.corner(2)
     hidden_spread.finish()
 
     valid = lax.broadcasted_iota(jnp.int32, (group, 1), 0) < length
@@ -1378,7 +1511,8 @@
 
     pl.loop(0, count // 2)(one_head)
     packed_to[0].start()
-    scattering[2]()
+    sums.corner(3)
+    sums.side(0)
     for _, back in hidden_to:
         back.wait_recv()
     line_spread.start()
@@ -1393,7 +1527,7 @@
         for i in range(1, width // size):
             small[row : row + 1, i * size : (i + 1) * size] = part
     line_spread.forward()
-    scattering[3]()
+    sums.side(1)
     back_part[...] = (
         dot(packed[:, :units], query_weight_ref[...], 1, 1)
         + dot(packed[:, units : units + size], key_weight_ref[...], 1, 1)
@@ -1406,21 +1540,24 @@
     def weight_piece(i):
         a, b = cuts[i]
         packed_to[i].wait_recv()
-        for k, z in enumerate(order):
+        for k in reversed(range(DEPTH)):
+            z = p.near(k)
             grad = dot(xnorm1_ref[:, columns(z, p.y)], packed[:, a:b], 0, 0) + dot(
                 xnorm_in[z], packed_in[:, a:b], 0, 0
             )
-            if k < DEPTH - 1:
-                weight_out[k, :, a:b] = grad.astype(LOW)
-                weight_to[i][k][0].start()
+            if k:
+                weight_out[k - 1, :, a:b] = grad.astype(LOW)
+                weight_sums[i].send(k)
             else:
                 packed_grad_ref[:, a:b] = grad
 
     weight_piece(0)
     fold.forward()
-    scattering[4]()
+    sums.side(2)
+    weight_sums[0].relay()
     weight_piece(1)
-    scattering[5]()
+    sums.side(3)
+    sums.close(0)
 
     xnorm1_grad = fold.finish()
     normed1, scale1 = normed_rows(tokens_ref[...].astype(F32))
@@ -1448,15 +1585,16 @@
     output_out[...] = output_piece(1 - p.y).astype(LOW)
     output_to.start()
     output_grad_ref[...] = output_piece(p.y)
-    scattering[6]()
+    weight_sums[1].relay()
+    sums.close(1)
     small_to_c.wait_recv()
     small_to_c.wait_send()
     small[...] += small_in[0]
     small_to_x.start()
     tokens_spread.forward()
-    scattering[7]()
-    block(mixed_ref, p.t)[...] = (hidden_ref[...] + moe_own[...]).astype(LOW)
-    mixed_spread.start()
+    sums.close(2)
+    sums.close(3)
+    sums.relay(0)
     small_to_x.wait_recv()
     small_to_x.wait_send()
     small[...] += small_in[1]
@@ -1470,20 +1608,19 @@
     small_side[2] += small_side[1]
     for there, _ in small_to:
         there.start()
-    mixed_spread.forward()
     tokens_spread.finish()
+    block(mixed_ref, p.t)[...] = (hidden_ref[...] + sums.finish()).astype(LOW)
+    mixed_spread.start()
     small_total = small_side[2, p.z]
     for (_, back), z in zip(small_to, order):
         back.wait_recv()
         small_total += small_line[z]
     small_out_ref[...] = small_total
+    mixed_spread.forward()
     mixed_spread.finish()
     for i, (a, b) in enumerate(cuts):
-        grad = packed_grad_ref[:, a:b]
-        for (_, back), z in zip(weight_to[i], order):
-            back.wait_recv()
-            grad += weight_in[z, :, a:b].astype(F32)
-        packed_grad_ref[:, a:b] = grad
+        for term in weight_sums[i].wait():
+            packed_grad_ref[:, a:b] += term[...].astype(F32)
     for copy in copies.made:
         if copy is not small_to_c and copy is not small_to_x:
             copy.wait_send()
@@ -1560,7 +1697,6 @@
             vmem((group, width), LOW),
             vmem((3, rows, width), LOW),
             vmem(moe.shape, LOW),
-            vmem((rows, width), F32),
             vmem((smalls, width), F32),
             vmem((2, smalls, width), F32),
             vmem((3, DEPTH, smalls, share), F32),
@@ -1634,7 +1770,7 @@
     half = head_size // 2
     sine = jnp.concatenate([-sine[:, :half], sine[:, half:]], axis=1)
     router_wide = jnp.pad(router_weight.T, ((0, 128 - experts), (0, 0)))
-    upstream_all, xnorm1, query, key, value, heads, hidden, own, router = run_front(
+    upstream_all, xnorm1, query, key, value, heads, line_heads, hidden, own, router = run_front(
         seq_length,
         tokens,
         cotangent,
@@ -1660,13 +1796,12 @@
     def from_units(grad):
         return grad.reshape(owned, -1, width).transpose(0, 2, 1)
 
-    summed, moe_part, line_heads, gate_grad, up_grad, down_grad = run_experts(
+    summed, moe_part, gate_grad, up_grad, down_grad = run_experts(
         own,
         upstream_all,
         by_unit(gate_weight),
         by_unit(up_weight),
         down_weight.reshape(-1, width),
-        heads,
         owned,
         experts,
         width,

time: 375 us -> 336 us (0.90)
  Pallas kernels: 347 us -> 305 us
    pallas_call x1, Pallas kernels: 148 us -> 110 us  [run_tail(): pl.pallas_call(functools.partial(tail_kernel, rows, experts), out_shape=(...]
    pallas_call x1, Pallas kernels: 132 us -> 114 us  [run_experts(): pl.pallas_call(functools.partial(experts_kernel, rows, width, experts, ow...]
    pallas_call x1, Pallas kernels: 67.1 us -> 80.7 us  [run_front(): pl.pallas_call(functools.partial(front_kernel, rows, experts), out_shape=...]
where the time goes in v4:
time: 336 us; the launch traced here: 331 us
  Pallas kernels  305 us (91%)
  local copies, waits for them, and re-layouts  23.7 us (7%)
    pallas_call x1, Pallas kernels, run_experts(): pl.pallas_call(functools.partial(experts_kernel, rows, width, experts, ow...  114 us
    pallas_call x1, Pallas kernels, run_tail(): pl.pallas_call(functools.partial(tail_kernel, rows, experts), out_shape=(...  110 us
    pallas_call x1, Pallas kernels, run_front(): pl.pallas_call(functools.partial(front_kernel, rows, experts), out_shape=...  80.7 us
    unnamed x23, local copies, waits for them, and re-layouts  12 us

profile of v4, /device:TPU:0, one launch (start us, length us, event | category | flops | bytes accessed | tf_op | source)
XLA Modules:
  0.0 331.2 jit_solution(6182234423645570454)
XLA Ops:
  0.6 0.0 copy-start
  0.7 0.7 copy-done
  1.3 0.1 constant_dynamic-slice_fusion.4
  1.4 0.7 copy.31.routes_ref
  2.1 0.5 fusion.2
  2.6 0.8 pad_maximum_fusion
  3.5 1.7 pad.4.router_weight_ref
  5.8 80.7 %front.1 = (bf16[2048,2048]{1,0:T(8,128)(2,1)}, bf16[256,2048]{1,0:T(8,128)(2,1)}, f32[256,1024]{1,0:T(8,128)}, f32[256,128]{1,0:T(8,128)}, bf16[256,128]{1,0:T(...) custom-call(s32[1]{0:T(128)S(6)} %copy.38.length_ref, ...), custom_call_target="tpu_custom_call" | custom-call | tf_op jit(solution)/shard_map/front/pallas_call | solution.py:1241
  86.6 114.3 %experts.1 = (f32[64,2176]{1,0:T(8,128)}, bf16[2048,2048]{1,0:T(8,128)(2,1)}, f32[384,2048]{1,0:T(8,128)}, f32[384,2048]{1,0:T(8,128)}, f32[384,2048]{1,0:T(8,128)}) custom-call(bf16[64,2176]{1,0:T(8,128)(2,1)} %get-tuple-element.34.own_ref, bf16[2048,2048]{1,0:T(8,128)(2,1)} %get-tuple-element.35.upstream_ref, bf16[384,2048]{1,0:T(8,128)(2,1)} %bitcast.30, ...), custom_call_target="tpu_custom_call" | custom-call | tf_op jit(solution)/shard_map/experts/pallas_call | solution.py:987
  200.8 1.9 constant_dynamic-slice_fusion.2
  202.7 109.8 %tail.1 = (bf16[256,2048]{1,0:T(8,128)(2,1)}, bf16[256,2048]{1,0:T(8,128)(2,1)}, f32[256,1024]{1,0:T(8,128)}, f32[256,1280]{1,0:T(8,128)}, f32[24,256]{1,0:T(8,128)}) custom-call(s32[1]{0:T(128)S(6)} %copy.38.length_ref, f32[64,2176]{1,0:T(8,128)} %get-tuple-element.36.summed_ref, bf16[64,2176]{1,0:T(8,128)(2,1)} %get-tuple-element.34.own_ref, ...), custom_call_target="tpu_custom_call" | custom-call | tf_op jit(solution)/shard_map/tail/pallas_call | solution.py:1667
  312.5 0.0 copy-start.7
  312.5 0.0 copy-start.6
  312.5 0.0 copy-start.5
  312.5 2.5 slice.25
  315.0 1.7 fusion.5
  316.7 1.3 slice_bitcast_fusion
  318.0 1.4 fusion.6
  319.4 0.6 fusion.3
  320.0 0.6 fusion.4
  320.6 0.0 copy-done.7
  320.6 1.0 copy.39
  321.5 0.0 copy-done.6
  321.5 1.0 copy.40
  322.5 0.0 copy-done.5
  322.5 1.0 copy.41
  323.5 0.0 copy-done.4
  323.5 1.7 copy.42
  325.2 1.4 copy-done.3
  326.5 1.7 copy.43
  328.2 1.4 copy-done.2
  329.5 1.7 copy.44
  (6 shorter events, 0.0 us)
Async XLA Ops:
  0.6 0.7 copy-start
  312.5 8.1 %copy-start.7 = (bf16[256,2048]{1,0:T(8,128)(2,1)S(1)}, bf16[256,2048]{1,0:T(8,128)(2,1)}, u32[]{:S(2)}) copy-start(bf16[256,2048]{1,0:T(8,128)(2,1)} %get-tuple-element.81) | copy-start | bytes 3145732
  312.5 9.0 %copy-start.6 = (bf16[256,2048]{1,0:T(8,128)(2,1)S(1)}, bf16[256,2048]{1,0:T(8,128)(2,1)}, u32[]{:S(2)}) copy-start(bf16[256,2048]{1,0:T(8,128)(2,1)} %get-tuple-element.82) | copy-start | bytes 3145732
  312.5 10.0 %copy-start.5 = (f32[256,1024]{1,0:T(8,128)S(1)}, f32[256,1024]{1,0:T(8,128)}, u32[]{:S(2)}) copy-start(f32[256,1024]{1,0:T(8,128)} %get-tuple-element.89) | copy-start | bytes 3145732
  320.6 2.9 copy-start.4
  323.5 3.0 copy-start.3
  326.5 3.0 copy-start.2
  326.5 4.7 %copy-start.1 = (s32[256,8]{0,1:T(8,128)S(1)}, s32[256,8]{0,1:T(8,128)}, u32[]{:S(2)}) copy-start(s32[256,8]{0,1:T(8,128)} %param.18) | copy-start | bytes 24580

commit v5 on v4

--- a/solution.py
+++ b/solution.py
@@ -811,11 +811,19 @@
     owned,
     own_ref,
     upstream_ref,
+    gate_from,
+    up_from,
+    down_from,
+    heads_ref,
+    grad_ref,
+    moe_ref,
+    line_heads_ref,
+    gate_grad_to,
+    up_grad_to,
+    down_grad_to,
     gate_ref,
     up_ref,
     down_ref,
-    grad_ref,
-    moe_ref,
     gate_grad_ref,
     up_grad_ref,
     down_grad_ref,
@@ -833,12 +841,23 @@
     gather_recv,
     scatter_send,
     scatter_recv,
+    heads_send,
+    heads_recv,
+    store_sems,
 ):
     p = Place()
     group = rows * 4
     units = down_ref.shape[0]
     hidden = units // owned
     extra = all_ref.shape[1] - width
+    loads = [
+        pltpu.make_async_copy(src, dst, local_sems.at[5 + i])
+        for i, (src, dst) in enumerate(
+            ((gate_from, gate_ref), (up_from, up_ref), (down_from, down_ref))
+        )
+    ]
+    for copy in loads:
+        copy.start()
     enter(p.peers())
     whole, _, _ = pieces_of(all_ref, rows)
     own_copy = pltpu.make_async_copy(own_ref, whole(p.block()), local_sems.at[0])
@@ -898,10 +917,18 @@
 
     fetch(0).start()
     gathering[0]()
+    heads_copies = Copies(heads_send, heads_recv)
+    half = heads_ref.shape[1] // 2
+    heads_line = LineSend(
+        p, heads_copies, heads_ref.at[:, half:], lambda z: line_heads_ref.at[z]
+    )
+    heads_line.start()
     down_grad_ref[...] = jnp.zeros_like(down_grad_ref)
     first = p.e * owned
     lane = lax.broadcasted_iota(jnp.int32, (group, extra), 1)
     unit = lax.broadcasted_iota(jnp.int32, (group, units), 1)
+    for copy in loads:
+        copy.wait()
 
     @pl.loop(0, count)
     def _(i):
@@ -963,6 +990,18 @@
 
     tile = width // count
 
+    def store_tile(i):
+        at = pl.ds(pl.multiple_of(i * tile, tile), tile)
+        return [
+            pltpu.make_async_copy(ref.at[:, at], to.at[:, at], store_sems.at[i, j])
+            for j, (ref, to) in enumerate(
+                ((gate_grad_ref, gate_grad_to), (up_grad_ref, up_grad_to))
+            )
+        ]
+
+    store_down = pltpu.make_async_copy(down_grad_ref, down_grad_to, local_sems.at[5])
+    store_down.start()
+
     @pl.loop(0, count)
     def _(i):
         for k, actions in beside_tiles.items():
@@ -971,15 +1010,24 @@
         x = all_ref[:, at]
         gate_grad_ref[:, at] = dot(back_rows[:, :units], x, 0, 0)
         up_grad_ref[:, at] = dot(back_rows[:, units:], x, 0, 0)
+        for copy in store_tile(i):
+            copy.start()
 
     finish()
     gather_copies.finish()
     scatter_copies.finish()
+    for k in range(1, DEPTH):
+        heads_line.wait(k)
+    heads_copies.finish()
     store(count - 2).wait()
     store(count - 1).wait()
-
-
-def run_experts(own, upstream_all, gate, up, down, owned, experts, width, collective_id):
+    store_down.wait()
+    for i in range(count):
+        for copy in store_tile(i):
+            copy.wait()
+
+
+def run_experts(own, upstream_all, gate, up, down, heads, owned, experts, width, collective_id):
     rows, full = own.shape
     total = upstream_all.shape[0]
     units = down.shape[0]
@@ -989,11 +1037,14 @@
         out_shape=(
             jax.ShapeDtypeStruct((rows, full), F32),
             jax.ShapeDtypeStruct((total, width), LOW),
+            jax.ShapeDtypeStruct((DEPTH, group, heads.shape[1] // 2), LOW),
             *[jax.ShapeDtypeStruct((units, width), F32)] * 3,
         ),
-        in_specs=[VMEM_SPEC, ANY_SPEC, VMEM_SPEC, VMEM_SPEC, VMEM_SPEC],
-        out_specs=(VMEM_SPEC, ANY_SPEC, VMEM_SPEC, VMEM_SPEC, VMEM_SPEC),
-        scratch_shapes=[
+        in_specs=[VMEM_SPEC] + [ANY_SPEC] * 5,
+        out_specs=[VMEM_SPEC] + [ANY_SPEC] * 5,
+        scratch_shapes=[pltpu.VMEM((units, width), LOW)] * 3
+        + [pltpu.VMEM((units, width), F32)] * 3
+        + [
             pltpu.VMEM((total, full), LOW),
             pltpu.VMEM((2, group, width), LOW),
             pltpu.VMEM((2, group, width), LOW),
@@ -1001,12 +1052,13 @@
             pltpu.VMEM((total, 2 * units), LOW),
         ]
         + scatter_scratch(rows, full)
-        + semaphores(5, GATHER_SEMS, GATHER_SEMS, SCATTER_SEMS, SCATTER_SEMS),
+        + semaphores(8, GATHER_SEMS, GATHER_SEMS, SCATTER_SEMS, SCATTER_SEMS, DEPTH, DEPTH)
+        + [pltpu.SemaphoreType.DMA((2 * DEPTH, 2))],
         compiler_params=pltpu.CompilerParams(
             collective_id=collective_id, has_side_effects=True, vmem_limit_bytes=64000000
         ),
         name="experts",
-    )(own, upstream_all, gate, up, down)
+    )(own, upstream_all, gate, up, down, heads)
 
 
 def normed_rows(values):
@@ -1082,7 +1134,14 @@
 
 
 FOLD_SEMS = 3
-FRONT_SEMS = FOLD_SEMS + 2 * LineSend.SEMS
+FRONT_SEMS = FOLD_SEMS + LineSend.SEMS
+LANES = 128
+
+
+def widen(wide_ref, router_weight_ref):
+    experts, width = router_weight_ref.shape
+    wide_ref[:experts, :] = router_weight_ref[...]
+    wide_ref[experts:, :] = jnp.zeros((LANES - experts, width), LOW)
 
 
 def front_kernel(
@@ -1101,8 +1160,8 @@
     query_weight_ref,
     key_weight_ref,
     value_weight_ref,
-    output_weight_ref,
-    router_weight_ref,
+    output_weight_from,
+    router_weight_from,
     upstream_ref,
     xnorm1_ref,
     query_ref,
@@ -1113,6 +1172,8 @@
     hidden_ref,
     own_ref,
     router_ref,
+    output_weight_ref,
+    router_weight_ref,
     part,
     part_in,
     local_sems,
@@ -1127,6 +1188,8 @@
     size = cosine_ref.shape[1]
     count = units // size
     length = length_ref[0]
+    load = pltpu.make_async_copy(output_weight_from, output_weight_ref, local_sems.at[1])
+    load.start()
     enter(p.peers())
     copies = Copies(send_sems, recv_sems)
     gather_copies = Copies(gather_send, gather_recv)
@@ -1136,19 +1199,9 @@
     own_copy = pltpu.make_async_copy(own_cotangent, whole(p.block()), local_sems.at[0])
     gathering = gather_steps(p, gather_copies, rows, own_cotangent, upstream_ref, own_copy)
     fold = Fold(p, copies, rows, part, part_in)
-    line = [
-        LineSend(
-            p,
-            copies,
-            heads_ref.at[:, a:b],
-            lambda z, a=a, b=b: line_heads_ref.at[z, :, a:b],
-        )
-        for a, b in ((0, units // 2), (units // 2, units))
-    ]
-
-    def send_heads(i):
-        line[i].start()
-
+    line = LineSend(
+        p, copies, heads_ref.at[:, : units // 2], lambda z: line_heads_ref.at[z]
+    )
     gathering[0]()
 
     normed1, _ = normed_rows(tokens_ref[...].astype(F32))
@@ -1167,7 +1220,7 @@
 
     @pl.loop(0, count)
     def _(h):
-        pl.when(h == count // 2)(functools.partial(send_heads, 0))
+        pl.when(h == count // 2)(line.start)
         for k in (2, 3):
             pl.when(h == 2 * k)(gathering[k])
         at = pl.ds(pl.multiple_of(h * size, size), size)
@@ -1177,7 +1230,7 @@
         probs = attention_probs(query_low, key_low, allowed).astype(LOW)
         heads_ref[:, at] = jnp.where(valid, dot(probs, value_ref[...], 1, 0), 0.0).astype(LOW)
 
-    send_heads(1)
+    load.wait()
     part[...] = dot(heads_ref[...], output_weight_ref[...], 1, 1).astype(LOW)
     fold.start()
     gathering[4]()
@@ -1189,6 +1242,7 @@
     xnorm2 = (normed2 * routing_gain_ref[...]).astype(LOW)
     own_ref[:, :width] = xnorm2
     gathering[6]()
+    widen(router_weight_ref, router_weight_from)
     logits = dot(xnorm2, router_weight_ref[...], 1, 1)
     lanes = logits.shape[1]
     lane = lax.broadcasted_iota(jnp.int32, logits.shape, 1)
@@ -1207,9 +1261,8 @@
     router_ref[:, 2 * lanes :] = named
     gathering[7]()
     gathering[8]()
-    for half in line:
-        for k in range(1, DEPTH):
-            half.wait(k)
+    for k in range(1, DEPTH):
+        line.wait(k)
     gather_copies.finish()
     copies.finish()
 
@@ -1235,7 +1288,7 @@
 ):
     group, width = tokens.shape
     rows = routes.shape[0]
-    lanes = router_weight.shape[0]
+    lanes = LANES
     total = group * lax.axis_size("expert")
     struct = jax.ShapeDtypeStruct
     return pl.pallas_call(
@@ -1247,15 +1300,22 @@
             struct((group, key_weight.shape[1]), F32),
             struct((group, value_weight.shape[1]), LOW),
             struct((group, query_weight.shape[1]), LOW),
-            struct((DEPTH, group, query_weight.shape[1]), LOW),
+            struct((DEPTH, group, query_weight.shape[1] // 2), LOW),
             struct((rows, width), F32),
             struct((rows, width + lanes), LOW),
             struct((rows, 3 * lanes), F32),
         ),
-        in_specs=[pl.BlockSpec(memory_space=pltpu.SMEM), VMEM_SPEC, ANY_SPEC] + [VMEM_SPEC] * 12,
+        in_specs=[pl.BlockSpec(memory_space=pltpu.SMEM), VMEM_SPEC, ANY_SPEC]
+        + [VMEM_SPEC] * 10
+        + [ANY_SPEC, VMEM_SPEC],
         out_specs=[ANY_SPEC] + [VMEM_SPEC] * 5 + [ANY_SPEC] + [VMEM_SPEC] * 3,
-        scratch_shapes=[pltpu.VMEM((group, width), LOW), pltpu.VMEM((3, rows, width), LOW)]
-        + semaphores(1, GATHER_SEMS, GATHER_SEMS, FRONT_SEMS, FRONT_SEMS),
+        scratch_shapes=[
+            pltpu.VMEM(output_weight.shape, LOW),
+            pltpu.VMEM((lanes, width), LOW),
+            pltpu.VMEM((group, width), LOW),
+            pltpu.VMEM((3, rows, width), LOW),
+        ]
+        + semaphores(2, GATHER_SEMS, GATHER_SEMS, FRONT_SEMS, FRONT_SEMS),
         compiler_params=pltpu.CompilerParams(
             collective_id=collective_id, has_side_effects=True, vmem_limit_bytes=60000000
         ),
@@ -1280,7 +1340,8 @@
 
 
 SPREAD_SEMS = 3
-TAIL_SEMS = 4 * SPREAD_SEMS + DEPTH + DEPTH + 2 + 2 * LineSum.SEMS + 1 + 3 + 3 + DEPTH
+PIECES = 4
+TAIL_SEMS = 4 * SPREAD_SEMS + DEPTH * 3 + PIECES * (1 + LineSum.SEMS) + 1 + FOLD_SEMS + 3
 
 
 def tail_kernel(
@@ -1291,12 +1352,13 @@
     own_ref,
     router_ref,
     hidden_ref,
-    cotangent_ref,
-    tokens_ref,
+    cotangent_from,
+    tokens_from,
     xnorm1_ref,
     moe_ref,
     heads_ref,
-    line_heads_ref,
+    line_first_ref,
+    line_second_ref,
     query_ref,
     key_ref,
     value_ref,
@@ -1306,16 +1368,26 @@
     routing_gain_ref,
     query_gain_ref,
     key_gain_ref,
+    query_weight_from,
+    key_weight_from,
+    value_weight_from,
+    output_weight_from,
+    router_weight_from,
+    mixed_ref,
+    tokens_grad_ref,
+    output_grad_ref,
+    query_grad_ref,
+    key_grad_ref,
+    value_grad_ref,
+    small_out_ref,
+    cotangent_ref,
+    tokens_ref,
     query_weight_ref,
     key_weight_ref,
     value_weight_ref,
     output_weight_ref,
     router_weight_ref,
-    mixed_ref,
-    tokens_grad_ref,
-    output_grad_ref,
     packed_grad_ref,
-    small_out_ref,
     hidden_grad_ref,
     hidden_low_ref,
     hidden_all,
@@ -1356,14 +1428,24 @@
     packed_width = packed.shape[1]
     share = width // (2 * DEPTH)
     length = length_ref[0]
+    mine = pl.ds(pl.multiple_of(p.t * rows, rows), rows)
+    pairs = [
+        (cotangent_from.at[mine], cotangent_ref),
+        (moe_ref, moe),
+        (output_weight_from, output_weight_ref),
+        (tokens_from.at[mine], tokens_ref),
+        (query_weight_from, query_weight_ref),
+        (key_weight_from, key_weight_ref),
+        (value_weight_from, value_weight_ref),
+    ]
+    for i in range(1, DEPTH):
+        z = p.near(i)
+        pairs += [
+            (line_first_ref.at[z], line_heads.at[z, :, : units // 2]),
+            (line_second_ref.at[z], line_heads.at[z, :, units // 2 :]),
+        ]
     fetch = [
-        pltpu.make_async_copy(moe_ref, moe, local_sems.at[0]),
-        *[
-            pltpu.make_async_copy(
-                line_heads_ref.at[p.near(k)], line_heads.at[p.near(k)], local_sems.at[k]
-            )
-            for k in range(1, DEPTH)
-        ],
+        pltpu.make_async_copy(src, dst, local_sems.at[i]) for i, (src, dst) in enumerate(pairs)
     ]
     for copy in fetch:
         copy.start()
@@ -1409,7 +1491,9 @@
     xnorm_to = [
         copies.make(xnorm1_ref.at[:, columns(z, 1 - p.y)], xnorm_in.at[z], yn) for z in range(DEPTH)
     ]
-    cuts = [(0, units // 2), (units // 2, packed_width)]
+    cut = units // PIECES
+    cuts = [(i * cut, (i + 1) * cut) for i in range(PIECES - 1)]
+    cuts.append((cuts[-1][1], packed_width))
     packed_to = [copies.make(packed.at[:, a:b], packed_in.at[:, a:b], yn) for a, b in cuts]
     weight_sums = [
         LineSum(
@@ -1431,6 +1515,7 @@
         [(z, small_side.at[2, z], small_line.at[p.z]) for z in order[: DEPTH - 1]], along, p.z
     )
 
+    widen(router_weight_ref, router_weight_from)
     lanes = router_weight_ref.shape[0]
     gain_row = experts + 2
     route_grad = summed_ref[:, width:]
@@ -1445,9 +1530,10 @@
     )
     small[...] = jnp.zeros_like(small)
     small[:experts, :] = dot(logit_low, own_ref[:, :width], 0, 0)[:experts]
-    fetch[0].wait()
+    fetch[1].wait()
     for k in range(DEPTH):
         sums.start(k)
+    fetch[0].wait()
     xnorm2_grad = summed_ref[:, :width] + dot(logit_low, router_weight_ref[...], 1, 0)
     normed2, scale2 = normed_rows(hidden_ref[...])
     small[experts : experts + 1, :] = jnp.sum(xnorm2_grad * normed2, axis=0, keepdims=True)
@@ -1475,6 +1561,7 @@
 
     valid = lax.broadcasted_iota(jnp.int32, (group, 1), 0) < length
     allowed = allowed_keys(group, length)
+    fetch[2].wait()
     heads_grad[...] = jnp.where(
         valid, dot(hidden_all[...], output_weight_ref[...], 1, 0), 0.0
     ).astype(LOW)
@@ -1509,33 +1596,8 @@
         packed[:, at] = back.astype(LOW)
         small[gain_row : gain_row + 1, :size] += gain_part
 
-    pl.loop(0, count // 2)(one_head)
-    packed_to[0].start()
-    sums.corner(3)
-    sums.side(0)
-    for _, back in hidden_to:
-        back.wait_recv()
-    line_spread.start()
-    pl.loop(count // 2, count)(one_head)
-    key_back, key_part = norm_back(key_sum[...] * factor, key_hat, key_scale, key_gain)
-    packed[:, units : units + size] = key_back.astype(LOW)
-    packed[:, units + size :] = value_sum[...].astype(LOW)
-    packed_to[1].start()
-    small[gain_row + 1 : gain_row + 2, :size] = key_part
-    for row in (gain_row, gain_row + 1):
-        part = small[row : row + 1, :size]
-        for i in range(1, width // size):
-            small[row : row + 1, i * size : (i + 1) * size] = part
-    line_spread.forward()
-    sums.side(1)
-    back_part[...] = (
-        dot(packed[:, :units], query_weight_ref[...], 1, 1)
-        + dot(packed[:, units : units + size], key_weight_ref[...], 1, 1)
-        + dot(packed[:, units + size :], value_weight_ref[...], 1, 1)
-    ).astype(LOW)
-    fold.start()
-    for copy in xnorm_to:
-        copy.wait_recv()
+    def heads_piece(i):
+        pl.loop(i * count // PIECES, (i + 1) * count // PIECES)(one_head)
 
     def weight_piece(i):
         a, b = cuts[i]
@@ -1551,11 +1613,48 @@
             else:
                 packed_grad_ref[:, a:b] = grad
 
+    heads_piece(0)
+    packed_to[0].start()
+    sums.corner(3)
+    heads_piece(1)
+    packed_to[1].start()
+    for copy in xnorm_to:
+        copy.wait_recv()
     weight_piece(0)
+    sums.side(0)
+    for _, back in hidden_to:
+        back.wait_recv()
+    line_spread.start()
+    heads_piece(2)
+    packed_to[2].start()
+    weight_piece(1)
+    weight_sums[0].relay()
+    sums.side(1)
+    heads_piece(3)
+    key_back, key_part = norm_back(key_sum[...] * factor, key_hat, key_scale, key_gain)
+    packed[:, units : units + size] = key_back.astype(LOW)
+    packed[:, units + size :] = value_sum[...].astype(LOW)
+    packed_to[3].start()
+    small[gain_row + 1 : gain_row + 2, :size] = key_part
+    for row in (gain_row, gain_row + 1):
+        part = small[row : row + 1, :size]
+        for i in range(1, width // size):
+            small[row : row + 1, i * size : (i + 1) * size] = part
+    line_spread.forward()
+    weight_piece(2)
+    weight_sums[1].relay()
+    for copy in fetch[3:7]:
+        copy.wait()
+    back_part[...] = (
+        dot(packed[:, :units], query_weight_ref[...], 1, 1)
+        + dot(packed[:, units : units + size], key_weight_ref[...], 1, 1)
+        + dot(packed[:, units + size :], value_weight_ref[...], 1, 1)
+    ).astype(LOW)
+    fold.start()
+    weight_piece(3)
     fold.forward()
+    weight_sums[2].relay()
     sums.side(2)
-    weight_sums[0].relay()
-    weight_piece(1)
     sums.side(3)
     sums.close(0)
 
@@ -1571,7 +1670,7 @@
     tokens_spread.start()
 
     line_spread.finish()
-    for copy in fetch[1:]:
+    for copy in fetch[7:]:
         copy.wait()
 
     def output_piece(y):
@@ -1585,7 +1684,7 @@
     output_out[...] = output_piece(1 - p.y).astype(LOW)
     output_to.start()
     output_grad_ref[...] = output_piece(p.y)
-    weight_sums[1].relay()
+    weight_sums[3].relay()
     sums.close(1)
     small_to_c.wait_recv()
     small_to_c.wait_send()
@@ -1619,8 +1718,12 @@
     mixed_spread.forward()
     mixed_spread.finish()
     for i, (a, b) in enumerate(cuts):
+        grad = packed_grad_ref[:, a:b]
         for term in weight_sums[i].wait():
-            packed_grad_ref[:, a:b] += term[...].astype(F32)
+            grad += term[...].astype(F32)
+        query_grad_ref[:, a : min(b, units)] = grad[:, : min(b, units) - a]
+    key_grad_ref[...] = grad[:, -2 * size : -size]
+    value_grad_ref[...] = grad[:, -size:]
     for copy in copies.made:
         if copy is not small_to_c and copy is not small_to_x:
             copy.wait_send()
@@ -1638,7 +1741,8 @@
     xnorm1,
     moe,
     heads,
-    line_heads,
+    line_first,
+    line_second,
     query,
     key,
     value,
@@ -1670,15 +1774,28 @@
             jax.ShapeDtypeStruct((group, width), LOW),
             jax.ShapeDtypeStruct((group, width), LOW),
             jax.ShapeDtypeStruct((share, units), F32),
-            jax.ShapeDtypeStruct((share, packed_width), F32),
+            jax.ShapeDtypeStruct((share, units), F32),
+            jax.ShapeDtypeStruct((share, size), F32),
+            jax.ShapeDtypeStruct((share, size), F32),
             jax.ShapeDtypeStruct((smalls, share), F32),
         ),
         in_specs=[pl.BlockSpec(memory_space=pltpu.SMEM)]
-        + [VMEM_SPEC] * 7
-        + [ANY_SPEC, VMEM_SPEC, ANY_SPEC]
-        + [VMEM_SPEC] * 14,
-        out_specs=[VMEM_SPEC] * 5,
+        + [VMEM_SPEC] * 4
+        + [ANY_SPEC, ANY_SPEC, VMEM_SPEC]
+        + [ANY_SPEC, VMEM_SPEC, ANY_SPEC, ANY_SPEC]
+        + [VMEM_SPEC] * 9
+        + [ANY_SPEC] * 4
+        + [VMEM_SPEC],
+        out_specs=[VMEM_SPEC] * 7,
         scratch_shapes=[
+            vmem((rows, width), LOW),
+            vmem((rows, width), LOW),
+            vmem(query_weight.shape, LOW),
+            vmem(key_weight.shape, LOW),
+            vmem(value_weight.shape, LOW),
+            vmem(output_weight.shape, LOW),
+            vmem((LANES, width), LOW),
+            vmem((share, packed_width), F32),
             vmem((rows, width), F32),
             vmem((rows, width), LOW),
             vmem((group, width), LOW),
@@ -1703,7 +1820,7 @@
             vmem((DEPTH, smalls, share), F32),
         ]
         + scatter_scratch(rows, width)
-        + semaphores(DEPTH, TAIL_SEMS, TAIL_SEMS, SCATTER_SEMS, SCATTER_SEMS),
+        + semaphores(7 + 2 * (DEPTH - 1), TAIL_SEMS, TAIL_SEMS, SCATTER_SEMS, SCATTER_SEMS),
         compiler_params=pltpu.CompilerParams(
             collective_id=collective_id, has_side_effects=True, vmem_limit_bytes=64000000
         ),
@@ -1719,7 +1836,8 @@
         xnorm1,
         moe,
         heads,
-        line_heads,
+        line_first,
+        line_second,
         query,
         key,
         value,
@@ -1769,8 +1887,7 @@
     cosine, sine = rope_tables(count, head_size)
     half = head_size // 2
     sine = jnp.concatenate([-sine[:, :half], sine[:, half:]], axis=1)
-    router_wide = jnp.pad(router_weight.T, ((0, 128 - experts), (0, 0)))
-    upstream_all, xnorm1, query, key, value, heads, line_heads, hidden, own, router = run_front(
+    upstream_all, xnorm1, query, key, value, heads, line_first, hidden, own, router = run_front(
         seq_length,
         tokens,
         cotangent,
@@ -1785,7 +1902,7 @@
         key_weight,
         value_weight,
         output_weight,
-        router_wide,
+        router_weight.T,
         experts,
         0,
     )
@@ -1796,29 +1913,31 @@
     def from_units(grad):
         return grad.reshape(owned, -1, width).transpose(0, 2, 1)
 
-    summed, moe_part, gate_grad, up_grad, down_grad = run_experts(
+    summed, moe_part, line_second, gate_grad, up_grad, down_grad = run_experts(
         own,
         upstream_all,
         by_unit(gate_weight),
         by_unit(up_weight),
         down_weight.reshape(-1, width),
+        heads,
         owned,
         experts,
         width,
         1,
     )
-    mixed, tokens_grad, output_grad, packed_grad, small_sum = run_tail(
+    mixed, tokens_grad, output_grad, query_grad, key_grad, value_grad, small_sum = run_tail(
         seq_length,
         summed,
         own,
         router,
         hidden,
-        own_rows(cotangent),
-        own_rows(tokens),
+        cotangent,
+        tokens,
         xnorm1,
         moe_part,
         heads,
-        line_heads,
+        line_first,
+        line_second,
         query,
         key,
         value,
@@ -1832,12 +1951,10 @@
         key_weight,
         value_weight,
         output_weight,
-        router_wide,
+        router_weight.T,
         experts,
         2,
     )
-    query_end = query_weight.shape[1]
-    key_end = query_end + key_weight.shape[1]
     share = head_size // lax.axis_size("expert")
 
     def own_gain(row):
@@ -1847,9 +1964,9 @@
         mixed,
         tokens_grad,
         small_sum[experts + 1],
-        packed_grad[:, :query_end],
-        packed_grad[:, query_end:key_end],
-        packed_grad[:, key_end:],
+        query_grad,
+        key_grad,
+        value_grad,
         own_gain(experts + 2),
         own_gain(experts + 3),
         output_grad,

time: 336 us -> 306 us (0.911)
  Pallas kernels: 305 us -> 280 us
    pallas_call x1, Pallas kernels: 80.7 us -> 65.7 us  [run_front(): pl.pallas_call(functools.partial(front_kernel, rows, experts), out_shape=...]
    pallas_call x1, Pallas kernels: 110 us -> 97.6 us  [run_tail(): pl.pallas_call(functools.partial(tail_kernel, rows, experts), out_shape=(...]
    unnamed x23 -> x28, local copies, waits for them, and re-layouts: 12 us -> 16.6 us
    slice x2 -> x0, local copies, waits for them, and re-layouts: 4.14 us -> none  [the longest x1 2.46 us: gathered_shards(): packed_grad[:, :query_end]]
where the time goes in v5:
time: 306 us; the launch traced here: 303 us
  Pallas kernels  280 us (92%)
  local copies, waits for them, and re-layouts  20.5 us (7%)
    pallas_call x1, Pallas kernels, run_experts(): pl.pallas_call(functools.partial(experts_kernel, rows, width, experts, ow...  116 us
    pallas_call x1, Pallas kernels, run_tail(): pl.pallas_call(functools.partial(tail_kernel, rows, experts), out_shape=(...  97.6 us
    pallas_call x1, Pallas kernels, run_front(): pl.pallas_call(functools.partial(front_kernel, rows, experts), out_shape=...  65.7 us
    unnamed x28, local copies, waits for them, and re-layouts  16.6 us

profile of v5, /device:TPU:0, one launch (start us, length us, event | category | flops | bytes accessed | tf_op | source)
XLA Modules:
  0.0 302.8 jit_solution(8633103599331937717)
XLA Ops:
  0.6 0.0 copy-start
  1.3 0.0 copy-done
  1.3 0.1 constant_dynamic-slice_fusion.2
  1.4 0.7 copy.31.routes_ref
  2.1 0.5 fusion.2
  2.6 0.8 pad_maximum_fusion
  3.5 65.7 %front.1 = (bf16[2048,2048]{1,0:T(8,128)(2,1)}, bf16[256,2048]{1,0:T(8,128)(2,1)}, f32[256,1024]{1,0:T(8,128)}, f32[256,128]{1,0:T(8,128)}, bf16[256,128]{1,0:T(...) custom-call(s32[1]{0:T(128)S(6)} %copy.41.length_ref, ...), custom_call_target="tpu_custom_call" | custom-call | tf_op jit(solution)/shard_map/front/pallas_call | solution.py:1294
  69.1 116.3 %experts.1 = (f32[64,2176]{1,0:T(8,128)}, bf16[2048,2048]{1,0:T(8,128)(2,1)}, bf16[4,256,512]{2,1,0:T(8,128)(2,1)}, f32[384,2048]{1,0:T(8,128)}, f32[384,2048]{1,0:T(8,128)}, /*index=5*/f32[384,2048]{1,0:T(8,128)}) custom-call(bf16[64,2176]{1,0:T(8,128)(2,1)} %get-tuple-element.37.own_ref, bf16[2048,2048]{1,0:T(8,128)(2,1)} %get-tuple-element.38.upstream_ref, ...), custom_call_target="tpu_custom_call" | custom-call | tf_op jit(solution)/shard_map/experts/pallas_call | solution.py:1035
  185.4 97.6 %tail.1 = (bf16[256,2048]{1,0:T(8,128)(2,1)}, bf16[256,2048]{1,0:T(8,128)(2,1)}, f32[256,1024]{1,0:T(8,128)}, f32[256,1024]{1,0:T(8,128)}, f32[256,128]{1,0:T(8,...) custom-call(s32[1]{0:T(128)S(6)} %copy.41.length_ref, f32[64,2176]{1,0:T(8,128)} %get-tuple-element.40.summed_ref, ...), custom_call_target="tpu_custom_call" | custom-call | tf_op jit(solution)/shard_map/tail/pallas_call | solution.py:1771
  283.0 0.0 copy-start.6
  283.0 1.4 fusion.5
  284.4 1.3 slice_bitcast_fusion
  285.8 0.6 fusion.4
  286.3 0.6 fusion.3
  286.9 0.0 copy-start.8
  286.9 2.4 copy.42
  289.3 2.5 copy.43
  291.8 0.0 copy-done.6
  291.8 1.0 copy.44
  292.8 0.0 copy-done.8
  292.8 0.7 copy.45
  293.4 0.0 copy-done.7
  293.4 0.7 copy.46
  294.1 0.0 copy-done.5
  294.1 1.0 copy.47
  295.1 0.0 copy-done.4
  295.1 1.7 copy.48
  296.7 1.4 copy-done.3
  298.1 1.7 copy.49
  299.8 1.4 copy-done.2
  301.1 1.7 copy.50
  302.8 0.0 copy-done.1
  (7 shorter events, 0.0 us)
Async XLA Ops:
  0.6 0.7 copy-start
  283.0 8.8 %copy-start.6 = (f32[256,1024]{1,0:T(8,128)S(1)}, f32[256,1024]{1,0:T(8,128)}, u32[]{:S(2)}) copy-start(f32[256,1024]{1,0:T(8,128)} %get-tuple-element.86) | copy-start | bytes 3145732
  286.9 5.8 %copy-start.8 = (f32[256,128]{1,0:T(8,128)S(1)}, f32[256,128]{1,0:T(8,128)}, u32[]{:S(2)}) copy-start(f32[256,128]{1,0:T(8,128)} %get-tuple-element.87) | copy-start | bytes 393220
  286.9 6.5 %copy-start.7 = (f32[256,128]{1,0:T(8,128)S(1)}, f32[256,128]{1,0:T(8,128)}, u32[]{:S(2)}) copy-start(f32[256,128]{1,0:T(8,128)} %get-tuple-element.88) | copy-start | bytes 393220
  286.9 7.2 %copy-start.5 = (f32[256,1024]{1,0:T(8,128)S(1)}, f32[256,1024]{1,0:T(8,128)}, u32[]{:S(2)}) copy-start(f32[256,1024]{1,0:T(8,128)} %get-tuple-element.91) | copy-start | bytes 3145732
  289.3 5.7 %copy-start.4 = (f32[384,2048]{1,0:T(8,128)S(1)}, f32[384,2048]{1,0:T(8,128)}, u32[]{:S(2)}) copy-start(f32[384,2048]{1,0:T(8,128)} %get-tuple-element.57) | copy-start | bytes 9437188
  295.1 3.0 copy-start.3
  298.1 3.0 copy-start.2
  298.1 4.7 %copy-start.1 = (s32[256,8]{0,1:T(8,128)S(1)}, s32[256,8]{0,1:T(8,128)}, u32[]{:S(2)}) copy-start(s32[256,8]{0,1:T(8,128)} %param.18) | copy-start | bytes 24580
